TPU v7x, 512 devices: a whole 4x8x8 slice. The times are simulated.
512 devices in a mesh: fsdp: 64 (over x, y, core), dp: 8 (over z).
Axes of the slice: x: 4, y: 8, z: 8, core: 2. Of those that a mesh axis runs over, the one named last changes fastest.
Arguments:
- grads: bfloat16 [8, 1024, 28672], P('dp', 'fsdp')
- block_slot: int32 [28], replicated, may hold values from 0 to 63, as said below
- left_stats: float32 [64, 1024, 1024], P('fsdp', 'dp')
- right_stats: float32 [64, 1024, 1024], P('fsdp', 'dp')
- left_root: bfloat16 [64, 1024, 1024], P('fsdp', 'dp')
- right_root: bfloat16 [64, 1024, 1024], P('fsdp', 'dp')
Outputs:
- left_new: float32 [64, 1024, 1024], P('fsdp', 'dp')
- right_new: float32 [64, 1024, 1024], P('fsdp', 'dp')
- update: bfloat16 [1024, 28672], P('fsdp')
Inputs may be any that keep to these rules, and one draw needn't show every extreme that they name: The entries of block_slot are distinct. Block b's statistics and roots sit in slot block_slot[b], which belongs to the fsdp device of index block_slot[b]; slots that no block names are empty and their statistics pass through unchanged.
All inputs are finite; a program needn't handle non-finite values.
Results may differ from a plain program's by a relative error of at most 0.015.
Values may be sent and summed in bfloat16 or wider, within the bound.
No kernel may reach another device: no remote copies, remote signals or barrier semaphores. Data moves between devices by JAX's collectives and lax.ppermute only.
A program may use at most 64 MiB of HBM per device.

v0:
```python
import jax
import jax.numpy as jnp
from jax import lax
from jax.sharding import Mesh
from jax.sharding import PartitionSpec as P

FSDP = ("fsdp_0", "fsdp_1", "fsdp_2")


epsilon = 1e-06


def in_blocks(array, dim, count):
    lengths = array.shape
    tiles = array.reshape(*lengths[:dim], count, lengths[dim] // count, *lengths[dim + 1 :])
    return jnp.moveaxis(tiles, dim, 0)


def sum_at_owner(array, axis, dim):
    count = lax.axis_size(axis)
    tiles = lax.all_to_all(in_blocks(array, dim, count), axis, 0, 0, tiled=True)
    return jnp.sum(tiles.astype(jnp.float32), axis=0)


def in_order(tiles, dim):
    tiles = jnp.moveaxis(tiles, 0, dim)
    lengths = tiles.shape
    return tiles.reshape(*lengths[:dim], lengths[dim] * lengths[dim + 1], *lengths[dim + 2 :])


def exchange_in_order(tiles, axes, sequence):
    inside = tiles.shape[1:]
    result = tiles.reshape(*(lax.axis_size(a) for a in axes), *inside)
    for k in sequence:
        result = lax.all_to_all(result, axes[k], k, k, tiled=True)
    return result.reshape(-1, *inside)


def core_and_chips(array, groups, sequence, split_dim, concat_dim):
    count = lax.axis_size(groups[0]) * lax.axis_size(groups[1])
    tiles = in_blocks(array, split_dim, count)
    return in_order(exchange_in_order(tiles, groups, sequence), concat_dim)


def per_device(grads, block_slot, left_stats, right_stats, left_root, right_root):
    local_rows = grads[0]
    row_dev, col_count = local_rows.shape
    block_size = left_stats.shape[2]
    block_count = col_count // block_size
    slot_count = left_stats.shape[0]
    shared_rows = left_stats.shape[1]
    total_slots = slot_count * lax.axis_size(FSDP)
    slot_ids = jnp.arange(total_slots, dtype=jnp.int32)
    matches = block_slot[None, :] == slot_ids[:, None]
    filled = jnp.any(matches, axis=1)
    source = jnp.sum(
        jnp.where(matches, jnp.arange(block_count, dtype=jnp.int32)[None, :], 0), axis=1
    )
    row_start = lax.axis_index("dp") * shared_rows
    band = local_rows.astype(jnp.float32).reshape(row_dev, block_count, block_size)
    shares = sum_at_owner(band.astype(jnp.bfloat16), "dp", 2).astype(jnp.bfloat16)
    outgoing = jnp.where(
        filled[None, :, None], jnp.take(shares, source, axis=1), jnp.zeros((), jnp.bfloat16)
    )
    incoming = lax.all_to_all(outgoing, FSDP, split_axis=1, concat_axis=0, tiled=True)
    gradient = lax.all_gather(incoming, "dp", axis=2, tiled=True)
    own_rows = lax.dynamic_slice_in_dim(gradient, row_start, shared_rows, 0)
    whole_right = lax.all_gather(right_root, "dp", axis=1, tiled=True)
    left_new = left_stats + jnp.einsum(
        "rjc,kjc->jrk", own_rows, gradient, preferred_element_type=jnp.float32
    )
    columns = lax.dynamic_slice_in_dim(gradient, row_start, shared_rows, 2)
    right_new = right_stats + jnp.einsum(
        "rjc,rjk->jck", columns, gradient, preferred_element_type=jnp.float32
    )
    left_applied = jnp.einsum(
        "jrk,kjc->rjc", left_root, gradient, preferred_element_type=jnp.float32
    ).astype(jnp.bfloat16)
    both_applied = jnp.einsum(
        "rjc,jck->rjk", left_applied, whole_right, preferred_element_type=jnp.float32
    )
    squares = lax.psum(jnp.sum(both_applied * both_applied, axis=(0, 2)), "dp")
    factor = lax.rsqrt(squares / (block_size * block_size) + epsilon)
    scaled = (both_applied * factor[None, :, None]).astype(jnp.bfloat16)
    full_rows = lax.all_gather(scaled, "dp", axis=0, tiled=True)
    returned = core_and_chips(full_rows, (("fsdp_0", "fsdp_1"), "fsdp_2"), (1, 0), 0, 1)
    update = jnp.take(returned, block_slot, axis=1).reshape(row_dev, col_count)
    return (left_new, right_new, update)


def solution(mesh):
    split = Mesh(
        mesh.devices.reshape(4, 8, 2, mesh.shape["dp"]), ("fsdp_0", "fsdp_1", "fsdp_2", "dp")
    )
    placed = (
        P("dp", FSDP, None),
        P(),
        P(FSDP, "dp", None),
        P(FSDP, "dp", None),
        P(FSDP, "dp", None),
        P(FSDP, "dp", None),
    )
    return jax.shard_map(
        per_device,
        mesh=split,
        in_specs=placed,
        out_specs=(P(FSDP, "dp", None), P(FSDP, "dp", None), P(FSDP, None)),
        check_vma=False,
    )
```

profile of v0, /device:TPU:16, one launch (start us, length us, event | category | flops | bytes accessed | tf_op | source)
XLA Modules:
  0.0 264.3 jit_solution(12434636869901836517)
XLA Ops:
  7.2 0.0 copy-start
  7.2 0.0 all-gather.6.cloned.1.call-start
  7.2 0.7 all-gather.6.cloned.1.call-update
  7.9 1.3 copy.35
  9.2 0.0 copy-start.4
  9.2 1.3 copy.27
  10.5 10.3 %all-to-all-start = ((bf16[8,16,28,128]{3,1,2,0:T(8,128)(2,1)}), bf16[8,16,28,128]{3,1,2,0:T(8,128)(2,1)S(1)}, u32[]{:S(2)}, u32[]{:S(2)}) async-start(bf16[8,16,28,128]{3,1,2,0:T(8,128)(2,1)} %copy.27), calls=%async_computation | async-start | bytes 1835008 | tf_op jit(solution)/shard_map/all_to_all | solution.py:21
  20.8 0.0 all-gather.4.cloned.1.call-start
  20.9 0.0 copy-done.4
  20.9 0.1 select_reduce_fusion
  21.0 0.1 fusion.35
  21.1 32.4 %all-to-all-done = bf16[8,16,28,128]{3,1,2,0:T(8,128)(2,1)S(1)} async-done(((bf16[8,16,28,128]{3,1,2,0:T(8,128)(2,1)}), bf16[8,16,28,128]{3,1,2,0:T(8,128)(2,1)S(1)}, u32[]{:S(2)}, u32[]{:S(2)}) %all-to-all-start) | async-done | bytes 917536 | tf_op jit(solution)/shard_map/all_to_all | solution.py:21
  53.5 0.1 reduce_sum.35
  53.6 0.6 gather_fusion
  54.2 0.2 select_bitcast_fusion
  54.4 22.2 %all_to_all.33 = bf16[16,64,128]{2,0,1:T(8,128)(2,1)} all-to-all(bf16[16,64,128]{2,0,1:T(8,128)(2,1)S(1)} %select_bitcast_fusion), channel_id=1, replica_groups=mesh['fsdp_0'=4,'fsdp_1'=8,'fsdp_2'=2,'dp'=8] {'fsdp_0','fsdp_1','fsdp_2'}, dimensions={1} | all-to-all | bytes 524288 | tf_op jit(solution)/shard_map/all_to_all | solution.py:65
  76.6 0.0 all-gather.4.cloned.1.call-update
  76.6 0.0 all-gather.8.cloned.1.call-start
  76.7 0.0 all-gather.6.cloned.1.call-done
  76.7 43.8 %all-gather.4.cloned.1.call-done = bf16[1024,1,1024]{2,0,1:T(8,128)(2,1)} async-done(((bf16[1024,1,128]{2,0,1:T(8,128)(2,1)}), bf16[1024,1,1024]{2,0,1:T(8,128)(2,1)}) %all-gather.4.cloned.1.call-update) | async-done | bytes 2097168 | tf_op jit(solution)/shard_map/all_gather | solution.py:66
  120.5 0.0 copy-done
  120.5 4.3 %multiply_reduce_fusion = (f32[]{:T(128)}, f32[128,1024]{1,0:T(8,128)S(1)}) fusion(bf16[1,1024,1024]{2,1,0:T(8,128)(2,1)} %all-gather.6.cloned.1.call-done, bf16[1024,1,1024]{2,0,1:T(8,128)(2,1)} %all-gather.4.cloned.1.call-done, bf16[1,128,1024]{2,1,0:T(8,128)(2,1)S(1)} %copy-done), kind=kOutput, calls=%fused_computation.18 | convolution fusion | flops 537264128 | bytes 4980740 | tf_op jit(solution)/shard_map/rjc,jck->rjk/dot_general | solution.py:79
  124.8 17.1 %psum.7 = f32[1]{0:T(128)} all-reduce(f32[1]{0:T(128)} %bitcast.17), channel_id=1, replica_groups=mesh['fsdp_0'=4,'fsdp_1'=8,'fsdp_2'=2,'dp'=8] {'dp'}, use_global_device_ids=true, to_apply=%region_4.5 | all-reduce | flops 1 | bytes 8 | tf_op jit(solution)/shard_map/psum | solution.py:82
  142.6 0.7 fusion.28
  143.3 0.0 all-gather.8.cloned.1.call-update
  143.4 41.8 %all-gather.8.cloned.1.call-done = bf16[1024,1,1024]{2,0,1:T(8,128)(2,1)} async-done(((bf16[128,1,1024]{2,0,1:T(8,128)(2,1)}), bf16[1024,1,1024]{2,0,1:T(8,128)(2,1)}) %all-gather.8.cloned.1.call-update) | async-done | bytes 2097168 | tf_op jit(solution)/shard_map/all_gather | solution.py:85
  185.1 1.8 copy.30
  186.9 5.4 %all_to_all.34 = bf16[32,2,16,1,1024]{4,2,0,3,1:T(8,128)(2,1)S(1)} all-to-all(bf16[32,2,16,1,1024]{4,2,0,3,1:T(8,128)(2,1)S(1)} %copy.30), channel_id=1, replica_groups=mesh['fsdp_0'=4,'fsdp_1'=8,'fsdp_2'=2,'dp'=8] {'fsdp_2'}, dimensions={1} | all-to-all | bytes 4194304 | tf_op jit(solution)/shard_map/all_to_all | solution.py:35
  192.3 1.5 copy.31
  193.8 0.0 copy-start.1
  193.8 0.0 copy-start.2
  193.8 10.1 %all-to-all-start.3 = ((bf16[32,2,16,1,1024]{4,2,1,3,0:T(8,128)(2,1)}), bf16[32,2,16,1,1024]{4,2,1,3,0:T(8,128)(2,1)}, u32[]{:S(2)}, u32[]{:S(2)}) async-start(bf16[32,2,16,1,1024]{4,2,1,3,0:T(8,128)(2,1)} %copy.31), calls=%async_computation.3 | async-start | bytes 4194304 | tf_op jit(solution)/shard_map/all_to_all | solution.py:35
  204.0 0.0 copy-start.3
  204.0 0.1 broadcast_in_dim.61
  204.1 0.1 broadcast_in_dim.62
  204.2 0.0 copy-done.1
  204.2 0.0 copy-done.2
  204.2 1.3 fusion.14
  205.5 0.0 copy-done.3
  205.5 1.6 fusion.17
  207.1 47.3 %all-to-all-done.3 = bf16[32,2,16,1,1024]{4,2,1,3,0:T(8,128)(2,1)} async-done(((bf16[32,2,16,1,1024]{4,2,1,3,0:T(8,128)(2,1)}), bf16[32,2,16,1,1024]{4,2,1,3,0:T(8,128)(2,1)}, u32[]{:S(2)}, u32[]{:S(2)}) %all-to-all-start.3) | async-done | bytes 2097184 | tf_op jit(solution)/shard_map/all_to_all | solution.py:35
  254.4 2.2 gather_fusion.1
  256.6 0.1 copy.34
  256.6 1.1 broadcast_select_fusion
  (6 shorter events, 0.0 us)
Async XLA Ops:
  7.2 113.3 %copy-start = (bf16[1,128,1024]{2,1,0:T(8,128)(2,1)S(1)}, bf16[1,128,1024]{2,1,0:T(8,128)(2,1)}, u32[]{:S(2)}) copy-start(bf16[1,128,1024]{2,1,0:T(8,128)(2,1)} %param.10) | copy-start | bytes 786436
  7.2 69.5 %all-gather.6.cloned.1.call-start = ((), (), s32[]{:S(2)}) async-start(), calls=%async_computation.5 | async-start | bytes 2359296 | tf_op jit(solution)/shard_map/all_gather | solution.py:68
  9.2 11.7 %copy-start.4 = (s32[28]{0:T(128)S(1)}, s32[28]{0:T(128)}, u32[]{:S(2)}) copy-start(s32[28]{0:T(128)} %param.7) | copy-start | bytes 340
  10.5 43.0 %all-to-all-start = ((bf16[8,16,28,128]{3,1,2,0:T(8,128)(2,1)}), bf16[8,16,28,128]{3,1,2,0:T(8,128)(2,1)S(1)}, u32[]{:S(2)}, u32[]{:S(2)}) async-start(bf16[8,16,28,128]{3,1,2,0:T(8,128)(2,1)} %copy.27), calls=%async_computation | async-start | bytes 1835008 | tf_op jit(solution)/shard_map/all_to_all | solution.py:21
  20.8 99.7 %all-gather.4.cloned.1.call-start = ((), (), s32[]{:S(2)}) async-start(), calls=%async_computation.4 | async-start | bytes 2359296 | tf_op jit(solution)/shard_map/all_gather | solution.py:66
  76.6 108.5 %all-gather.8.cloned.1.call-start = ((), (), s32[]{:S(2)}) async-start(), calls=%async_computation.6 | async-start | bytes 2359296 | tf_op jit(solution)/shard_map/all_gather | solution.py:85
  193.8 10.4 %copy-start.1 = (bf16[1024,1,1024]{2,0,1:T(8,128)(2,1)S(1)}, bf16[1024,1,1024]{2,0,1:T(8,128)(2,1)}, u32[]{:S(2)}) copy-start(bf16[1024,1,1024]{2,0,1:T(8,128)(2,1)} %all-gather.4.cloned.1.call-done) | copy-start | bytes 6291460
  193.8 10.4 %copy-start.2 = (f32[1,128,1024]{2,1,0:T(8,128)S(1)}, f32[1,128,1024]{2,1,0:T(8,128)}, u32[]{:S(2)}) copy-start(f32[1,128,1024]{2,1,0:T(8,128)} %param.9) | copy-start | bytes 1572868
  193.8 60.5 %all-to-all-start.3 = ((bf16[32,2,16,1,1024]{4,2,1,3,0:T(8,128)(2,1)}), bf16[32,2,16,1,1024]{4,2,1,3,0:T(8,128)(2,1)}, u32[]{:S(2)}, u32[]{:S(2)}) async-start(bf16[32,2,16,1,1024]{4,2,1,3,0:T(8,128)(2,1)} %copy.31), calls=%async_computation.3 | async-start | bytes 4194304 | tf_op jit(solution)/shard_map/all_to_all | solution.py:35
  204.0 1.5 copy-start.3
Sparse Core Ops, SparseCore 0:
  10.1 58.1 all-gather.5
  76.8 43.6 all-gather.3
  143.5 41.6 all-gather.7
where the time goes:
time: 265 us; the launch traced here: 264 us
  waiting for transfers between devices  166 us (63%)
  blocking collectives  44.7 us (17%)
  starting transfers between devices  20.6 us (8%)
  between operations  14.6 us (6%)
  local copies, waits for them, and re-layouts  8.89 us (3%)
  matrix products  7.23 us (3%)
    all_to_all x1, waiting for transfers between devices, exchange_in_order(): result = lax.all_to_all(result, axes[k], k, k, tiled=True)  47.3 us
    all_gather x1, waiting for transfers between devices, per_device(): gradient = lax.all_gather(incoming, 'dp', axis=2, tiled=True)  43.8 us
    all_gather x1, waiting for transfers between devices, per_device(): full_rows = lax.all_gather(scaled, 'dp', axis=0, tiled=True)  41.8 us
    all_to_all x1, waiting for transfers between devices, sum_at_owner(): tiles = lax.all_to_all(in_blocks(array, dim, count), axis, 0, 0, tiled=True)  32.4 us
    all_to_all x1, blocking collectives, per_device(): lax.all_to_all(outgoing, FSDP, split_axis=1, concat_axis=0, tiled=True)  22.2 us
    psum x1, blocking collectives, per_device(): squares = lax.psum(jnp.sum(both_applied * both_applied, axis=(0, 2)), 'dp')  17.1 us
    all_to_all x1, starting transfers between devices, sum_at_owner(): tiles = lax.all_to_all(in_blocks(array, dim, count), axis, 0, 0, tiled=True)  10.3 us
    all_to_all x1, starting transfers between devices, exchange_in_order(): result = lax.all_to_all(result, axes[k], k, k, tiled=True)  10.1 us
  transfers between devices with their start and end apart: 5, of which 4 were waited for; matrix products, arithmetic and copies ran while one was open for 3% of the time, Pallas kernels for 0%

commit v1 on v0

v1 whole, which is shorter than its diff:
```python
import jax
import jax.numpy as jnp
from jax import lax
from jax.sharding import Mesh
from jax.sharding import PartitionSpec as P

FSDP = ("fsdp_0", "fsdp_1", "fsdp_2")


epsilon = 1e-06


def per_device(grads, block_slot, left_stats, right_stats, left_root, right_root):
    rows = grads[0]
    row_dev, col_count = rows.shape
    block_size = left_stats.shape[2]
    block_count = col_count // block_size
    shared = left_stats.shape[1]
    replicas = lax.axis_size("dp")
    total_slots = lax.axis_size(FSDP)

    slot_ids = jnp.arange(total_slots, dtype=jnp.int32)
    matches = block_slot[None, :] == slot_ids[:, None]
    filled = jnp.any(matches, axis=1)
    numbers = jnp.arange(block_count, dtype=jnp.int32)
    source = jnp.sum(jnp.where(matches, numbers[None, :], 0), axis=1)

    whole_left = lax.all_gather(left_root[0], "dp", axis=0, tiled=True)

    shares = rows.reshape(row_dev, block_count, replicas, shared).transpose(2, 1, 0, 3)
    shares = shares.reshape(replicas, block_count * row_dev, shared)
    roots = right_root[0].reshape(shared, replicas, shared).transpose(1, 0, 2)
    message = jnp.concatenate([shares, roots], axis=1)
    received = lax.all_to_all(message, "dp", 0, 0, tiled=True)
    summed = jnp.sum(received[:, : block_count * row_dev].astype(jnp.float32), axis=0)
    summed = summed.astype(jnp.bfloat16).reshape(block_count, row_dev, shared)
    right_cols = received[:, block_count * row_dev :]

    outgoing = jnp.where(
        filled[:, None, None], jnp.take(summed, source, axis=0), jnp.zeros((), jnp.bfloat16)
    )
    incoming = lax.all_to_all(outgoing, FSDP, 0, 0, tiled=True)
    mine, whole_left = lax.optimization_barrier((incoming.reshape(block_size, shared), whole_left))
    gradient = lax.all_gather(mine, "dp", axis=1, tiled=True)

    inner = jnp.einsum(
        "rk,kc->rc",
        gradient,
        right_cols.reshape(block_size, shared),
        preferred_element_type=jnp.float32,
    )
    high = lax.reduce_precision(inner, 8, 7)
    low = (inner - high).astype(jnp.bfloat16)
    high = high.astype(jnp.bfloat16)
    both = jnp.einsum(
        "kr,rc->kc", whole_left, high, preferred_element_type=jnp.float32
    ) + jnp.einsum("kr,rc->kc", whole_left, low, preferred_element_type=jnp.float32)
    both = both.astype(jnp.bfloat16).reshape(total_slots, row_dev, shared)
    back = lax.all_to_all(both, FSDP, 0, 0, tiled=True)

    row_start = lax.axis_index("dp") * shared
    own_rows = lax.dynamic_slice_in_dim(gradient, row_start, shared, 0)
    left_new = left_stats + jnp.einsum(
        "rc,kc->rk", own_rows, gradient, preferred_element_type=jnp.float32
    )
    right_new = right_stats + jnp.einsum(
        "rc,rk->ck", mine, gradient, preferred_element_type=jnp.float32
    )

    wide = back.astype(jnp.float32)
    squares = lax.psum(jnp.sum(wide * wide, axis=(1, 2)), FSDP + ("dp",))
    picked = jnp.take(back, block_slot, axis=0)
    full = lax.all_gather(picked, "dp", axis=0, tiled=False)
    factor = lax.rsqrt(jnp.take(squares, block_slot) / (block_size * block_size) + epsilon)
    update = (full.astype(jnp.float32) * factor[None, :, None, None]).astype(jnp.bfloat16)
    update = update.transpose(2, 1, 0, 3).reshape(row_dev, col_count)
    return (left_new, right_new, update)


def solution(mesh):
    split = Mesh(
        mesh.devices.reshape(4, 8, 2, mesh.shape["dp"]), ("fsdp_0", "fsdp_1", "fsdp_2", "dp")
    )
    placed = (
        P("dp", FSDP, None),
        P(),
        P(FSDP, "dp", None),
        P(FSDP, "dp", None),
        P(FSDP, "dp", None),
        P(FSDP, "dp", None),
    )
    return jax.shard_map(
        per_device,
        mesh=split,
        in_specs=placed,
        out_specs=(P(FSDP, "dp", None), P(FSDP, "dp", None), P(FSDP, None)),
        check_vma=False,
    )
```

time: 265 us -> 292 us (1.10)
  the two profiles are of different devices: /device:TPU:16 before, /device:TPU:2 now
where the time goes in v1:
time: 292 us; the launch traced here: 291 us
  blocking collectives  145 us (50%)
  waiting for transfers between devices  94 us (32%)
  starting transfers between devices  20.8 us (7%)
  between operations  14.2 us (5%)
  local copies, waits for them, and re-layouts  7.68 us (3%)
  matrix products  7.32 us (3%)
    psum x1, blocking collectives, per_device(): squares = lax.psum(jnp.sum(wide * wide, axis=(1, 2)), FSDP + ('dp',))  96.1 us
    all_gather x1, waiting for transfers between devices, per_device(): gradient = lax.all_gather(mine, 'dp', axis=1, tiled=True)  42.8 us
    all_to_all x1, waiting for transfers between devices, per_device(): received = lax.all_to_all(message, 'dp', 0, 0, tiled=True)  41.9 us
    all_gather x1, blocking collectives, per_device(): full = lax.all_gather(picked, 'dp', axis=0, tiled=False)  26.4 us
    all_to_all x1, blocking collectives, per_device(): incoming = lax.all_to_all(outgoing, FSDP, 0, 0, tiled=True)  22.4 us
    all_to_all x1, starting transfers between devices, per_device(): back = lax.all_to_all(both, FSDP, 0, 0, tiled=True)  10.4 us
    all_to_all x1, starting transfers between devices, per_device(): received = lax.all_to_all(message, 'dp', 0, 0, tiled=True)  10.3 us
    all_to_all x1, waiting for transfers between devices, per_device(): back = lax.all_to_all(both, FSDP, 0, 0, tiled=True)  8.59 us
  transfers between devices with their start and end apart: 4, of which 3 were waited for; matrix products, arithmetic and copies ran while one was open for 3% of the time, Pallas kernels for 0%

profile of v1, /device:TPU:2, one launch (start us, length us, event | category | flops | bytes accessed | tf_op | source)
XLA Modules:
  0.0 291.5 jit_solution(8681560645915231170)
XLA Ops:
  7.2 0.0 all-gather.6.cloned.1.call-start
  7.2 0.7 all-gather.6.cloned.1.call-update
  7.9 1.1 copy.24
  9.0 0.2 copy.25
  9.2 1.3 copy.27
  10.5 0.4 copy.23
  10.9 0.0 copy-start.6
  10.9 1.1 pad_maximum_fusion
  12.0 10.3 %all-to-all-start = ((bf16[8,576,128]{2,1,0:T(8,128)(2,1)}), bf16[8,576,128]{2,1,0:T(8,128)(2,1)S(1)}, u32[]{:S(2)}, u32[]{:S(2)}) async-start(bf16[8,576,128]{2,1,0:T(8,128)(2,1)} %pad_maximum_fusion), calls=%async_computation | async-start | bytes 2359296 | tf_op jit(solution)/shard_map/all_to_all | solution.py:34
  22.3 0.0 all-gather.4.cloned.1.call-start
  22.4 0.0 copy-done.6
  22.4 0.1 select_reduce_fusion
  22.5 0.1 fusion.8
  22.6 41.9 %all-to-all-done = bf16[8,576,128]{2,1,0:T(8,128)(2,1)S(1)} async-done(((bf16[8,576,128]{2,1,0:T(8,128)(2,1)}), bf16[8,576,128]{2,1,0:T(8,128)(2,1)S(1)}, u32[]{:S(2)}, u32[]{:S(2)}) %all-to-all-start) | async-done | bytes 1179680 | tf_op jit(solution)/shard_map/all_to_all | solution.py:34
  64.5 0.1 slice_reduce_fusion
  64.6 0.6 gather_fusion
  65.3 0.2 select_select_fusion
  65.5 22.4 %all_to_all.15 = bf16[64,16,128]{2,1,0:T(8,128)(2,1)} all-to-all(bf16[64,16,128]{2,1,0:T(8,128)(2,1)S(1)} %select_select_fusion), channel_id=1, replica_groups=mesh['fsdp_0'=4,'fsdp_1'=8,'fsdp_2'=2,'dp'=8] {'fsdp_0','fsdp_1','fsdp_2'}, dimensions={0} | all-to-all | bytes 524288 | tf_op jit(solution)/shard_map/all_to_all | solution.py:42
  87.9 0.0 all-gather.6.cloned.1.call-done
  87.9 0.0 copy-start.1
  87.9 0.0 all-gather.4.cloned.1.call-update
  88.0 42.8 %all-gather.4.cloned.1.call-done = bf16[1024,1024]{1,0:T(8,128)(2,1)} async-done(((bf16[1024,128]{1,0:T(8,128)(2,1)}), bf16[1024,1024]{1,0:T(8,128)(2,1)}) %all-gather.4.cloned.1.call-update) | async-done | bytes 2097168 | tf_op jit(solution)/shard_map/all_gather | solution.py:44
  130.7 2.3 fusion.11
  133.0 0.0 copy-done.1
  133.0 0.0 copy-start.2
  133.0 0.7 fusion.6
  133.8 0.9 copy-done.2
  134.6 0.0 copy-start
  134.6 0.0 copy-start.4
  134.6 1.4 fusion.2
  136.1 10.4 %all-to-all-start.2 = ((bf16[64,16,128]{2,1,0:T(8,128)(2,1)}), bf16[64,16,128]{2,1,0:T(8,128)(2,1)S(1)}, u32[]{:S(2)}, u32[]{:S(2)}) async-start(bf16[64,16,128]{2,1,0:T(8,128)(2,1)} %bitcast.12), calls=%async_computation.2 | async-start | bytes 524288 | tf_op jit(solution)/shard_map/all_to_all | solution.py:59
  146.5 0.0 copy-done
  146.5 0.0 copy-done.4
  146.5 0.0 copy-start.5
  146.5 1.6 fusion
  148.1 0.0 copy-done.3
  148.1 0.0 copy-done.5
  148.1 1.3 fusion.1
  149.4 8.6 %all-to-all-done.2 = bf16[64,16,128]{2,1,0:T(8,128)(2,1)S(1)} async-done(((bf16[64,16,128]{2,1,0:T(8,128)(2,1)}), bf16[64,16,128]{2,1,0:T(8,128)(2,1)S(1)}, u32[]{:S(2)}, u32[]{:S(2)}) %all-to-all-start.2) | async-done | bytes 262176 | tf_op jit(solution)/shard_map/all_to_all | solution.py:59
  158.0 0.6 multiply_reduce_fusion
  158.6 96.1 %psum.7 = f32[64]{0:T(128)S(1)} all-reduce(f32[64]{0:T(128)S(1)} %multiply_reduce_fusion), channel_id=1, replica_groups=mesh['fsdp_0'=4,'fsdp_1'=8,'fsdp_2'=2,'dp'=8] {'fsdp_0','fsdp_1','fsdp_2..., use_global_device_ids=true, to_apply=%region_4.5 | all-reduce | flops 64 | bytes 512 | tf_op jit(solution)/shard_map/psum | solution.py:71
  254.6 0.7 gather_fusion.2
  255.3 0.6 gather_fusion.1
  255.9 0.1 bitcast_select_fusion
  256.0 26.4 %all_gather.12 = bf16[8,28,16,128]{3,2,1,0:T(8,128)(2,1)S(1)} all-gather(bf16[1,28,16,128]{3,2,1,0:T(8,128)(2,1)S(1)} %bitcast_select_fusion), channel_id=1, replica_groups=mesh['fsdp_0'=4,'fsdp_1'=8,'fsdp_2'=2,'dp'=8] {'dp'}, dimensions={0}, use_global_device_ids=true | all-gather | bytes 1032192 | tf_op jit(solution)/shard_map/all_gather | solution.py:73
  282.5 0.3 fusion.3
  282.8 0.6 copy.26
  283.4 1.3 copy.30
  (8 shorter events, 0.1 us)
Async XLA Ops:
  7.2 80.7 %all-gather.6.cloned.1.call-start = ((), (), s32[]{:S(2)}) async-start(), calls=%async_computation.4 | async-start | bytes 2359296 | tf_op jit(solution)/shard_map/all_gather | solution.py:28
  10.9 11.5 %copy-start.6 = (s32[28]{0:T(128)S(1)}, s32[28]{0:T(128)}, u32[]{:S(2)}) copy-start(s32[28]{0:T(128)} %param.7) | copy-start | bytes 340
  12.0 52.5 %all-to-all-start = ((bf16[8,576,128]{2,1,0:T(8,128)(2,1)}), bf16[8,576,128]{2,1,0:T(8,128)(2,1)S(1)}, u32[]{:S(2)}, u32[]{:S(2)}) async-start(bf16[8,576,128]{2,1,0:T(8,128)(2,1)} %pad_maximum_fusion), calls=%async_computation | async-start | bytes 2359296 | tf_op jit(solution)/shard_map/all_to_all | solution.py:34
  22.3 108.4 %all-gather.4.cloned.1.call-start = ((), (), s32[]{:S(2)}) async-start(), calls=%async_computation.3 | async-start | bytes 2359296 | tf_op jit(solution)/shard_map/all_gather | solution.py:44
  87.9 45.1 %copy-start.1 = (bf16[1,1024,1024]{2,1,0:T(8,128)(2,1)S(1)}, bf16[1,1024,1024]{2,1,0:T(8,128)(2,1)}, u32[]{:S(2)}) copy-start(bf16[1,1024,1024]{2,1,0:T(8,128)(2,1)} %all-gather.6.cloned.1.call-done) | copy-start | bytes 6291460
  133.0 1.6 copy-start.2
  134.6 11.8 %copy-start = (bf16[1024,1024]{1,0:T(8,128)(2,1)S(1)}, bf16[1024,1024]{1,0:T(8,128)(2,1)}, u32[]{:S(2)}) copy-start(bf16[1024,1024]{1,0:T(8,128)(2,1)} %all-gather.4.cloned.1.call-done) | copy-start | bytes 6291460
  134.6 11.9 %copy-start.4 = (f32[1,128,1024]{2,1,0:T(8,128)S(1)}, f32[1,128,1024]{2,1,0:T(8,128)}, u32[]{:S(2)}) copy-start(f32[1,128,1024]{2,1,0:T(8,128)} %param.8) | copy-start | bytes 1572868
  136.1 12.1 %copy-start.3 = (bf16[64,16,128]{2,1,0:T(8,128)(2,1)S(1)}, bf16[64,16,128]{2,1,0:T(8,128)(2,1)}, u32[]{:S(2)}) copy-start(bf16[64,16,128]{2,1,0:T(8,128)(2,1)} %all_to_all.15) | copy-start | bytes 786436
  136.1 21.9 %all-to-all-start.2 = ((bf16[64,16,128]{2,1,0:T(8,128)(2,1)}), bf16[64,16,128]{2,1,0:T(8,128)(2,1)S(1)}, u32[]{:S(2)}, u32[]{:S(2)}) async-start(bf16[64,16,128]{2,1,0:T(8,128)(2,1)} %bitcast.12), calls=%async_computation.2 | async-start | bytes 524288 | tf_op jit(solution)/shard_map/all_to_all | solution.py:59
  146.5 1.7 copy-start.5
Sparse Core Ops, SparseCore 0:
  10.1 64.5 all-gather.5
  88.0 42.6 all-gather.3

commit v2 on v1

--- a/solution.py
+++ b/solution.py
@@ -8,6 +8,13 @@
 
 
 epsilon = 1e-06
+
+
+def split_terms(value):
+    high = lax.reduce_precision(value, 8, 7)
+    middle = lax.reduce_precision(value - high, 8, 7)
+    low = (value - high) - middle
+    return [term.astype(jnp.bfloat16) for term in (high, middle, low)]
 
 
 def per_device(grads, block_slot, left_stats, right_stats, left_root, right_root):
@@ -55,8 +62,11 @@
     both = jnp.einsum(
         "kr,rc->kc", whole_left, high, preferred_element_type=jnp.float32
     ) + jnp.einsum("kr,rc->kc", whole_left, low, preferred_element_type=jnp.float32)
+    partial = split_terms(jnp.sum(both * both))
+    lanes = jnp.concatenate([jnp.stack(partial), jnp.zeros(shared - 3, jnp.bfloat16)])
+    marks = jnp.broadcast_to(lanes[None, None, :], (total_slots, 8, shared))
     both = both.astype(jnp.bfloat16).reshape(total_slots, row_dev, shared)
-    back = lax.all_to_all(both, FSDP, 0, 0, tiled=True)
+    back = lax.all_to_all(jnp.concatenate([both, marks], axis=1), FSDP, 0, 0, tiled=True)
 
     row_start = lax.axis_index("dp") * shared
     own_rows = lax.dynamic_slice_in_dim(gradient, row_start, shared, 0)
@@ -67,11 +77,14 @@
         "rc,rk->ck", mine, gradient, preferred_element_type=jnp.float32
     )
 
-    wide = back.astype(jnp.float32)
-    squares = lax.psum(jnp.sum(wide * wide, axis=(1, 2)), FSDP + ("dp",))
     picked = jnp.take(back, block_slot, axis=0)
-    full = lax.all_gather(picked, "dp", axis=0, tiled=False)
-    factor = lax.rsqrt(jnp.take(squares, block_slot) / (block_size * block_size) + epsilon)
+    terms = jnp.zeros((32, shared), jnp.bfloat16).at[:block_count].set(picked[:, row_dev, :])
+    tiles = picked[:, :row_dev].reshape(block_count * row_dev, shared)
+    gathered = lax.all_gather(jnp.concatenate([tiles, terms]), "dp", axis=0, tiled=False)
+    full = gathered[:, : block_count * row_dev].reshape(replicas, block_count, row_dev, shared)
+    terms = gathered[:, block_count * row_dev :][:, :block_count, :3].astype(jnp.float32)
+    squares = jnp.sum(terms, axis=(0, 2))
+    factor = lax.rsqrt(squares / (block_size * block_size) + epsilon)
     update = (full.astype(jnp.float32) * factor[None, :, None, None]).astype(jnp.bfloat16)
     update = update.transpose(2, 1, 0, 3).reshape(row_dev, col_count)
     return (left_new, right_new, update)

time: 292 us -> 204 us (0.70)
  the two profiles are of different devices: /device:TPU:2 before, /device:TPU:8 now
where the time goes in v2:
time: 204 us; the launch traced here: 203 us
  waiting for transfers between devices  96.7 us (47%)
  blocking collectives  49.1 us (24%)
  starting transfers between devices  20.8 us (10%)
  between operations  19.2 us (9%)
  matrix products  7.21 us (4%)
  local copies, waits for them, and re-layouts  7.09 us (3%)
  other arithmetic  3.03 us (1%)
    all_gather x1, waiting for transfers between devices, per_device(): gradient = lax.all_gather(mine, 'dp', axis=1, tiled=True)  42.6 us
    all_to_all x1, waiting for transfers between devices, per_device(): received = lax.all_to_all(message, 'dp', 0, 0, tiled=True)  42 us
    all_gather x1, blocking collectives, per_device(): lax.all_gather(jnp.concatenate([tiles, terms]), 'dp', axis=0, tiled=False)  26.6 us
    all_to_all x1, blocking collectives, per_device(): incoming = lax.all_to_all(outgoing, FSDP, 0, 0, tiled=True)  22.5 us
    all_to_all x1, waiting for transfers between devices, per_device(): lax.all_to_all(jnp.concatenate([both, marks], axis=1), FSDP, 0, 0, tiled=...  11.5 us
    all_to_all x1, starting transfers between devices, per_device(): lax.all_to_all(jnp.concatenate([both, marks], axis=1), FSDP, 0, 0, tiled=...  10.4 us
    all_to_all x1, starting transfers between devices, per_device(): received = lax.all_to_all(message, 'dp', 0, 0, tiled=True)  10.3 us
    unnamed x18, local copies, waits for them, and re-layouts  4.6 us
  transfers between devices with their start and end apart: 4, of which 3 were waited for; matrix products, arithmetic and copies ran while one was open for 4% of the time, Pallas kernels for 0%

profile of v2, /device:TPU:8, one launch (start us, length us, event | category | flops | bytes accessed | tf_op | source)
XLA Modules:
  0.0 203.1 jit_solution(17511728519001342608)
XLA Ops:
  7.2 0.0 all-gather.7.cloned.1.call-start
  7.2 0.7 all-gather.7.cloned.1.call-update
  7.9 1.1 copy.15
  9.0 0.2 copy.16
  9.2 1.3 copy.19
  10.5 0.4 copy.14
  10.9 0.0 copy-start.6
  10.9 1.1 pad_maximum_fusion
  12.0 10.3 %all-to-all-start = ((bf16[8,576,128]{2,1,0:T(8,128)(2,1)}), bf16[8,576,128]{2,1,0:T(8,128)(2,1)S(1)}, u32[]{:S(2)}, u32[]{:S(2)}) async-start(bf16[8,576,128]{2,1,0:T(8,128)(2,1)} %pad_maximum_fusion), calls=%async_computation | async-start | bytes 2359296 | tf_op jit(solution)/shard_map/all_to_all | solution.py:41
  22.3 0.0 all-gather.5.cloned.1.call-start
  22.4 0.0 copy-done.6
  22.4 0.1 select_reduce_fusion
  22.5 0.1 fusion.10
  22.6 42.0 %all-to-all-done = bf16[8,576,128]{2,1,0:T(8,128)(2,1)S(1)} async-done(((bf16[8,576,128]{2,1,0:T(8,128)(2,1)}), bf16[8,576,128]{2,1,0:T(8,128)(2,1)S(1)}, u32[]{:S(2)}, u32[]{:S(2)}) %all-to-all-start) | async-done | bytes 1179680 | tf_op jit(solution)/shard_map/all_to_all | solution.py:41
  64.5 0.1 slice_reduce_fusion
  64.7 0.6 gather_fusion
  65.3 0.2 select_select_fusion
  65.5 22.5 %all_to_all.15 = bf16[64,16,128]{2,1,0:T(8,128)(2,1)} all-to-all(bf16[64,16,128]{2,1,0:T(8,128)(2,1)S(1)} %select_select_fusion), channel_id=1, replica_groups=mesh['fsdp_0'=4,'fsdp_1'=8,'fsdp_2'=2,'dp'=8] {'fsdp_0','fsdp_1','fsdp_2'}, dimensions={0} | all-to-all | bytes 524288 | tf_op jit(solution)/shard_map/all_to_all | solution.py:49
  88.0 0.0 all-gather.7.cloned.1.call-done
  88.0 0.0 copy-start.1
  88.0 0.0 all-gather.5.cloned.1.call-update
  88.0 42.6 %all-gather.5.cloned.1.call-done = bf16[1024,1024]{1,0:T(8,128)(2,1)} async-done(((bf16[1024,128]{1,0:T(8,128)(2,1)}), bf16[1024,1024]{1,0:T(8,128)(2,1)}) %all-gather.5.cloned.1.call-update) | async-done | bytes 2097168 | tf_op jit(solution)/shard_map/all_gather | solution.py:51
  130.7 2.3 %fusion.14 = f32[1024,128]{1,0:T(8,128)S(1)} fusion(bf16[1024,1024]{1,0:T(8,128)(2,1)} %all-gather.5.cloned.1.call-done, bf16[1024,128]{1,0:T(8,128)(2,1)S(1)} %bitcast.64), kind=kOutput, calls=%fused_computation.42 | convolution fusion | flops 268435456 | bytes 2883584 | tf_op jit(solution)/shard_map/rk,kc->rc/dot_general | solution.py:53
  133.0 0.0 copy-done.1
  133.0 0.0 copy-start.2
  133.0 0.7 fusion.6
  133.7 0.9 copy-done.2
  134.6 0.0 copy-start
  134.6 1.3 fusion.13
  140.8 0.1 pad_maximum_fusion.2
  140.9 0.8 pad_maximum_fusion.1
  141.7 10.4 %all-to-all-start.2 = ((bf16[64,24,128]{2,1,0:T(8,128)(2,1)}), bf16[64,24,128]{2,1,0:T(8,128)(2,1)S(1)}, u32[]{:S(2)}, u32[]{:S(2)}) async-start(bf16[64,24,128]{2,1,0:T(8,128)(2,1)} %pad_maximum_fusion.1), calls=%async_computation.2 | async-start | bytes 786432 | tf_op jit(solution)/shard_map/all_to_all | solution.py:69
  152.1 0.0 copy-start.5
  152.1 0.0 copy-done
  152.2 0.0 copy-done.4
  152.2 1.6 fusion.1
  153.8 0.0 copy-done.3
  153.8 0.0 copy-done.5
  153.8 1.3 fusion.2
  155.1 11.5 %all-to-all-done.2 = bf16[64,24,128]{2,1,0:T(8,128)(2,1)S(1)} async-done(((bf16[64,24,128]{2,1,0:T(8,128)(2,1)}), bf16[64,24,128]{2,1,0:T(8,128)(2,1)S(1)}, u32[]{:S(2)}, u32[]{:S(2)}) %all-to-all-start.2) | async-done | bytes 393248 | tf_op jit(solution)/shard_map/all_to_all | solution.py:69
  166.5 0.6 gather_fusion.1
  167.1 0.1 broadcast_select_fusion
  167.3 26.6 %all-gather.1 = bf16[3840,128]{1,0:T(8,128)(2,1)S(1)} all-gather(bf16[480,128]{1,0:T(8,128)(2,1)S(1)} %fusion.9), channel_id=3, replica_groups=mesh['fsdp_0'=4,'fsdp_1'=8,'fsdp_2'=2,'dp'=8] {'dp'}, dimensions={0}, use_global_device_ids=true | all-gather | bytes 1105920 | tf_op jit(solution)/shard_map/all_gather | solution.py:83
  193.9 0.1 convert_reduce_fusion
  194.1 0.1 slice.50
  194.2 0.3 fusion.3
  194.4 0.6 copy.17
  195.0 1.3 copy.23
  (16 shorter events, 0.1 us)
Async XLA Ops:
  7.2 80.8 %all-gather.7.cloned.1.call-start = ((), (), s32[]{:S(2)}) async-start(), calls=%async_computation.4 | async-start | bytes 2359296 | tf_op jit(solution)/shard_map/all_gather | solution.py:35
  10.9 11.5 %copy-start.6 = (s32[28]{0:T(128)S(1)}, s32[28]{0:T(128)}, u32[]{:S(2)}) copy-start(s32[28]{0:T(128)} %param.9) | copy-start | bytes 340
  12.0 52.5 %all-to-all-start = ((bf16[8,576,128]{2,1,0:T(8,128)(2,1)}), bf16[8,576,128]{2,1,0:T(8,128)(2,1)S(1)}, u32[]{:S(2)}, u32[]{:S(2)}) async-start(bf16[8,576,128]{2,1,0:T(8,128)(2,1)} %pad_maximum_fusion), calls=%async_computation | async-start | bytes 2359296 | tf_op jit(solution)/shard_map/all_to_all | solution.py:41
  22.3 108.3 %all-gather.5.cloned.1.call-start = ((), (), s32[]{:S(2)}) async-start(), calls=%async_computation.3 | async-start | bytes 2359296 | tf_op jit(solution)/shard_map/all_gather | solution.py:51
  88.0 45.0 %copy-start.1 = (bf16[1,1024,1024]{2,1,0:T(8,128)(2,1)S(1)}, bf16[1,1024,1024]{2,1,0:T(8,128)(2,1)}, u32[]{:S(2)}) copy-start(bf16[1,1024,1024]{2,1,0:T(8,128)(2,1)} %all-gather.7.cloned.1.call-done) | copy-start | bytes 6291460
  133.0 1.6 copy-start.2
  134.6 17.6 %copy-start = (bf16[1024,1024]{1,0:T(8,128)(2,1)S(1)}, bf16[1024,1024]{1,0:T(8,128)(2,1)}, u32[]{:S(2)}) copy-start(bf16[1024,1024]{1,0:T(8,128)(2,1)} %all-gather.5.cloned.1.call-done) | copy-start | bytes 6291460
  134.6 17.6 %copy-start.4 = (f32[1,128,1024]{2,1,0:T(8,128)S(1)}, f32[1,128,1024]{2,1,0:T(8,128)}, u32[]{:S(2)}) copy-start(f32[1,128,1024]{2,1,0:T(8,128)} %param.10) | copy-start | bytes 1572868
  141.7 12.1 %copy-start.3 = (bf16[64,16,128]{2,1,0:T(8,128)(2,1)S(1)}, bf16[64,16,128]{2,1,0:T(8,128)(2,1)}, u32[]{:S(2)}) copy-start(bf16[64,16,128]{2,1,0:T(8,128)(2,1)} %all_to_all.15) | copy-start | bytes 786436
  141.7 24.8 %all-to-all-start.2 = ((bf16[64,24,128]{2,1,0:T(8,128)(2,1)}), bf16[64,24,128]{2,1,0:T(8,128)(2,1)S(1)}, u32[]{:S(2)}, u32[]{:S(2)}) async-start(bf16[64,24,128]{2,1,0:T(8,128)(2,1)} %pad_maximum_fusion.1), calls=%async_computation.2 | async-start | bytes 786432 | tf_op jit(solution)/shard_map/all_to_all | solution.py:69
  152.1 1.7 copy-start.5
Sparse Core Ops, SparseCore 0:
  10.1 64.5 all-gather.6
  88.1 42.4 all-gather.4

commit v3 on v2

v3 whole, which is shorter than its diff:
```python
import functools

import jax
import jax.numpy as jnp
from jax import lax
from jax.experimental import pallas as pl
from jax.experimental.pallas import tpu as pltpu
from jax.sharding import Mesh
from jax.sharding import PartitionSpec as P


FSDP = ("fsdp_0", "fsdp_1", "fsdp_2")


epsilon = 1e-06
VMEM = pl.BlockSpec(memory_space=pltpu.VMEM)


def ring(array, axis, step):
    count = lax.axis_size(axis)
    return lax.ppermute(array, axis, [(i, (i + step) % count) for i in range(count)])


def offsets(count):
    return [0] + [-s for s in range(1, count // 2 + 1)] + list(range(1, (count + 1) // 2))


def ring_gather(array, axis):
    count = lax.axis_size(axis)
    up, down, ups, downs = array, array, [], []
    for s in range(1, count // 2 + 1):
        up = ring(up, axis, 1)
        ups.append(up)
        if s < (count + 1) // 2:
            down = ring(down, axis, -1)
            downs.append(down)
    return [array] + ups + downs


def dot(a, b, dims=((1,), (0,))):
    return lax.dot_general(a, b, (dims, ((), ())), preferred_element_type=jnp.float32)


def roots_kernel(count, left, right, *outs):
    me = lax.axis_index("dp")
    half = left.shape[0] // 2
    rows = right.shape[0] // 4
    width = right.shape[1] // 4
    for k, out in enumerate(outs):
        target = (me + k) % count
        upper = (target // 4) > 0
        start = pl.multiple_of((target % 4) * width, width)
        for f in range(half // 8):
            low, high = left[16 * f : 16 * f + 8, :], left[16 * f + 8 : 16 * f + 16, :]
            out[8 * f : 8 * f + 8, :] = jnp.where(upper, high, low)
        for g in range(4):
            out[half:, g * width : (g + 1) * width] = right[g * rows : (g + 1) * rows, pl.ds(start, width)]


def precondition_kernel(count, *refs):
    shards, roots, (out,) = refs[:count], refs[count : 2 * count], refs[2 * count :]
    me = lax.axis_index("dp")
    width = shards[0].shape[1]
    half = 64
    quarter = roots[0].shape[1] // 4

    def right(i):
        return [roots[i][half:, g * quarter : (g + 1) * quarter] for g in range(4)]

    inner = None
    for i in range(0, count, 2):
        pair = jnp.concatenate([shards[i][...], shards[i + 1][...]], axis=1)
        term = dot(pair, jnp.concatenate(right(i) + right(i + 1), axis=0))
        inner = term if inner is None else inner + term
    high = inner.astype(jnp.bfloat16)
    low = (inner - high.astype(jnp.float32)).astype(jnp.bfloat16)
    left = jnp.concatenate([root[:half, :] for root in roots], axis=0)
    both = dot(left, high) + dot(left, low)
    total = jnp.sum(jnp.sum(both * both, axis=0, keepdims=True), axis=1, keepdims=True)
    first = total.astype(jnp.bfloat16).astype(jnp.float32)
    second = (total - first).astype(jnp.bfloat16).astype(jnp.float32)
    third = (total - first) - second
    lane = lax.broadcasted_iota(jnp.int32, (8, width), 1)
    marks = jnp.where(lane == 0, first, jnp.where(lane == 1, second, jnp.where(lane == 2, third, 0.0)))
    for i, offset in enumerate(offsets(count)):
        start = ((me + offset + count) % count) * 8
        rows = both[i * half : (i + 1) * half]
        for part in range(2):
            tile = rows[:, part * width : (part + 1) * width].reshape(8, 8, width)
            out[pl.ds(start, 8), part * 8 : (part + 1) * 8, :] = tile.astype(jnp.bfloat16)
    out[:, 16:24, :] = jnp.broadcast_to(marks.astype(jnp.bfloat16)[None], (out.shape[0], 8, width))


def statistics_kernel(count, *refs):
    shards, (left, right, left_out, right_out) = refs[:count], refs[count:]
    me = lax.axis_index("dp")
    width = shards[0].shape[1]
    own = pl.multiple_of(me * width, width)
    total = left[0]
    for offset, shard in zip(offsets(count), shards):
        start = pl.multiple_of(((me + offset + count) % count) * width, width)
        total = total + dot(shard[pl.ds(own, width), :], shard[...], ((1,), (1,)))
        right_out[0, :, pl.ds(start, width)] = right[0, :, pl.ds(start, width)] + dot(
            shards[0][...], shard[...], ((0,), (0,))
        )
    left_out[0] = total


def step(grads, block_slot, left_stats, right_stats, left_root, right_root):
    rows = grads[0]
    row_dev, col_count = rows.shape
    block_size = left_stats.shape[2]
    block_count = col_count // block_size
    shared = left_stats.shape[1]
    replicas = lax.axis_size("dp")
    total_slots = lax.axis_size(FSDP)
    half_rows = row_dev // 2
    quarters = replicas // 2

    slot_ids = jnp.arange(total_slots, dtype=jnp.int32)
    matches = block_slot[None, :] == slot_ids[:, None]
    filled = jnp.any(matches, axis=1)
    numbers = jnp.arange(block_count, dtype=jnp.int32)
    source = jnp.sum(jnp.where(matches, numbers[None, :], 0), axis=1)

    shares = rows.reshape(row_dev, block_count, replicas, shared).transpose(2, 1, 0, 3)
    shares = shares.reshape(replicas, block_count * row_dev, shared)
    received = lax.all_to_all(shares, "dp", 0, 0, tiled=True)

    pieces = pl.pallas_call(
        functools.partial(roots_kernel, replicas),
        out_shape=[jax.ShapeDtypeStruct((3 * shared // 4, block_size), jnp.bfloat16)] * replicas,
        in_specs=[VMEM] * 2,
        out_specs=[VMEM] * replicas,
    )(left_root[0], right_root[0])
    arrived = {0: pieces[0]}
    for k in (4, 3, 5, 2, 6, 1, 7):
        arrived[k] = ring(pieces[k], "dp", k)
    roots = [arrived[-offset % replicas] for offset in offsets(replicas)]

    summed = jnp.sum(received.astype(jnp.float32), axis=0)
    summed = summed.astype(jnp.bfloat16).reshape(block_count, row_dev, shared)
    outgoing = jnp.where(
        filled[:, None, None], jnp.take(summed, source, axis=0), jnp.zeros((), jnp.bfloat16)
    )
    incoming = lax.all_to_all(outgoing, FSDP, 0, 0, tiled=True)
    shards = ring_gather(incoming.reshape(block_size, shared), "dp")

    message = pl.pallas_call(
        functools.partial(precondition_kernel, replicas),
        out_shape=jax.ShapeDtypeStruct((total_slots, row_dev + 8, shared), jnp.bfloat16),
        in_specs=[VMEM] * (2 * replicas),
        out_specs=VMEM,
    )(*shards, *roots)
    back = lax.all_to_all(message, FSDP, 0, 0, tiled=True)

    left_new, right_new = pl.pallas_call(
        functools.partial(statistics_kernel, replicas),
        out_shape=[jax.ShapeDtypeStruct(left_stats.shape, jnp.float32)] * 2,
        in_specs=[VMEM] * (replicas + 2),
        out_specs=[VMEM] * 2,
    )(*shards, left_stats, right_stats)

    picked = jnp.take(back, block_slot, axis=0)
    terms = jnp.zeros((32, shared), jnp.bfloat16).at[:block_count].set(picked[:, row_dev, :])
    tiles = picked[:, :row_dev].reshape(block_count * row_dev, shared)
    gathered = lax.all_gather(jnp.concatenate([tiles, terms]), "dp", axis=0, tiled=False)
    terms = gathered[:, block_count * row_dev :][:, :block_count, :3].astype(jnp.float32)
    squares = jnp.sum(terms, axis=(0, 2))
    factor = lax.rsqrt(squares / (block_size * block_size) + epsilon)
    full = gathered[:, : block_count * row_dev]
    full = full.reshape(2, quarters, block_count, 2, half_rows, shared).astype(jnp.float32)
    update = (full * factor[None, None, :, None, None, None]).astype(jnp.bfloat16)
    update = update.transpose(0, 4, 2, 1, 3, 5).reshape(row_dev, col_count)
    return (left_new, right_new, update)


def solution(mesh):
    split = Mesh(
        mesh.devices.reshape(4, 8, 2, mesh.shape["dp"]), ("fsdp_0", "fsdp_1", "fsdp_2", "dp")
    )
    placed = (
        P("dp", FSDP, None),
        P(),
        P(FSDP, "dp", None),
        P(FSDP, "dp", None),
        P(FSDP, "dp", None),
        P(FSDP, "dp", None),
    )
    return jax.shard_map(
        step,
        mesh=split,
        in_specs=placed,
        out_specs=(P(FSDP, "dp", None), P(FSDP, "dp", None), P(FSDP, None)),
        check_vma=False,
    )
```

time: 204 us -> 199 us (0.975)
  starting transfers between devices: 20.8 us -> 57.8 us
  waiting for transfers between devices: 96.7 us -> 73 us
  between operations: 19.2 us -> 1.05 us
  Pallas kernels: 0 us -> 11.3 us
  matrix products: 7.21 us -> 0 us
    all_gather x2 -> x0, waiting for transfers between devices: 42.6 us -> none  [the longest x1 42.6 us: per_device(): gradient = lax.all_gather(mine, 'dp', axis=1, tiled=True)]
    ppermute x0 -> x14, starting transfers between devices: none -> 41.3 us  [ring(): lax.ppermute(array, axis, [(i, (i + step) % count) for i in range(count)])]
    ppermute x0 -> x14, waiting for transfers between devices: none -> 36.9 us  [ring(): lax.ppermute(array, axis, [(i, (i + step) % count) for i in range(count)])]
    all_to_all x2, waiting for transfers between devices: 53.4 us -> 36.1 us  [the longest x1 25.7 us: step(): received = lax.all_to_all(shares, 'dp', 0, 0, tiled=True)]
    pallas_call x0 -> x3, Pallas kernels: none -> 11.3 us  [the longest x1 5.06 us: step(): pl.pallas_call(functools.partial(precondition_kernel, replicas), out_shap...]
    dot_general x5 -> x0, matrix products: 7.21 us -> none  [the longest x1 2.29 us: per_device(): jnp.einsum('rk,kc->rc', gradient, right_cols.reshape(block_size, shared),...]
    all_to_all x2, starting transfers between devices: 20.7 us -> 16.4 us  [the longest x1 10.4 us: step(): received = lax.all_to_all(shares, 'dp', 0, 0, tiled=True)]
    unnamed x18 -> x34, local copies, waits for them, and re-layouts: 4.6 us -> 2.08 us
  transfers between devices with their start and end apart: 4 -> 16, of which waited for: 3 -> 9; matrix products, arithmetic and copies ran while one was open for 4% -> 0% of each run, Pallas kernels for 0% -> 3%
where the time goes in v3:
time: 199 us
  waiting for transfers between devices  73 us (37%)
  starting transfers between devices  57.8 us (29%)
  blocking collectives  48.7 us (24%)
  Pallas kernels  11.3 us (6%)
  local copies, waits for them, and re-layouts  5.86 us (3%)
    ppermute x14, starting transfers between devices, ring(): lax.ppermute(array, axis, [(i, (i + step) % count) for i in range(count)])  41.3 us
    ppermute x14, waiting for transfers between devices, ring(): lax.ppermute(array, axis, [(i, (i + step) % count) for i in range(count)])  36.9 us
    all_gather x1, blocking collectives, step(): lax.all_gather(jnp.concatenate([tiles, terms]), 'dp', axis=0, tiled=False)  26.6 us
    all_to_all x1, waiting for transfers between devices, step(): received = lax.all_to_all(shares, 'dp', 0, 0, tiled=True)  25.7 us
    all_to_all x1, blocking collectives, step(): incoming = lax.all_to_all(outgoing, FSDP, 0, 0, tiled=True)  22.1 us
    all_to_all x1, starting transfers between devices, step(): received = lax.all_to_all(shares, 'dp', 0, 0, tiled=True)  10.4 us
    all_to_all x1, waiting for transfers between devices, step(): back = lax.all_to_all(message, FSDP, 0, 0, tiled=True)  10.4 us
    all_to_all x1, starting transfers between devices, step(): back = lax.all_to_all(message, FSDP, 0, 0, tiled=True)  6 us
  transfers between devices with their start and end apart: 16, of which 9 were waited for; matrix products, arithmetic and copies ran while one was open for 0% of the time, Pallas kernels for 3%

profile of v3, /device:TPU:8, one launch (start us, length us, event | category | flops | bytes accessed | tf_op | source)
XLA Modules:
  0.0 198.7 jit_solution(14720377540603572262)
XLA Ops:
  0.6 1.3 copy.14
  1.9 1.3 copy.11
  3.2 10.4 %all-to-all-start = ((bf16[8,448,128]{2,1,0:T(8,128)(2,1)}), bf16[8,448,128]{2,1,0:T(8,128)(2,1)S(1)}, u32[]{:S(2)}, u32[]{:S(2)}) async-start(bf16[8,448,128]{2,1,0:T(8,128)(2,1)} %bitcast.1), calls=%async_computation | async-start | bytes 1835008 | tf_op jit(solution)/shard_map/all_to_all | solution.py:128
  13.7 0.1 select_reduce_fusion
  13.8 0.1 fusion.4
  13.9 25.7 %all-to-all-done = bf16[8,448,128]{2,1,0:T(8,128)(2,1)S(1)} async-done(((bf16[8,448,128]{2,1,0:T(8,128)(2,1)}), bf16[8,448,128]{2,1,0:T(8,128)(2,1)S(1)}, u32[]{:S(2)}, u32[]{:S(2)}) %all-to-all-start) | async-done | bytes 917536 | tf_op jit(solution)/shard_map/all_to_all | solution.py:128
  39.6 0.1 reduce_sum.33
  39.7 0.6 gather_fusion
  40.3 0.2 select_select_fusion
  40.6 22.1 %all_to_all.15 = bf16[64,16,128]{2,1,0:T(8,128)(2,1)S(1)} all-to-all(bf16[64,16,128]{2,1,0:T(8,128)(2,1)S(1)} %select_select_fusion), channel_id=1, replica_groups=mesh['fsdp_0'=4,'fsdp_1'=8,'fsdp_2'=2,'dp'=8] {'fsdp_0','fsdp_1','fsdp_2'}, dimensions={0} | all-to-all | bytes 524288 | tf_op jit(solution)/shard_map/all_to_all | solution.py:146
  62.6 2.5 %collective-permute-start = (bf16[1024,128]{1,0:T(8,128)(2,1)S(1)}, bf16[1024,128]{1,0:T(8,128)(2,1)S(1)}, u32[]{:S(2)}, u32[]{:S(2)}) collective-permute-start(bf16[1024,128]{1,0:T(8,128)(2,1)S(1)} %bitcast.29), channel_id=1, source_target_pairs={{0,1},{1,2},{2,3},{3,4},{4,5},{5,6},{6,7},{7,0},{8,9},{9,10},{10,1... | collective-permute-start | bytes 786440 | tf_op jit(solution)/shard_map/ppermute | solution.py:21
  65.1 4.6 %collective-permute-start.4 = (bf16[1024,128]{1,0:T(8,128)(2,1)S(1)}, bf16[1024,128]{1,0:T(8,128)(2,1)S(1)}, u32[]{:S(2)}, u32[]{:S(2)}) collective-permute-start(bf16[1024,128]{1,0:T(8,128)(2,1)S(1)} %bitcast.30), channel_id=1, source_target_pairs={{0,7},{1,0},{2,1},{3,2},{4,3},{5,4},{6,5},{7,6},{8,15},{9,8},{10,9... | collective-permute-start | bytes 786440 | tf_op jit(solution)/shard_map/ppermute | solution.py:21
  69.7 4.4 %collective-permute-done.refs_1_ = bf16[1024,128]{1,0:T(8,128)(2,1)S(1)} collective-permute-done((bf16[1024,128]{1,0:T(8,128)(2,1)S(1)}, bf16[1024,128]{1,0:T(8,128)(2,1)S(1)}, u32[]{:S(2)}, u32[]{:S(2)}) %collective-permute-start) | collective-permute-done | bytes 262176 | tf_op jit(solution)/shard_map/ppermute | solution.py:21
  74.1 1.9 collective-permute-start.1
  76.0 2.2 %shard_map.86 = (bf16[96,1024]{1,0:T(8,128)(2,1)}, bf16[96,1024]{1,0:T(8,128)(2,1)}, bf16[96,1024]{1,0:T(8,128)(2,1)}, bf16[96,1024]{1,0:T(8,128)(2,1)}, bf16[96...) custom-call(bf16[128,1024]{1,0:T(8,128)(2,1)} %bitcast.37, ...), custom_call_target="tpu_custom_call" | custom-call | tf_op jit(solution)/shard_map/pallas_call | solution.py:130
  78.2 2.7 %collective-permute-start.10 = (bf16[96,1024]{1,0:T(8,128)(2,1)}, bf16[96,1024]{1,0:T(8,128)(2,1)S(1)}, u32[]{:S(2)}, u32[]{:S(2)}) collective-permute-start(bf16[96,1024]{1,0:T(8,128)(2,1)} %get-tuple-element.31), channel_id=1, source_target_pairs={{0,4},{1,5},{2,6},{3,7},{4,0},{5,1},{6,2},{7,3},{8,12},{9,13},{10,... | collective-permute-start | bytes 589832 | tf_op jit(solution)/shard_map/ppermute | solution.py:21
  81.0 4.9 %collective-permute-start.5 = (bf16[1024,128]{1,0:T(8,128)(2,1)S(1)}, bf16[1024,128]{1,0:T(8,128)(2,1)S(1)}, u32[]{:S(2)}, u32[]{:S(2)}) collective-permute-start(bf16[1024,128]{1,0:T(8,128)(2,1)S(1)} %collective-permute-done.4.refs_5_), channel_id=1, source_target_pairs={{0,7},{1,0},{2,1},{3,2},{4,3},{5,4},{6,5},{7,6},{8,15},{9,8},{10,9... | collective-permute-start | bytes 786440 | tf_op jit(solution)/shard_map/ppermute | solution.py:21
  85.9 4.2 %collective-permute-done.1.refs_2_ = bf16[1024,128]{1,0:T(8,128)(2,1)S(1)} collective-permute-done((bf16[1024,128]{1,0:T(8,128)(2,1)S(1)}, bf16[1024,128]{1,0:T(8,128)(2,1)S(1)}, u32[]{:S(2)}, u32[]{:S(2)}) %collective-permute-start.1) | collective-permute-done | bytes 262176 | tf_op jit(solution)/shard_map/ppermute | solution.py:21
  90.1 1.9 collective-permute-start.2
  92.0 5.1 %collective-permute-start.11 = (bf16[96,1024]{1,0:T(8,128)(2,1)}, bf16[96,1024]{1,0:T(8,128)(2,1)S(1)}, u32[]{:S(2)}, u32[]{:S(2)}) collective-permute-start(bf16[96,1024]{1,0:T(8,128)(2,1)} %get-tuple-element.32), channel_id=1, source_target_pairs={{0,7},{1,0},{2,1},{3,2},{4,3},{5,4},{6,5},{7,6},{8,15},{9,8},{10,9... | collective-permute-start | bytes 589832 | tf_op jit(solution)/shard_map/ppermute | solution.py:21
  97.2 1.9 collective-permute-start.12
  99.1 0.0 collective-permute-done.10.refs_12_
  99.1 3.1 %collective-permute-start.13 = (bf16[96,1024]{1,0:T(8,128)(2,1)}, bf16[96,1024]{1,0:T(8,128)(2,1)S(1)}, u32[]{:S(2)}, u32[]{:S(2)}) collective-permute-start(bf16[96,1024]{1,0:T(8,128)(2,1)} %get-tuple-element.34), channel_id=1, source_target_pairs={{0,5},{1,6},{2,7},{3,0},{4,1},{5,2},{6,3},{7,4},{8,13},{9,14},{10,... | collective-permute-start | bytes 589832 | tf_op jit(solution)/shard_map/ppermute | solution.py:21
  102.2 2.5 %collective-permute-start.6 = (bf16[1024,128]{1,0:T(8,128)(2,1)S(1)}, bf16[1024,128]{1,0:T(8,128)(2,1)S(1)}, u32[]{:S(2)}, u32[]{:S(2)}) collective-permute-start(bf16[1024,128]{1,0:T(8,128)(2,1)S(1)} %collective-permute-done.5.refs_6_), channel_id=1, source_target_pairs={{0,7},{1,0},{2,1},{3,2},{4,3},{5,4},{6,5},{7,6},{8,15},{9,8},{10,9... | collective-permute-start | bytes 786440 | tf_op jit(solution)/shard_map/ppermute | solution.py:21
  104.7 3.4 %collective-permute-start.3 = (bf16[1024,128]{1,0:T(8,128)(2,1)S(1)}, bf16[1024,128]{1,0:T(8,128)(2,1)S(1)}, u32[]{:S(2)}, u32[]{:S(2)}) collective-permute-start(bf16[1024,128]{1,0:T(8,128)(2,1)S(1)} %collective-permute-done.2.refs_3_), channel_id=1, source_target_pairs={{0,1},{1,2},{2,3},{3,4},{4,5},{5,6},{6,7},{7,0},{8,9},{9,10},{10,1... | collective-permute-start | bytes 786440 | tf_op jit(solution)/shard_map/ppermute | solution.py:21
  108.1 0.9 collective-permute-done.11.refs_13_
  109.0 3.1 %collective-permute-start.7 = (bf16[96,1024]{1,0:T(8,128)(2,1)}, bf16[96,1024]{1,0:T(8,128)(2,1)S(1)}, u32[]{:S(2)}, u32[]{:S(2)}) collective-permute-start(bf16[96,1024]{1,0:T(8,128)(2,1)} %get-tuple-element.28), channel_id=1, source_target_pairs={{0,1},{1,2},{2,3},{3,4},{4,5},{5,6},{6,7},{7,0},{8,9},{9,10},{10,1... | collective-permute-start | bytes 589832 | tf_op jit(solution)/shard_map/ppermute | solution.py:21
  112.0 3.6 %collective-permute-done.12.refs_14_ = bf16[96,1024]{1,0:T(8,128)(2,1)S(1)} collective-permute-done((bf16[96,1024]{1,0:T(8,128)(2,1)}, bf16[96,1024]{1,0:T(8,128)(2,1)S(1)}, u32[]{:S(2)}, u32[]{:S(2)}) %collective-permute-start.12) | collective-permute-done | bytes 196640 | tf_op jit(solution)/shard_map/ppermute | solution.py:21
  115.7 1.9 collective-permute-start.8
  117.6 6.7 %collective-permute-done.13.refs_15_ = bf16[96,1024]{1,0:T(8,128)(2,1)S(1)} collective-permute-done((bf16[96,1024]{1,0:T(8,128)(2,1)}, bf16[96,1024]{1,0:T(8,128)(2,1)S(1)}, u32[]{:S(2)}, u32[]{:S(2)}) %collective-permute-start.13) | collective-permute-done | bytes 196640 | tf_op jit(solution)/shard_map/ppermute | solution.py:21
  124.3 1.9 collective-permute-start.9
  126.3 0.0 copy-start.12
  126.3 2.0 collective-permute-done.8.refs_10_
  128.3 15.0 %collective-permute-done.9.refs_11_ = bf16[96,1024]{1,0:T(8,128)(2,1)S(1)} collective-permute-done((bf16[96,1024]{1,0:T(8,128)(2,1)}, bf16[96,1024]{1,0:T(8,128)(2,1)S(1)}, u32[]{:S(2)}, u32[]{:S(2)}) %collective-permute-start.9) | collective-permute-done | bytes 196640 | tf_op jit(solution)/shard_map/ppermute | solution.py:21
  143.4 0.5 copy-done.14
  144.0 0.1 copy-done.6
  144.1 0.1 copy-done.7
  144.1 5.1 %shard_map.87 = bf16[64,24,128]{2,1,0:T(8,128)(2,1)} custom-call(bf16[1024,128]{1,0:T(8,128)(2,1)} %bitcast.31, bf16[1024,128]{1,0:T(8,128)(2,1)} %copy-done.1, bf16[1024,128]{1,0:T(8,128)(2,1)} %copy-done.3, bf16[1024,128]{1,0:T(8,128)(2,1)} %copy-done.5, bf16[1024,128]{1,0:T(8,128)(2,1)} %copy-done.7, bf16[1024,128]{1,0:T(8,128)(2,1)} %copy-done.2, ...), custom_call_target="tpu_custom_call" | custom-call | tf_op jit(solution)/shard_map/pallas_call | solution.py:149
  149.2 6.0 %all-to-all-start.2 = ((bf16[64,24,128]{2,1,0:T(8,128)(2,1)}), bf16[64,24,128]{2,1,0:T(8,128)(2,1)S(1)}, u32[]{:S(2)}, u32[]{:S(2)}) async-start(bf16[64,24,128]{2,1,0:T(8,128)(2,1)} %shard_map.87), calls=%async_computation.2 | async-start | bytes 786432 | tf_op jit(solution)/shard_map/all_to_all | solution.py:155
  155.2 4.0 %shard_map.85 = (f32[1,128,1024]{2,1,0:T(8,128)}, f32[1,128,1024]{2,1,0:T(8,128)}) custom-call(bf16[1024,128]{1,0:T(8,128)(2,1)} %bitcast.32, bf16[1024,128]{1,0:T(8,128)(2,1)} %copy-done.1, bf16[1024,128]{1,0:T(8,128)(2,1)} %copy-done.3, bf16[1024,128]{1,0:T(8,128)(2,1)} %copy-done.5, bf16[1024,128]{1,0:T(8,128)(2,1)} %copy-done.7, ...), custom_call_target="tpu_custom_call" | custom-call | tf_op jit(solution)/shard_map/pallas_call | solution.py:157
  159.3 10.4 %all-to-all-done.2 = bf16[64,24,128]{2,1,0:T(8,128)(2,1)S(1)} async-done(((bf16[64,24,128]{2,1,0:T(8,128)(2,1)}), bf16[64,24,128]{2,1,0:T(8,128)(2,1)S(1)}, u32[]{:S(2)}, u32[]{:S(2)}) %all-to-all-start.2) | async-done | bytes 393248 | tf_op jit(solution)/shard_map/all_to_all | solution.py:155
  169.6 0.6 gather_fusion.1
  170.2 0.1 broadcast_select_fusion
  170.4 26.6 %all-gather = bf16[3840,128]{1,0:T(8,128)(2,1)S(1)} all-gather(bf16[480,128]{1,0:T(8,128)(2,1)S(1)} %fusion.3), channel_id=2, replica_groups=mesh['fsdp_0'=4,'fsdp_1'=8,'fsdp_2'=2,'dp'=8] {'dp'}, dimensions={0}, use_global_device_ids=true | all-gather | bytes 1105920 | tf_op jit(solution)/shard_map/all_gather | solution.py:167
  197.0 0.1 slice.40
  197.1 0.1 convert_reduce_fusion
  197.2 0.3 fusion.1
  197.5 1.2 copy.12
  (45 shorter events, 0.2 us)
Async XLA Ops:
  3.2 10.5 %copy-start.15 = (s32[28]{0:T(128)S(1)}, s32[28]{0:T(128)}, u32[]{:S(2)}) copy-start(s32[28]{0:T(128)} %param.9) | copy-start | bytes 340
  3.2 36.4 %all-to-all-start = ((bf16[8,448,128]{2,1,0:T(8,128)(2,1)}), bf16[8,448,128]{2,1,0:T(8,128)(2,1)S(1)}, u32[]{:S(2)}, u32[]{:S(2)}) async-start(bf16[8,448,128]{2,1,0:T(8,128)(2,1)} %bitcast.1), calls=%async_computation | async-start | bytes 1835008 | tf_op jit(solution)/shard_map/all_to_all | solution.py:128
  62.6 80.7 %copy-start = (bf16[64,16,128]{2,1,0:T(8,128)(2,1)}, bf16[64,16,128]{2,1,0:T(8,128)(2,1)S(1)}, u32[]{:S(2)}) copy-start(bf16[64,16,128]{2,1,0:T(8,128)(2,1)S(1)} %all_to_all.15) | copy-start | bytes 786436
  62.6 11.5 %collective-permute-start = (bf16[1024,128]{1,0:T(8,128)(2,1)S(1)}, bf16[1024,128]{1,0:T(8,128)(2,1)S(1)}, u32[]{:S(2)}, u32[]{:S(2)}) collective-permute-start(bf16[1024,128]{1,0:T(8,128)(2,1)S(1)} %bitcast.29), channel_id=1, source_target_pairs={{0,1},{1,2},{2,3},{3,4},{4,5},{5,6},{6,7},{7,0},{8,9},{9,10},{10,1... | collective-permute-start | bytes 786440 | tf_op jit(solution)/shard_map/ppermute | solution.py:21
  65.1 15.8 %collective-permute-start.4 = (bf16[1024,128]{1,0:T(8,128)(2,1)S(1)}, bf16[1024,128]{1,0:T(8,128)(2,1)S(1)}, u32[]{:S(2)}, u32[]{:S(2)}) collective-permute-start(bf16[1024,128]{1,0:T(8,128)(2,1)S(1)} %bitcast.30), channel_id=1, source_target_pairs={{0,7},{1,0},{2,1},{3,2},{4,3},{5,4},{6,5},{7,6},{8,15},{9,8},{10,9... | collective-permute-start | bytes 786440 | tf_op jit(solution)/shard_map/ppermute | solution.py:21
  74.1 69.2 %copy-start.1 = (bf16[1024,128]{1,0:T(8,128)(2,1)}, bf16[1024,128]{1,0:T(8,128)(2,1)S(1)}, u32[]{:S(2)}) copy-start(bf16[1024,128]{1,0:T(8,128)(2,1)S(1)} %collective-permute-done.refs_1_) | copy-start | bytes 786436
  74.1 16.0 %collective-permute-start.1 = (bf16[1024,128]{1,0:T(8,128)(2,1)S(1)}, bf16[1024,128]{1,0:T(8,128)(2,1)S(1)}, u32[]{:S(2)}, u32[]{:S(2)}) collective-permute-start(bf16[1024,128]{1,0:T(8,128)(2,1)S(1)} %collective-permute-done.refs_1_), channel_id=1, source_target_pairs={{0,1},{1,2},{2,3},{3,4},{4,5},{5,6},{6,7},{7,0},{8,9},{9,10},{10,1... | collective-permute-start | bytes 786440 | tf_op jit(solution)/shard_map/ppermute | solution.py:21
  78.2 20.9 %collective-permute-start.10 = (bf16[96,1024]{1,0:T(8,128)(2,1)}, bf16[96,1024]{1,0:T(8,128)(2,1)S(1)}, u32[]{:S(2)}, u32[]{:S(2)}) collective-permute-start(bf16[96,1024]{1,0:T(8,128)(2,1)} %get-tuple-element.31), channel_id=1, source_target_pairs={{0,4},{1,5},{2,6},{3,7},{4,0},{5,1},{6,2},{7,3},{8,12},{9,13},{10,... | collective-permute-start | bytes 589832 | tf_op jit(solution)/shard_map/ppermute | solution.py:21
  81.0 62.4 %copy-start.2 = (bf16[1024,128]{1,0:T(8,128)(2,1)}, bf16[1024,128]{1,0:T(8,128)(2,1)S(1)}, u32[]{:S(2)}) copy-start(bf16[1024,128]{1,0:T(8,128)(2,1)S(1)} %collective-permute-done.4.refs_5_) | copy-start | bytes 786436
  81.0 21.2 %collective-permute-start.5 = (bf16[1024,128]{1,0:T(8,128)(2,1)S(1)}, bf16[1024,128]{1,0:T(8,128)(2,1)S(1)}, u32[]{:S(2)}, u32[]{:S(2)}) collective-permute-start(bf16[1024,128]{1,0:T(8,128)(2,1)S(1)} %collective-permute-done.4.refs_5_), channel_id=1, source_target_pairs={{0,7},{1,0},{2,1},{3,2},{4,3},{5,4},{6,5},{7,6},{8,15},{9,8},{10,9... | collective-permute-start | bytes 786440 | tf_op jit(solution)/shard_map/ppermute | solution.py:21
  90.1 53.2 %copy-start.3 = (bf16[1024,128]{1,0:T(8,128)(2,1)}, bf16[1024,128]{1,0:T(8,128)(2,1)S(1)}, u32[]{:S(2)}) copy-start(bf16[1024,128]{1,0:T(8,128)(2,1)S(1)} %collective-permute-done.1.refs_2_) | copy-start | bytes 786436
  90.1 14.6 %collective-permute-start.2 = (bf16[1024,128]{1,0:T(8,128)(2,1)S(1)}, bf16[1024,128]{1,0:T(8,128)(2,1)S(1)}, u32[]{:S(2)}, u32[]{:S(2)}) collective-permute-start(bf16[1024,128]{1,0:T(8,128)(2,1)S(1)} %collective-permute-done.1.refs_2_), channel_id=1, source_target_pairs={{0,1},{1,2},{2,3},{3,4},{4,5},{5,6},{6,7},{7,0},{8,9},{9,10},{10,1... | collective-permute-start | bytes 786440 | tf_op jit(solution)/shard_map/ppermute | solution.py:21
  92.0 16.9 %collective-permute-start.11 = (bf16[96,1024]{1,0:T(8,128)(2,1)}, bf16[96,1024]{1,0:T(8,128)(2,1)S(1)}, u32[]{:S(2)}, u32[]{:S(2)}) collective-permute-start(bf16[96,1024]{1,0:T(8,128)(2,1)} %get-tuple-element.32), channel_id=1, source_target_pairs={{0,7},{1,0},{2,1},{3,2},{4,3},{5,4},{6,5},{7,6},{8,15},{9,8},{10,9... | collective-permute-start | bytes 589832 | tf_op jit(solution)/shard_map/ppermute | solution.py:21
  97.2 18.5 %collective-permute-start.12 = (bf16[96,1024]{1,0:T(8,128)(2,1)}, bf16[96,1024]{1,0:T(8,128)(2,1)S(1)}, u32[]{:S(2)}, u32[]{:S(2)}) collective-permute-start(bf16[96,1024]{1,0:T(8,128)(2,1)} %get-tuple-element.33), channel_id=1, source_target_pairs={{0,6},{1,7},{2,0},{3,1},{4,2},{5,3},{6,4},{7,5},{8,14},{9,15},{10,... | collective-permute-start | bytes 589832 | tf_op jit(solution)/shard_map/ppermute | solution.py:21
  99.1 44.2 %copy-start.8 = (bf16[96,1024]{1,0:T(8,128)(2,1)}, bf16[96,1024]{1,0:T(8,128)(2,1)S(1)}, u32[]{:S(2)}) copy-start(bf16[96,1024]{1,0:T(8,128)(2,1)S(1)} %collective-permute-done.10.refs_12_) | copy-start | bytes 589828
  99.1 25.2 %collective-permute-start.13 = (bf16[96,1024]{1,0:T(8,128)(2,1)}, bf16[96,1024]{1,0:T(8,128)(2,1)S(1)}, u32[]{:S(2)}, u32[]{:S(2)}) collective-permute-start(bf16[96,1024]{1,0:T(8,128)(2,1)} %get-tuple-element.34), channel_id=1, source_target_pairs={{0,5},{1,6},{2,7},{3,0},{4,1},{5,2},{6,3},{7,4},{8,13},{9,14},{10,... | collective-permute-start | bytes 589832 | tf_op jit(solution)/shard_map/ppermute | solution.py:21
  102.2 41.2 %copy-start.4 = (bf16[1024,128]{1,0:T(8,128)(2,1)}, bf16[1024,128]{1,0:T(8,128)(2,1)S(1)}, u32[]{:S(2)}) copy-start(bf16[1024,128]{1,0:T(8,128)(2,1)S(1)} %collective-permute-done.5.refs_6_) | copy-start | bytes 786436
  102.2 41.1 %collective-permute-start.6 = (bf16[1024,128]{1,0:T(8,128)(2,1)S(1)}, bf16[1024,128]{1,0:T(8,128)(2,1)S(1)}, u32[]{:S(2)}, u32[]{:S(2)}) collective-permute-start(bf16[1024,128]{1,0:T(8,128)(2,1)S(1)} %collective-permute-done.5.refs_6_), channel_id=1, source_target_pairs={{0,7},{1,0},{2,1},{3,2},{4,3},{5,4},{6,5},{7,6},{8,15},{9,8},{10,9... | collective-permute-start | bytes 786440 | tf_op jit(solution)/shard_map/ppermute | solution.py:21
  104.7 38.7 %copy-start.5 = (bf16[1024,128]{1,0:T(8,128)(2,1)}, bf16[1024,128]{1,0:T(8,128)(2,1)S(1)}, u32[]{:S(2)}) copy-start(bf16[1024,128]{1,0:T(8,128)(2,1)S(1)} %collective-permute-done.2.refs_3_) | copy-start | bytes 786436
  104.7 38.6 %collective-permute-start.3 = (bf16[1024,128]{1,0:T(8,128)(2,1)S(1)}, bf16[1024,128]{1,0:T(8,128)(2,1)S(1)}, u32[]{:S(2)}, u32[]{:S(2)}) collective-permute-start(bf16[1024,128]{1,0:T(8,128)(2,1)S(1)} %collective-permute-done.2.refs_3_), channel_id=1, source_target_pairs={{0,1},{1,2},{2,3},{3,4},{4,5},{5,6},{6,7},{7,0},{8,9},{9,10},{10,1... | collective-permute-start | bytes 786440 | tf_op jit(solution)/shard_map/ppermute | solution.py:21
  109.0 34.4 %copy-start.9 = (bf16[96,1024]{1,0:T(8,128)(2,1)}, bf16[96,1024]{1,0:T(8,128)(2,1)S(1)}, u32[]{:S(2)}) copy-start(bf16[96,1024]{1,0:T(8,128)(2,1)S(1)} %collective-permute-done.11.refs_13_) | copy-start | bytes 589828
  109.0 17.3 %collective-permute-start.7 = (bf16[96,1024]{1,0:T(8,128)(2,1)}, bf16[96,1024]{1,0:T(8,128)(2,1)S(1)}, u32[]{:S(2)}, u32[]{:S(2)}) collective-permute-start(bf16[96,1024]{1,0:T(8,128)(2,1)} %get-tuple-element.28), channel_id=1, source_target_pairs={{0,1},{1,2},{2,3},{3,4},{4,5},{5,6},{6,7},{7,0},{8,9},{9,10},{10,1... | collective-permute-start | bytes 589832 | tf_op jit(solution)/shard_map/ppermute | solution.py:21
  115.7 27.7 %copy-start.10 = (bf16[96,1024]{1,0:T(8,128)(2,1)}, bf16[96,1024]{1,0:T(8,128)(2,1)S(1)}, u32[]{:S(2)}) copy-start(bf16[96,1024]{1,0:T(8,128)(2,1)S(1)} %collective-permute-done.12.refs_14_) | copy-start | bytes 589828
  115.7 12.6 %collective-permute-start.8 = (bf16[96,1024]{1,0:T(8,128)(2,1)}, bf16[96,1024]{1,0:T(8,128)(2,1)S(1)}, u32[]{:S(2)}, u32[]{:S(2)}) collective-permute-start(bf16[96,1024]{1,0:T(8,128)(2,1)} %get-tuple-element.29), channel_id=1, source_target_pairs={{0,2},{1,3},{2,4},{3,5},{4,6},{5,7},{6,0},{7,1},{8,10},{9,11},{10,... | collective-permute-start | bytes 589832 | tf_op jit(solution)/shard_map/ppermute | solution.py:21
  124.3 19.1 %copy-start.11 = (bf16[96,1024]{1,0:T(8,128)(2,1)}, bf16[96,1024]{1,0:T(8,128)(2,1)S(1)}, u32[]{:S(2)}) copy-start(bf16[96,1024]{1,0:T(8,128)(2,1)S(1)} %collective-permute-done.13.refs_15_) | copy-start | bytes 589828
  124.3 18.9 %collective-permute-start.9 = (bf16[96,1024]{1,0:T(8,128)(2,1)}, bf16[96,1024]{1,0:T(8,128)(2,1)S(1)}, u32[]{:S(2)}, u32[]{:S(2)}) collective-permute-start(bf16[96,1024]{1,0:T(8,128)(2,1)} %get-tuple-element.30), channel_id=1, source_target_pairs={{0,3},{1,4},{2,5},{3,6},{4,7},{5,0},{6,1},{7,2},{8,11},{9,12},{10,... | collective-permute-start | bytes 589832 | tf_op jit(solution)/shard_map/ppermute | solution.py:21
  126.3 17.1 %copy-start.12 = (bf16[96,1024]{1,0:T(8,128)(2,1)}, bf16[96,1024]{1,0:T(8,128)(2,1)S(1)}, u32[]{:S(2)}) copy-start(bf16[96,1024]{1,0:T(8,128)(2,1)S(1)} %collective-permute-done.7.refs_9_) | copy-start | bytes 589828
  128.3 15.1 %copy-start.13 = (bf16[96,1024]{1,0:T(8,128)(2,1)}, bf16[96,1024]{1,0:T(8,128)(2,1)S(1)}, u32[]{:S(2)}) copy-start(bf16[96,1024]{1,0:T(8,128)(2,1)S(1)} %collective-permute-done.8.refs_10_) | copy-start | bytes 589828
  143.3 0.7 copy-start.14
  143.3 0.8 copy-start.6
  143.3 0.8 copy-start.7
  149.2 20.4 %all-to-all-start.2 = ((bf16[64,24,128]{2,1,0:T(8,128)(2,1)}), bf16[64,24,128]{2,1,0:T(8,128)(2,1)S(1)}, u32[]{:S(2)}, u32[]{:S(2)}) async-start(bf16[64,24,128]{2,1,0:T(8,128)(2,1)} %shard_map.87), calls=%async_computation.2 | async-start | bytes 786432 | tf_op jit(solution)/shard_map/all_to_all | solution.py:155

commit v4 on v3

--- a/solution.py
+++ b/solution.py
@@ -39,6 +39,14 @@
 
 def dot(a, b, dims=((1,), (0,))):
     return lax.dot_general(a, b, (dims, ((), ())), preferred_element_type=jnp.float32)
+
+
+def shares_kernel(rows, out):
+    height, width = rows.shape[0], out.shape[2]
+    for d in range(out.shape[0]):
+        for b in range(out.shape[1] // height):
+            start = (b * out.shape[0] + d) * width
+            out[d, b * height : (b + 1) * height, :] = rows[:, start : start + width]
 
 
 def roots_kernel(count, left, right, *outs):
@@ -58,10 +66,19 @@
 
 
 def precondition_kernel(count, *refs):
-    shards, roots, (out,) = refs[:count], refs[count : 2 * count], refs[2 * count :]
+    sources, (out, shard_buffer, root_buffer, arrived) = refs[: 2 * count], refs[2 * count :]
+    shards = [shard_buffer.at[i] for i in range(count)]
+    roots = [root_buffer.at[i] for i in range(count)]
+    copies = [
+        pltpu.make_async_copy(source, target, arrived.at[i])
+        for i, (source, target) in enumerate(zip(sources, shards + roots))
+    ]
+    for i in range(0, count, 2):
+        for k in (i, i + 1, count + i, count + i + 1):
+            copies[k].start()
     me = lax.axis_index("dp")
     width = shards[0].shape[1]
-    half = 64
+    half = roots[0].shape[0] * 2 // 3
     quarter = roots[0].shape[1] // 4
 
     def right(i):
@@ -69,6 +86,8 @@
 
     inner = None
     for i in range(0, count, 2):
+        for k in (i, i + 1, count + i, count + i + 1):
+            copies[k].wait()
         pair = jnp.concatenate([shards[i][...], shards[i + 1][...]], axis=1)
         term = dot(pair, jnp.concatenate(right(i) + right(i + 1), axis=0))
         inner = term if inner is None else inner + term
@@ -123,8 +142,14 @@
     numbers = jnp.arange(block_count, dtype=jnp.int32)
     source = jnp.sum(jnp.where(matches, numbers[None, :], 0), axis=1)
 
-    shares = rows.reshape(row_dev, block_count, replicas, shared).transpose(2, 1, 0, 3)
-    shares = shares.reshape(replicas, block_count * row_dev, shared)
+    groups = 4 if block_count % 4 == 0 else 1
+    shares = pl.pallas_call(
+        shares_kernel,
+        grid=(groups,),
+        out_shape=jax.ShapeDtypeStruct((replicas, block_count * row_dev, shared), jnp.bfloat16),
+        in_specs=[pl.BlockSpec((row_dev, col_count // groups), lambda i: (0, i))],
+        out_specs=pl.BlockSpec((replicas, block_count * row_dev // groups, shared), lambda i: (0, i, 0)),
+    )(rows)
     received = lax.all_to_all(shares, "dp", 0, 0, tiled=True)
 
     pieces = pl.pallas_call(
@@ -149,8 +174,13 @@
     message = pl.pallas_call(
         functools.partial(precondition_kernel, replicas),
         out_shape=jax.ShapeDtypeStruct((total_slots, row_dev + 8, shared), jnp.bfloat16),
-        in_specs=[VMEM] * (2 * replicas),
+        in_specs=[pl.BlockSpec(memory_space=pl.ANY)] * (2 * replicas),
         out_specs=VMEM,
+        scratch_shapes=[
+            pltpu.VMEM((replicas,) + shards[0].shape, jnp.bfloat16),
+            pltpu.VMEM((replicas,) + roots[0].shape, jnp.bfloat16),
+            pltpu.SemaphoreType.DMA((2 * replicas,)),
+        ],
     )(*shards, *roots)
     back = lax.all_to_all(message, FSDP, 0, 0, tiled=True)
 

time: 199 us -> 200 us (level)
  Pallas kernels: 11.3 us -> 14.3 us
  local copies, waits for them, and re-layouts: 5.86 us -> 3.28 us
    pallas_call x0 -> x1, Pallas kernels: none -> 3.37 us  [step(): pl.pallas_call(shares_kernel, grid=(groups,), out_shape=jax.ShapeDtypeStr...]
where the time goes in v4:
time: 200 us; the launch traced here: 199 us
  waiting for transfers between devices  73 us (36%)
  starting transfers between devices  57.8 us (29%)
  blocking collectives  48.7 us (24%)
  Pallas kernels  14.3 us (7%)
  local copies, waits for them, and re-layouts  3.28 us (2%)
    ppermute x14, starting transfers between devices, ring(): lax.ppermute(array, axis, [(i, (i + step) % count) for i in range(count)])  41.3 us
    ppermute x14, waiting for transfers between devices, ring(): lax.ppermute(array, axis, [(i, (i + step) % count) for i in range(count)])  36.9 us
    all_gather x1, blocking collectives, step(): lax.all_gather(jnp.concatenate([tiles, terms]), 'dp', axis=0, tiled=False)  26.6 us
    all_to_all x1, waiting for transfers between devices, step(): received = lax.all_to_all(shares, 'dp', 0, 0, tiled=True)  25.7 us
    all_to_all x1, blocking collectives, step(): incoming = lax.all_to_all(outgoing, FSDP, 0, 0, tiled=True)  22.1 us
    all_to_all x1, starting transfers between devices, step(): received = lax.all_to_all(shares, 'dp', 0, 0, tiled=True)  10.4 us
    all_to_all x1, waiting for transfers between devices, step(): back = lax.all_to_all(message, FSDP, 0, 0, tiled=True)  10.4 us
    all_to_all x1, starting transfers between devices, step(): back = lax.all_to_all(message, FSDP, 0, 0, tiled=True)  6.01 us
  transfers between devices with their start and end apart: 16, of which 9 were waited for; matrix products, arithmetic and copies ran while one was open for 0% of the time, Pallas kernels for 3%

profile of v4, /device:TPU:8, one launch (start us, length us, event | category | flops | bytes accessed | tf_op | source)
XLA Modules:
  0.0 199.2 jit_solution(10942388469171259412)
XLA Ops:
  0.6 3.4 %shard_map.85 = bf16[8,448,128]{2,1,0:T(8,128)(2,1)} custom-call(bf16[16,28672]{1,0:T(8,128)(2,1)} %bitcast.27), custom_call_target="tpu_custom_call" | custom-call | tf_op jit(solution)/shard_map/pallas_call | solution.py:146
  4.0 10.4 %all-to-all-start = ((bf16[8,448,128]{2,1,0:T(8,128)(2,1)}), bf16[8,448,128]{2,1,0:T(8,128)(2,1)S(1)}, u32[]{:S(2)}, u32[]{:S(2)}) async-start(bf16[8,448,128]{2,1,0:T(8,128)(2,1)} %shard_map.85), calls=%async_computation | async-start | bytes 1835008 | tf_op jit(solution)/shard_map/all_to_all | solution.py:153
  14.5 0.1 select_reduce_fusion
  14.6 0.1 fusion.4
  14.7 25.7 %all-to-all-done = bf16[8,448,128]{2,1,0:T(8,128)(2,1)S(1)} async-done(((bf16[8,448,128]{2,1,0:T(8,128)(2,1)}), bf16[8,448,128]{2,1,0:T(8,128)(2,1)S(1)}, u32[]{:S(2)}, u32[]{:S(2)}) %all-to-all-start) | async-done | bytes 917536 | tf_op jit(solution)/shard_map/all_to_all | solution.py:153
  40.4 0.1 reduce_sum.33
  40.5 0.6 gather_fusion
  41.1 0.2 select_select_fusion
  41.3 22.1 %all_to_all.15 = bf16[64,16,128]{2,1,0:T(8,128)(2,1)S(1)} all-to-all(bf16[64,16,128]{2,1,0:T(8,128)(2,1)S(1)} %select_select_fusion), channel_id=1, replica_groups=mesh['fsdp_0'=4,'fsdp_1'=8,'fsdp_2'=2,'dp'=8] {'fsdp_0','fsdp_1','fsdp_2'}, dimensions={0} | all-to-all | bytes 524288 | tf_op jit(solution)/shard_map/all_to_all | solution.py:171
  63.4 2.5 %collective-permute-start = (bf16[1024,128]{1,0:T(8,128)(2,1)S(1)}, bf16[1024,128]{1,0:T(8,128)(2,1)S(1)}, u32[]{:S(2)}, u32[]{:S(2)}) collective-permute-start(bf16[1024,128]{1,0:T(8,128)(2,1)S(1)} %bitcast.22), channel_id=1, source_target_pairs={{0,1},{1,2},{2,3},{3,4},{4,5},{5,6},{6,7},{7,0},{8,9},{9,10},{10,1... | collective-permute-start | bytes 786440 | tf_op jit(solution)/shard_map/ppermute | solution.py:21
  65.9 4.6 %collective-permute-start.4 = (bf16[1024,128]{1,0:T(8,128)(2,1)S(1)}, bf16[1024,128]{1,0:T(8,128)(2,1)S(1)}, u32[]{:S(2)}, u32[]{:S(2)}) collective-permute-start(bf16[1024,128]{1,0:T(8,128)(2,1)S(1)} %bitcast.23), channel_id=1, source_target_pairs={{0,7},{1,0},{2,1},{3,2},{4,3},{5,4},{6,5},{7,6},{8,15},{9,8},{10,9... | collective-permute-start | bytes 786440 | tf_op jit(solution)/shard_map/ppermute | solution.py:21
  70.5 4.4 %collective-permute-done.refs_1_ = bf16[1024,128]{1,0:T(8,128)(2,1)S(1)} collective-permute-done((bf16[1024,128]{1,0:T(8,128)(2,1)S(1)}, bf16[1024,128]{1,0:T(8,128)(2,1)S(1)}, u32[]{:S(2)}, u32[]{:S(2)}) %collective-permute-start) | collective-permute-done | bytes 262176 | tf_op jit(solution)/shard_map/ppermute | solution.py:21
  74.9 1.9 collective-permute-start.1
  76.8 2.2 %shard_map.87 = (bf16[96,1024]{1,0:T(8,128)(2,1)}, bf16[96,1024]{1,0:T(8,128)(2,1)}, bf16[96,1024]{1,0:T(8,128)(2,1)}, bf16[96,1024]{1,0:T(8,128)(2,1)}, bf16[96...) custom-call(bf16[128,1024]{1,0:T(8,128)(2,1)} %bitcast.30, ...), custom_call_target="tpu_custom_call" | custom-call | tf_op jit(solution)/shard_map/pallas_call | solution.py:155
  79.0 2.7 %collective-permute-start.10 = (bf16[96,1024]{1,0:T(8,128)(2,1)}, bf16[96,1024]{1,0:T(8,128)(2,1)S(1)}, u32[]{:S(2)}, u32[]{:S(2)}) collective-permute-start(bf16[96,1024]{1,0:T(8,128)(2,1)} %get-tuple-element.31), channel_id=1, source_target_pairs={{0,4},{1,5},{2,6},{3,7},{4,0},{5,1},{6,2},{7,3},{8,12},{9,13},{10,... | collective-permute-start | bytes 589832 | tf_op jit(solution)/shard_map/ppermute | solution.py:21
  81.7 0.0 collective-permute-done.4.refs_5_
  81.8 4.9 %collective-permute-start.5 = (bf16[1024,128]{1,0:T(8,128)(2,1)S(1)}, bf16[1024,128]{1,0:T(8,128)(2,1)S(1)}, u32[]{:S(2)}, u32[]{:S(2)}) collective-permute-start(bf16[1024,128]{1,0:T(8,128)(2,1)S(1)} %collective-permute-done.4.refs_5_), channel_id=1, source_target_pairs={{0,7},{1,0},{2,1},{3,2},{4,3},{5,4},{6,5},{7,6},{8,15},{9,8},{10,9... | collective-permute-start | bytes 786440 | tf_op jit(solution)/shard_map/ppermute | solution.py:21
  86.7 4.2 %collective-permute-done.1.refs_2_ = bf16[1024,128]{1,0:T(8,128)(2,1)S(1)} collective-permute-done((bf16[1024,128]{1,0:T(8,128)(2,1)S(1)}, bf16[1024,128]{1,0:T(8,128)(2,1)S(1)}, u32[]{:S(2)}, u32[]{:S(2)}) %collective-permute-start.1) | collective-permute-done | bytes 262176 | tf_op jit(solution)/shard_map/ppermute | solution.py:21
  90.9 1.9 collective-permute-start.2
  92.8 5.1 %collective-permute-start.11 = (bf16[96,1024]{1,0:T(8,128)(2,1)}, bf16[96,1024]{1,0:T(8,128)(2,1)S(1)}, u32[]{:S(2)}, u32[]{:S(2)}) collective-permute-start(bf16[96,1024]{1,0:T(8,128)(2,1)} %get-tuple-element.32), channel_id=1, source_target_pairs={{0,7},{1,0},{2,1},{3,2},{4,3},{5,4},{6,5},{7,6},{8,15},{9,8},{10,9... | collective-permute-start | bytes 589832 | tf_op jit(solution)/shard_map/ppermute | solution.py:21
  98.0 1.9 collective-permute-start.12
  99.9 0.0 collective-permute-done.10.refs_12_
  99.9 3.1 %collective-permute-start.13 = (bf16[96,1024]{1,0:T(8,128)(2,1)}, bf16[96,1024]{1,0:T(8,128)(2,1)S(1)}, u32[]{:S(2)}, u32[]{:S(2)}) collective-permute-start(bf16[96,1024]{1,0:T(8,128)(2,1)} %get-tuple-element.34), channel_id=1, source_target_pairs={{0,5},{1,6},{2,7},{3,0},{4,1},{5,2},{6,3},{7,4},{8,13},{9,14},{10,... | collective-permute-start | bytes 589832 | tf_op jit(solution)/shard_map/ppermute | solution.py:21
  103.0 2.5 %collective-permute-start.6 = (bf16[1024,128]{1,0:T(8,128)(2,1)S(1)}, bf16[1024,128]{1,0:T(8,128)(2,1)S(1)}, u32[]{:S(2)}, u32[]{:S(2)}) collective-permute-start(bf16[1024,128]{1,0:T(8,128)(2,1)S(1)} %collective-permute-done.5.refs_6_), channel_id=1, source_target_pairs={{0,7},{1,0},{2,1},{3,2},{4,3},{5,4},{6,5},{7,6},{8,15},{9,8},{10,9... | collective-permute-start | bytes 786440 | tf_op jit(solution)/shard_map/ppermute | solution.py:21
  105.5 3.4 %collective-permute-start.3 = (bf16[1024,128]{1,0:T(8,128)(2,1)S(1)}, bf16[1024,128]{1,0:T(8,128)(2,1)S(1)}, u32[]{:S(2)}, u32[]{:S(2)}) collective-permute-start(bf16[1024,128]{1,0:T(8,128)(2,1)S(1)} %collective-permute-done.2.refs_3_), channel_id=1, source_target_pairs={{0,1},{1,2},{2,3},{3,4},{4,5},{5,6},{6,7},{7,0},{8,9},{9,10},{10,1... | collective-permute-start | bytes 786440 | tf_op jit(solution)/shard_map/ppermute | solution.py:21
  108.9 0.9 collective-permute-done.11.refs_13_
  109.7 3.1 %collective-permute-start.7 = (bf16[96,1024]{1,0:T(8,128)(2,1)}, bf16[96,1024]{1,0:T(8,128)(2,1)S(1)}, u32[]{:S(2)}, u32[]{:S(2)}) collective-permute-start(bf16[96,1024]{1,0:T(8,128)(2,1)} %get-tuple-element.28), channel_id=1, source_target_pairs={{0,1},{1,2},{2,3},{3,4},{4,5},{5,6},{6,7},{7,0},{8,9},{9,10},{10,1... | collective-permute-start | bytes 589832 | tf_op jit(solution)/shard_map/ppermute | solution.py:21
  112.8 3.6 %collective-permute-done.12.refs_14_ = bf16[96,1024]{1,0:T(8,128)(2,1)S(1)} collective-permute-done((bf16[96,1024]{1,0:T(8,128)(2,1)}, bf16[96,1024]{1,0:T(8,128)(2,1)S(1)}, u32[]{:S(2)}, u32[]{:S(2)}) %collective-permute-start.12) | collective-permute-done | bytes 196640 | tf_op jit(solution)/shard_map/ppermute | solution.py:21
  116.5 1.9 collective-permute-start.8
  118.4 6.7 %collective-permute-done.13.refs_15_ = bf16[96,1024]{1,0:T(8,128)(2,1)S(1)} collective-permute-done((bf16[96,1024]{1,0:T(8,128)(2,1)}, bf16[96,1024]{1,0:T(8,128)(2,1)S(1)}, u32[]{:S(2)}, u32[]{:S(2)}) %collective-permute-start.13) | collective-permute-done | bytes 196640 | tf_op jit(solution)/shard_map/ppermute | solution.py:21
  125.1 1.9 collective-permute-start.9
  127.1 0.0 copy-start.12
  127.1 2.0 collective-permute-done.8.refs_10_
  129.1 15.0 %collective-permute-done.9.refs_11_ = bf16[96,1024]{1,0:T(8,128)(2,1)S(1)} collective-permute-done((bf16[96,1024]{1,0:T(8,128)(2,1)}, bf16[96,1024]{1,0:T(8,128)(2,1)S(1)}, u32[]{:S(2)}, u32[]{:S(2)}) %collective-permute-start.9) | collective-permute-done | bytes 196640 | tf_op jit(solution)/shard_map/ppermute | solution.py:21
  144.2 0.5 copy-done.14
  144.7 0.1 copy-done.6
  144.8 0.1 copy-done.7
  144.9 4.7 %shard_map.88 = bf16[64,24,128]{2,1,0:T(8,128)(2,1)} custom-call(bf16[1024,128]{1,0:T(8,128)(2,1)} %bitcast.24, bf16[1024,128]{1,0:T(8,128)(2,1)} %copy-done.1, bf16[1024,128]{1,0:T(8,128)(2,1)} %copy-done.3, bf16[1024,128]{1,0:T(8,128)(2,1)} %copy-done.5, bf16[1024,128]{1,0:T(8,128)(2,1)} %copy-done.7, bf16[1024,128]{1,0:T(8,128)(2,1)} %copy-done.2, ...), custom_call_target="tpu_custom_call" | custom-call | tf_op jit(solution)/shard_map/pallas_call | solution.py:174
  149.7 6.0 %all-to-all-start.2 = ((bf16[64,24,128]{2,1,0:T(8,128)(2,1)}), bf16[64,24,128]{2,1,0:T(8,128)(2,1)S(1)}, u32[]{:S(2)}, u32[]{:S(2)}) async-start(bf16[64,24,128]{2,1,0:T(8,128)(2,1)} %shard_map.88), calls=%async_computation.2 | async-start | bytes 786432 | tf_op jit(solution)/shard_map/all_to_all | solution.py:185
  155.7 4.0 %shard_map.86 = (f32[1,128,1024]{2,1,0:T(8,128)}, f32[1,128,1024]{2,1,0:T(8,128)}) custom-call(bf16[1024,128]{1,0:T(8,128)(2,1)} %bitcast.25, bf16[1024,128]{1,0:T(8,128)(2,1)} %copy-done.1, bf16[1024,128]{1,0:T(8,128)(2,1)} %copy-done.3, bf16[1024,128]{1,0:T(8,128)(2,1)} %copy-done.5, bf16[1024,128]{1,0:T(8,128)(2,1)} %copy-done.7, ...), custom_call_target="tpu_custom_call" | custom-call | tf_op jit(solution)/shard_map/pallas_call | solution.py:187
  159.7 10.4 %all-to-all-done.2 = bf16[64,24,128]{2,1,0:T(8,128)(2,1)S(1)} async-done(((bf16[64,24,128]{2,1,0:T(8,128)(2,1)}), bf16[64,24,128]{2,1,0:T(8,128)(2,1)S(1)}, u32[]{:S(2)}, u32[]{:S(2)}) %all-to-all-start.2) | async-done | bytes 393248 | tf_op jit(solution)/shard_map/all_to_all | solution.py:185
  170.1 0.6 gather_fusion.1
  170.7 0.1 broadcast_select_fusion
  170.9 26.6 %all-gather = bf16[3840,128]{1,0:T(8,128)(2,1)S(1)} all-gather(bf16[480,128]{1,0:T(8,128)(2,1)S(1)} %fusion.3), channel_id=2, replica_groups=mesh['fsdp_0'=4,'fsdp_1'=8,'fsdp_2'=2,'dp'=8] {'dp'}, dimensions={0}, use_global_device_ids=true | all-gather | bytes 1105920 | tf_op jit(solution)/shard_map/all_gather | solution.py:197
  197.5 0.1 slice.40
  197.6 0.1 convert_reduce_fusion
  197.7 0.3 fusion.1
  198.0 1.2 copy.10
  (44 shorter events, 0.2 us)
Async XLA Ops:
  4.0 10.5 %copy-start.15 = (s32[28]{0:T(128)S(1)}, s32[28]{0:T(128)}, u32[]{:S(2)}) copy-start(s32[28]{0:T(128)} %param.9) | copy-start | bytes 340
  4.0 36.4 %all-to-all-start = ((bf16[8,448,128]{2,1,0:T(8,128)(2,1)}), bf16[8,448,128]{2,1,0:T(8,128)(2,1)S(1)}, u32[]{:S(2)}, u32[]{:S(2)}) async-start(bf16[8,448,128]{2,1,0:T(8,128)(2,1)} %shard_map.85), calls=%async_computation | async-start | bytes 1835008 | tf_op jit(solution)/shard_map/all_to_all | solution.py:153
  63.4 80.7 %copy-start = (bf16[64,16,128]{2,1,0:T(8,128)(2,1)}, bf16[64,16,128]{2,1,0:T(8,128)(2,1)S(1)}, u32[]{:S(2)}) copy-start(bf16[64,16,128]{2,1,0:T(8,128)(2,1)S(1)} %all_to_all.15) | copy-start | bytes 786436
  63.4 11.5 %collective-permute-start = (bf16[1024,128]{1,0:T(8,128)(2,1)S(1)}, bf16[1024,128]{1,0:T(8,128)(2,1)S(1)}, u32[]{:S(2)}, u32[]{:S(2)}) collective-permute-start(bf16[1024,128]{1,0:T(8,128)(2,1)S(1)} %bitcast.22), channel_id=1, source_target_pairs={{0,1},{1,2},{2,3},{3,4},{4,5},{5,6},{6,7},{7,0},{8,9},{9,10},{10,1... | collective-permute-start | bytes 786440 | tf_op jit(solution)/shard_map/ppermute | solution.py:21
  65.9 15.8 %collective-permute-start.4 = (bf16[1024,128]{1,0:T(8,128)(2,1)S(1)}, bf16[1024,128]{1,0:T(8,128)(2,1)S(1)}, u32[]{:S(2)}, u32[]{:S(2)}) collective-permute-start(bf16[1024,128]{1,0:T(8,128)(2,1)S(1)} %bitcast.23), channel_id=1, source_target_pairs={{0,7},{1,0},{2,1},{3,2},{4,3},{5,4},{6,5},{7,6},{8,15},{9,8},{10,9... | collective-permute-start | bytes 786440 | tf_op jit(solution)/shard_map/ppermute | solution.py:21
  74.9 69.2 %copy-start.1 = (bf16[1024,128]{1,0:T(8,128)(2,1)}, bf16[1024,128]{1,0:T(8,128)(2,1)S(1)}, u32[]{:S(2)}) copy-start(bf16[1024,128]{1,0:T(8,128)(2,1)S(1)} %collective-permute-done.refs_1_) | copy-start | bytes 786436
  74.9 16.0 %collective-permute-start.1 = (bf16[1024,128]{1,0:T(8,128)(2,1)S(1)}, bf16[1024,128]{1,0:T(8,128)(2,1)S(1)}, u32[]{:S(2)}, u32[]{:S(2)}) collective-permute-start(bf16[1024,128]{1,0:T(8,128)(2,1)S(1)} %collective-permute-done.refs_1_), channel_id=1, source_target_pairs={{0,1},{1,2},{2,3},{3,4},{4,5},{5,6},{6,7},{7,0},{8,9},{9,10},{10,1... | collective-permute-start | bytes 786440 | tf_op jit(solution)/shard_map/ppermute | solution.py:21
  79.0 20.9 %collective-permute-start.10 = (bf16[96,1024]{1,0:T(8,128)(2,1)}, bf16[96,1024]{1,0:T(8,128)(2,1)S(1)}, u32[]{:S(2)}, u32[]{:S(2)}) collective-permute-start(bf16[96,1024]{1,0:T(8,128)(2,1)} %get-tuple-element.31), channel_id=1, source_target_pairs={{0,4},{1,5},{2,6},{3,7},{4,0},{5,1},{6,2},{7,3},{8,12},{9,13},{10,... | collective-permute-start | bytes 589832 | tf_op jit(solution)/shard_map/ppermute | solution.py:21
  81.7 62.4 %copy-start.2 = (bf16[1024,128]{1,0:T(8,128)(2,1)}, bf16[1024,128]{1,0:T(8,128)(2,1)S(1)}, u32[]{:S(2)}) copy-start(bf16[1024,128]{1,0:T(8,128)(2,1)S(1)} %collective-permute-done.4.refs_5_) | copy-start | bytes 786436
  81.8 21.2 %collective-permute-start.5 = (bf16[1024,128]{1,0:T(8,128)(2,1)S(1)}, bf16[1024,128]{1,0:T(8,128)(2,1)S(1)}, u32[]{:S(2)}, u32[]{:S(2)}) collective-permute-start(bf16[1024,128]{1,0:T(8,128)(2,1)S(1)} %collective-permute-done.4.refs_5_), channel_id=1, source_target_pairs={{0,7},{1,0},{2,1},{3,2},{4,3},{5,4},{6,5},{7,6},{8,15},{9,8},{10,9... | collective-permute-start | bytes 786440 | tf_op jit(solution)/shard_map/ppermute | solution.py:21
  90.9 53.2 %copy-start.3 = (bf16[1024,128]{1,0:T(8,128)(2,1)}, bf16[1024,128]{1,0:T(8,128)(2,1)S(1)}, u32[]{:S(2)}) copy-start(bf16[1024,128]{1,0:T(8,128)(2,1)S(1)} %collective-permute-done.1.refs_2_) | copy-start | bytes 786436
  90.9 14.6 %collective-permute-start.2 = (bf16[1024,128]{1,0:T(8,128)(2,1)S(1)}, bf16[1024,128]{1,0:T(8,128)(2,1)S(1)}, u32[]{:S(2)}, u32[]{:S(2)}) collective-permute-start(bf16[1024,128]{1,0:T(8,128)(2,1)S(1)} %collective-permute-done.1.refs_2_), channel_id=1, source_target_pairs={{0,1},{1,2},{2,3},{3,4},{4,5},{5,6},{6,7},{7,0},{8,9},{9,10},{10,1... | collective-permute-start | bytes 786440 | tf_op jit(solution)/shard_map/ppermute | solution.py:21
  92.8 16.9 %collective-permute-start.11 = (bf16[96,1024]{1,0:T(8,128)(2,1)}, bf16[96,1024]{1,0:T(8,128)(2,1)S(1)}, u32[]{:S(2)}, u32[]{:S(2)}) collective-permute-start(bf16[96,1024]{1,0:T(8,128)(2,1)} %get-tuple-element.32), channel_id=1, source_target_pairs={{0,7},{1,0},{2,1},{3,2},{4,3},{5,4},{6,5},{7,6},{8,15},{9,8},{10,9... | collective-permute-start | bytes 589832 | tf_op jit(solution)/shard_map/ppermute | solution.py:21
  98.0 18.5 %collective-permute-start.12 = (bf16[96,1024]{1,0:T(8,128)(2,1)}, bf16[96,1024]{1,0:T(8,128)(2,1)S(1)}, u32[]{:S(2)}, u32[]{:S(2)}) collective-permute-start(bf16[96,1024]{1,0:T(8,128)(2,1)} %get-tuple-element.33), channel_id=1, source_target_pairs={{0,6},{1,7},{2,0},{3,1},{4,2},{5,3},{6,4},{7,5},{8,14},{9,15},{10,... | collective-permute-start | bytes 589832 | tf_op jit(solution)/shard_map/ppermute | solution.py:21
  99.9 44.2 %copy-start.8 = (bf16[96,1024]{1,0:T(8,128)(2,1)}, bf16[96,1024]{1,0:T(8,128)(2,1)S(1)}, u32[]{:S(2)}) copy-start(bf16[96,1024]{1,0:T(8,128)(2,1)S(1)} %collective-permute-done.10.refs_12_) | copy-start | bytes 589828
  99.9 25.2 %collective-permute-start.13 = (bf16[96,1024]{1,0:T(8,128)(2,1)}, bf16[96,1024]{1,0:T(8,128)(2,1)S(1)}, u32[]{:S(2)}, u32[]{:S(2)}) collective-permute-start(bf16[96,1024]{1,0:T(8,128)(2,1)} %get-tuple-element.34), channel_id=1, source_target_pairs={{0,5},{1,6},{2,7},{3,0},{4,1},{5,2},{6,3},{7,4},{8,13},{9,14},{10,... | collective-permute-start | bytes 589832 | tf_op jit(solution)/shard_map/ppermute | solution.py:21
  103.0 41.2 %copy-start.4 = (bf16[1024,128]{1,0:T(8,128)(2,1)}, bf16[1024,128]{1,0:T(8,128)(2,1)S(1)}, u32[]{:S(2)}) copy-start(bf16[1024,128]{1,0:T(8,128)(2,1)S(1)} %collective-permute-done.5.refs_6_) | copy-start | bytes 786436
  103.0 41.1 %collective-permute-start.6 = (bf16[1024,128]{1,0:T(8,128)(2,1)S(1)}, bf16[1024,128]{1,0:T(8,128)(2,1)S(1)}, u32[]{:S(2)}, u32[]{:S(2)}) collective-permute-start(bf16[1024,128]{1,0:T(8,128)(2,1)S(1)} %collective-permute-done.5.refs_6_), channel_id=1, source_target_pairs={{0,7},{1,0},{2,1},{3,2},{4,3},{5,4},{6,5},{7,6},{8,15},{9,8},{10,9... | collective-permute-start | bytes 786440 | tf_op jit(solution)/shard_map/ppermute | solution.py:21
  105.5 38.7 %copy-start.5 = (bf16[1024,128]{1,0:T(8,128)(2,1)}, bf16[1024,128]{1,0:T(8,128)(2,1)S(1)}, u32[]{:S(2)}) copy-start(bf16[1024,128]{1,0:T(8,128)(2,1)S(1)} %collective-permute-done.2.refs_3_) | copy-start | bytes 786436
  105.5 38.6 %collective-permute-start.3 = (bf16[1024,128]{1,0:T(8,128)(2,1)S(1)}, bf16[1024,128]{1,0:T(8,128)(2,1)S(1)}, u32[]{:S(2)}, u32[]{:S(2)}) collective-permute-start(bf16[1024,128]{1,0:T(8,128)(2,1)S(1)} %collective-permute-done.2.refs_3_), channel_id=1, source_target_pairs={{0,1},{1,2},{2,3},{3,4},{4,5},{5,6},{6,7},{7,0},{8,9},{9,10},{10,1... | collective-permute-start | bytes 786440 | tf_op jit(solution)/shard_map/ppermute | solution.py:21
  109.7 34.4 %copy-start.9 = (bf16[96,1024]{1,0:T(8,128)(2,1)}, bf16[96,1024]{1,0:T(8,128)(2,1)S(1)}, u32[]{:S(2)}) copy-start(bf16[96,1024]{1,0:T(8,128)(2,1)S(1)} %collective-permute-done.11.refs_13_) | copy-start | bytes 589828
  109.7 17.3 %collective-permute-start.7 = (bf16[96,1024]{1,0:T(8,128)(2,1)}, bf16[96,1024]{1,0:T(8,128)(2,1)S(1)}, u32[]{:S(2)}, u32[]{:S(2)}) collective-permute-start(bf16[96,1024]{1,0:T(8,128)(2,1)} %get-tuple-element.28), channel_id=1, source_target_pairs={{0,1},{1,2},{2,3},{3,4},{4,5},{5,6},{6,7},{7,0},{8,9},{9,10},{10,1... | collective-permute-start | bytes 589832 | tf_op jit(solution)/shard_map/ppermute | solution.py:21
  116.5 27.7 %copy-start.10 = (bf16[96,1024]{1,0:T(8,128)(2,1)}, bf16[96,1024]{1,0:T(8,128)(2,1)S(1)}, u32[]{:S(2)}) copy-start(bf16[96,1024]{1,0:T(8,128)(2,1)S(1)} %collective-permute-done.12.refs_14_) | copy-start | bytes 589828
  116.5 12.6 %collective-permute-start.8 = (bf16[96,1024]{1,0:T(8,128)(2,1)}, bf16[96,1024]{1,0:T(8,128)(2,1)S(1)}, u32[]{:S(2)}, u32[]{:S(2)}) collective-permute-start(bf16[96,1024]{1,0:T(8,128)(2,1)} %get-tuple-element.29), channel_id=1, source_target_pairs={{0,2},{1,3},{2,4},{3,5},{4,6},{5,7},{6,0},{7,1},{8,10},{9,11},{10,... | collective-permute-start | bytes 589832 | tf_op jit(solution)/shard_map/ppermute | solution.py:21
  125.1 19.1 %copy-start.11 = (bf16[96,1024]{1,0:T(8,128)(2,1)}, bf16[96,1024]{1,0:T(8,128)(2,1)S(1)}, u32[]{:S(2)}) copy-start(bf16[96,1024]{1,0:T(8,128)(2,1)S(1)} %collective-permute-done.13.refs_15_) | copy-start | bytes 589828
  125.1 18.9 %collective-permute-start.9 = (bf16[96,1024]{1,0:T(8,128)(2,1)}, bf16[96,1024]{1,0:T(8,128)(2,1)S(1)}, u32[]{:S(2)}, u32[]{:S(2)}) collective-permute-start(bf16[96,1024]{1,0:T(8,128)(2,1)} %get-tuple-element.30), channel_id=1, source_target_pairs={{0,3},{1,4},{2,5},{3,6},{4,7},{5,0},{6,1},{7,2},{8,11},{9,12},{10,... | collective-permute-start | bytes 589832 | tf_op jit(solution)/shard_map/ppermute | solution.py:21
  127.1 17.1 %copy-start.12 = (bf16[96,1024]{1,0:T(8,128)(2,1)}, bf16[96,1024]{1,0:T(8,128)(2,1)S(1)}, u32[]{:S(2)}) copy-start(bf16[96,1024]{1,0:T(8,128)(2,1)S(1)} %collective-permute-done.7.refs_9_) | copy-start | bytes 589828
  129.1 15.1 %copy-start.13 = (bf16[96,1024]{1,0:T(8,128)(2,1)}, bf16[96,1024]{1,0:T(8,128)(2,1)S(1)}, u32[]{:S(2)}) copy-start(bf16[96,1024]{1,0:T(8,128)(2,1)S(1)} %collective-permute-done.8.refs_10_) | copy-start | bytes 589828
  144.1 0.7 copy-start.14
  144.1 0.8 copy-start.6
  144.1 0.8 copy-start.7
  149.7 20.4 %all-to-all-start.2 = ((bf16[64,24,128]{2,1,0:T(8,128)(2,1)}), bf16[64,24,128]{2,1,0:T(8,128)(2,1)S(1)}, u32[]{:S(2)}, u32[]{:S(2)}) async-start(bf16[64,24,128]{2,1,0:T(8,128)(2,1)} %shard_map.88), calls=%async_computation.2 | async-start | bytes 786432 | tf_op jit(solution)/shard_map/all_to_all | solution.py:185

commit v5 on v3

--- a/solution.py
+++ b/solution.py
@@ -22,19 +22,23 @@
 
 
 def offsets(count):
-    return [0] + [-s for s in range(1, count // 2 + 1)] + list(range(1, (count + 1) // 2))
-
-
-def ring_gather(array, axis):
+    half = count // 2
+    return [0] + [sign * s for s in range(1, half) for sign in (-1, 1)] + [half]
+
+
+def ring_gather(array, axis, cores):
     count = lax.axis_size(axis)
-    up, down, ups, downs = array, array, [], []
-    for s in range(1, count // 2 + 1):
+    half = count // 2
+    up, down, shards = array, array, [array]
+    for _ in range(1, half):
         up = ring(up, axis, 1)
-        ups.append(up)
-        if s < (count + 1) // 2:
-            down = ring(down, axis, -1)
-            downs.append(down)
-    return [array] + ups + downs
+        down = ring(down, axis, -1)
+        shards += [up, down]
+    last = jnp.where(lax.axis_index(cores) == 0, up, down)
+    pairs = [(i, (i + 1) % count) for i in range(count)]
+    pairs += [(count + i, count + (i - 1) % count) for i in range(count)]
+    shards.append(lax.ppermute(last, (cores, axis), pairs))
+    return shards
 
 
 def dot(a, b, dims=((1,), (0,))):
@@ -57,25 +61,61 @@
             out[half:, g * width : (g + 1) * width] = right[g * rows : (g + 1) * rows, pl.ds(start, width)]
 
 
+def right_rows(root):
+    half = root.shape[0] * 2 // 3
+    quarter = root.shape[1] // 4
+    return [root[half:, g * quarter : (g + 1) * quarter] for g in range(4)]
+
+
+def inner_kernel(count, *refs):
+    sources, (out, shard_buffer, root_buffer, arrived) = refs[: 2 * count], refs[2 * count :]
+    shards = [shard_buffer.at[i] for i in range(count)]
+    roots = [root_buffer.at[i] for i in range(count)]
+    copies = [
+        pltpu.make_async_copy(source, target, arrived.at[i])
+        for i, (source, target) in enumerate(zip(sources, shards + roots))
+    ]
+    pairs = [tuple(range(i, min(i + 2, count))) for i in range(0, count, 2)]
+    for pair in pairs:
+        for i in pair:
+            copies[i].start()
+            copies[count + i].start()
+    inner = None
+    for pair in pairs:
+        for i in pair:
+            copies[i].wait()
+            copies[count + i].wait()
+        left = jnp.concatenate([shards[i][...] for i in pair], axis=1)
+        term = dot(left, jnp.concatenate([r for i in pair for r in right_rows(roots[i])], axis=0))
+        inner = term if inner is None else inner + term
+    out[...] = inner
+
+
 def precondition_kernel(count, *refs):
-    shards, roots, (out,) = refs[:count], refs[count : 2 * count], refs[2 * count :]
+    inner_in, shard_in, sources = refs[0], refs[1], refs[2 : 2 + count]
+    out, inner_buffer, shard_buffer, root_buffer, left, arrived = refs[2 + count :]
+    half = left.shape[0] // count
+    copies = [
+        pltpu.make_async_copy(shard_in, shard_buffer, arrived.at[0]),
+        pltpu.make_async_copy(sources[-1], root_buffer, arrived.at[1]),
+        pltpu.make_async_copy(inner_in, inner_buffer, arrived.at[2]),
+    ]
+    for i in range(count):
+        rows = left.at[i * half : (i + 1) * half]
+        copies.append(pltpu.make_async_copy(sources[i].at[:half], rows, arrived.at[3 + i]))
+    for copy in copies:
+        copy.start()
+    for copy in copies[:3]:
+        copy.wait()
     me = lax.axis_index("dp")
-    width = shards[0].shape[1]
-    half = 64
-    quarter = roots[0].shape[1] // 4
-
-    def right(i):
-        return [roots[i][half:, g * quarter : (g + 1) * quarter] for g in range(4)]
-
-    inner = None
-    for i in range(0, count, 2):
-        pair = jnp.concatenate([shards[i][...], shards[i + 1][...]], axis=1)
-        term = dot(pair, jnp.concatenate(right(i) + right(i + 1), axis=0))
-        inner = term if inner is None else inner + term
+    width = shard_buffer.shape[1]
+    last = dot(shard_buffer[...], jnp.concatenate(right_rows(root_buffer), axis=0))
+    inner = inner_buffer[...] + last
     high = inner.astype(jnp.bfloat16)
     low = (inner - high.astype(jnp.float32)).astype(jnp.bfloat16)
-    left = jnp.concatenate([root[:half, :] for root in roots], axis=0)
-    both = dot(left, high) + dot(left, low)
+    for copy in copies[3:]:
+        copy.wait()
+    both = dot(left[...], high) + dot(left[...], low)
     total = jnp.sum(jnp.sum(both * both, axis=0, keepdims=True), axis=1, keepdims=True)
     first = total.astype(jnp.bfloat16).astype(jnp.float32)
     second = (total - first).astype(jnp.bfloat16).astype(jnp.float32)
@@ -119,9 +159,8 @@
 
     slot_ids = jnp.arange(total_slots, dtype=jnp.int32)
     matches = block_slot[None, :] == slot_ids[:, None]
-    filled = jnp.any(matches, axis=1)
     numbers = jnp.arange(block_count, dtype=jnp.int32)
-    source = jnp.sum(jnp.where(matches, numbers[None, :], 0), axis=1)
+    source = block_count + jnp.sum(jnp.where(matches, numbers[None, :] - block_count, 0), axis=1)
 
     shares = rows.reshape(row_dev, block_count, replicas, shared).transpose(2, 1, 0, 3)
     shares = shares.reshape(replicas, block_count * row_dev, shared)
@@ -140,18 +179,38 @@
 
     summed = jnp.sum(received.astype(jnp.float32), axis=0)
     summed = summed.astype(jnp.bfloat16).reshape(block_count, row_dev, shared)
-    outgoing = jnp.where(
-        filled[:, None, None], jnp.take(summed, source, axis=0), jnp.zeros((), jnp.bfloat16)
-    )
+    summed = jnp.pad(summed, ((0, 4), (0, 0), (0, 0)))
+    outgoing = summed.at[source].get(mode="promise_in_bounds")
     incoming = lax.all_to_all(outgoing, FSDP, 0, 0, tiled=True)
-    shards = ring_gather(incoming.reshape(block_size, shared), "dp")
-
+    shards = ring_gather(incoming.reshape(block_size, shared), "dp", FSDP[2])
+
+    anywhere = pl.BlockSpec(memory_space=pl.ANY)
+    before = replicas - 1
+    quarter = block_size // quarters
+    inner = pl.pallas_call(
+        functools.partial(inner_kernel, before),
+        out_shape=jax.ShapeDtypeStruct((block_size, quarter), jnp.float32),
+        in_specs=[anywhere] * (2 * before),
+        out_specs=VMEM,
+        scratch_shapes=[
+            pltpu.VMEM((before,) + shards[0].shape, jnp.bfloat16),
+            pltpu.VMEM((before,) + roots[0].shape, jnp.bfloat16),
+            pltpu.SemaphoreType.DMA((2 * before,)),
+        ],
+    )(*shards[:-1], *roots[:-1])
     message = pl.pallas_call(
         functools.partial(precondition_kernel, replicas),
         out_shape=jax.ShapeDtypeStruct((total_slots, row_dev + 8, shared), jnp.bfloat16),
-        in_specs=[VMEM] * (2 * replicas),
+        in_specs=[anywhere] * (2 + replicas),
         out_specs=VMEM,
-    )(*shards, *roots)
+        scratch_shapes=[
+            pltpu.VMEM(inner.shape, jnp.float32),
+            pltpu.VMEM(shards[0].shape, jnp.bfloat16),
+            pltpu.VMEM(roots[0].shape, jnp.bfloat16),
+            pltpu.VMEM((block_size // 2, block_size), jnp.bfloat16),
+            pltpu.SemaphoreType.DMA((3 + replicas,)),
+        ],
+    )(inner, shards[-1], *roots)
     back = lax.all_to_all(message, FSDP, 0, 0, tiled=True)
 
     left_new, right_new = pl.pallas_call(
@@ -161,7 +220,7 @@
         out_specs=[VMEM] * 2,
     )(*shards, left_stats, right_stats)
 
-    picked = jnp.take(back, block_slot, axis=0)
+    picked = back.at[block_slot].get(mode="promise_in_bounds")
     terms = jnp.zeros((32, shared), jnp.bfloat16).at[:block_count].set(picked[:, row_dev, :])
     tiles = picked[:, :row_dev].reshape(block_count * row_dev, shared)
     gathered = lax.all_gather(jnp.concatenate([tiles, terms]), "dp", axis=0, tiled=False)

time: 199 us -> 196 us (0.985)
  the two profiles are of different devices: /device:TPU:8 before, /device:TPU:6 now
where the time goes in v5:
time: 196 us; the launch traced here: 195 us
  starting transfers between devices  67 us (34%)
  blocking collectives  53 us (27%)
  waiting for transfers between devices  52.9 us (27%)
  Pallas kernels  13.8 us (7%)
  local copies, waits for them, and re-layouts  6.42 us (3%)
    ppermute x13, starting transfers between devices, ring(): lax.ppermute(array, axis, [(i, (i + step) % count) for i in range(count)])  46.4 us
    all_gather x1, blocking collectives, step(): lax.all_gather(jnp.concatenate([tiles, terms]), 'dp', axis=0, tiled=False)  30.9 us
    all_to_all x1, waiting for transfers between devices, step(): received = lax.all_to_all(shares, 'dp', 0, 0, tiled=True)  25.8 us
    all_to_all x1, blocking collectives, step(): incoming = lax.all_to_all(outgoing, FSDP, 0, 0, tiled=True)  22.1 us
    ppermute x13, waiting for transfers between devices, ring(): lax.ppermute(array, axis, [(i, (i + step) % count) for i in range(count)])  17 us
    all_to_all x1, starting transfers between devices, step(): received = lax.all_to_all(shares, 'dp', 0, 0, tiled=True)  10.4 us
    all_to_all x1, waiting for transfers between devices, step(): back = lax.all_to_all(message, FSDP, 0, 0, tiled=True)  10.1 us
    all_to_all x1, starting transfers between devices, step(): back = lax.all_to_all(message, FSDP, 0, 0, tiled=True)  6.7 us
  transfers between devices with their start and end apart: 16, of which 6 were waited for; matrix products, arithmetic and copies ran while one was open for 0% of the time, Pallas kernels for 5%

profile of v5, /device:TPU:6, one launch (start us, length us, event | category | flops | bytes accessed | tf_op | source)
XLA Modules:
  0.0 194.9 jit_solution(14657412068011202417)
XLA Ops:
  0.6 1.3 copy.14
  1.9 1.3 copy.11
  3.2 10.4 %all-to-all-start = ((bf16[8,448,128]{2,1,0:T(8,128)(2,1)}), bf16[8,448,128]{2,1,0:T(8,128)(2,1)S(1)}, u32[]{:S(2)}, u32[]{:S(2)}) async-start(bf16[8,448,128]{2,1,0:T(8,128)(2,1)} %bitcast.1), calls=%async_computation | async-start | bytes 1835008 | tf_op jit(solution)/shard_map/all_to_all | solution.py:167
  13.7 0.1 select_reduce_fusion
  13.8 25.8 %all-to-all-done = bf16[8,448,128]{2,1,0:T(8,128)(2,1)S(1)} async-done(((bf16[8,448,128]{2,1,0:T(8,128)(2,1)}), bf16[8,448,128]{2,1,0:T(8,128)(2,1)S(1)}, u32[]{:S(2)}, u32[]{:S(2)}) %all-to-all-start) | async-done | bytes 917536 | tf_op jit(solution)/shard_map/all_to_all | solution.py:167
  39.6 0.1 reduce_sum.30
  39.7 0.6 gather_fusion
  40.4 22.1 %all_to_all.15 = bf16[64,16,128]{2,1,0:T(8,128)(2,1)S(1)} all-to-all(bf16[64,16,128]{2,1,0:T(8,128)(2,1)S(1)} %gather_fusion), channel_id=1, replica_groups=mesh['fsdp_0'=4,'fsdp_1'=8,'fsdp_2'=2,'dp'=8] {'fsdp_0','fsdp_1','fsdp_2'}, dimensions={0} | all-to-all | bytes 524288 | tf_op jit(solution)/shard_map/all_to_all | solution.py:184
  62.5 2.5 %collective-permute-start = (bf16[1024,128]{1,0:T(8,128)(2,1)S(1)}, bf16[1024,128]{1,0:T(8,128)(2,1)S(1)}, u32[]{:S(2)}, u32[]{:S(2)}) collective-permute-start(bf16[1024,128]{1,0:T(8,128)(2,1)S(1)} %bitcast.31), channel_id=1, source_target_pairs={{0,1},{1,2},{2,3},{3,4},{4,5},{5,6},{6,7},{7,0},{8,9},{9,10},{10,1... | collective-permute-start | bytes 786440 | tf_op jit(solution)/shard_map/ppermute | solution.py:21
  65.0 4.6 %collective-permute-start.1 = (bf16[1024,128]{1,0:T(8,128)(2,1)S(1)}, bf16[1024,128]{1,0:T(8,128)(2,1)S(1)}, u32[]{:S(2)}, u32[]{:S(2)}) collective-permute-start(bf16[1024,128]{1,0:T(8,128)(2,1)S(1)} %bitcast.32), channel_id=1, source_target_pairs={{0,7},{1,0},{2,1},{3,2},{4,3},{5,4},{6,5},{7,6},{8,15},{9,8},{10,9... | collective-permute-start | bytes 786440 | tf_op jit(solution)/shard_map/ppermute | solution.py:21
  69.6 4.4 %collective-permute-done.refs_1_ = bf16[1024,128]{1,0:T(8,128)(2,1)S(1)} collective-permute-done((bf16[1024,128]{1,0:T(8,128)(2,1)S(1)}, bf16[1024,128]{1,0:T(8,128)(2,1)S(1)}, u32[]{:S(2)}, u32[]{:S(2)}) %collective-permute-start) | collective-permute-done | bytes 262176 | tf_op jit(solution)/shard_map/ppermute | solution.py:21
  73.9 1.9 collective-permute-start.2
  75.9 0.0 collective-permute-done.1.refs_2_
  75.9 5.1 %collective-permute-start.3 = (bf16[1024,128]{1,0:T(8,128)(2,1)S(1)}, bf16[1024,128]{1,0:T(8,128)(2,1)S(1)}, u32[]{:S(2)}, u32[]{:S(2)}) collective-permute-start(bf16[1024,128]{1,0:T(8,128)(2,1)S(1)} %collective-permute-done.1.refs_2_), channel_id=1, source_target_pairs={{0,7},{1,0},{2,1},{3,2},{4,3},{5,4},{6,5},{7,6},{8,15},{9,8},{10,9... | collective-permute-start | bytes 786440 | tf_op jit(solution)/shard_map/ppermute | solution.py:21
  81.0 3.5 %collective-permute-done.2.refs_3_ = bf16[1024,128]{1,0:T(8,128)(2,1)S(1)} collective-permute-done((bf16[1024,128]{1,0:T(8,128)(2,1)S(1)}, bf16[1024,128]{1,0:T(8,128)(2,1)S(1)}, u32[]{:S(2)}, u32[]{:S(2)}) %collective-permute-start.2) | collective-permute-done | bytes 262176 | tf_op jit(solution)/shard_map/ppermute | solution.py:21
  84.5 1.9 collective-permute-start.4
  86.4 0.0 collective-permute-done.3.refs_4_
  86.5 5.1 %collective-permute-start.5 = (bf16[1024,128]{1,0:T(8,128)(2,1)S(1)}, bf16[1024,128]{1,0:T(8,128)(2,1)S(1)}, u32[]{:S(2)}, u32[]{:S(2)}) collective-permute-start(bf16[1024,128]{1,0:T(8,128)(2,1)S(1)} %collective-permute-done.3.refs_4_), channel_id=1, source_target_pairs={{0,7},{1,0},{2,1},{3,2},{4,3},{5,4},{6,5},{7,6},{8,15},{9,8},{10,9... | collective-permute-start | bytes 786440 | tf_op jit(solution)/shard_map/ppermute | solution.py:21
  91.6 2.2 %shard_map.86 = (bf16[96,1024]{1,0:T(8,128)(2,1)}, bf16[96,1024]{1,0:T(8,128)(2,1)}, bf16[96,1024]{1,0:T(8,128)(2,1)}, bf16[96,1024]{1,0:T(8,128)(2,1)}, bf16[96...) custom-call(bf16[128,1024]{1,0:T(8,128)(2,1)} %bitcast.39, ...), custom_call_target="tpu_custom_call" | custom-call | tf_op jit(solution)/shard_map/pallas_call | solution.py:169
  93.8 1.9 collective-permute-start.10
  95.7 3.1 %collective-permute-start.11 = (bf16[96,1024]{1,0:T(8,128)(2,1)}, bf16[96,1024]{1,0:T(8,128)(2,1)S(1)}, u32[]{:S(2)}, u32[]{:S(2)}) collective-permute-start(bf16[96,1024]{1,0:T(8,128)(2,1)} %get-tuple-element.32), channel_id=1, source_target_pairs={{0,3},{1,4},{2,5},{3,6},{4,7},{5,0},{6,1},{7,2},{8,11},{9,12},{10,... | collective-permute-start | bytes 589832 | tf_op jit(solution)/shard_map/ppermute | solution.py:21
  98.8 5.8 %collective-permute-start.12 = (bf16[96,1024]{1,0:T(8,128)(2,1)}, bf16[96,1024]{1,0:T(8,128)(2,1)S(1)}, u32[]{:S(2)}, u32[]{:S(2)}) collective-permute-start(bf16[96,1024]{1,0:T(8,128)(2,1)} %get-tuple-element.33), channel_id=1, source_target_pairs={{0,5},{1,6},{2,7},{3,0},{4,1},{5,2},{6,3},{7,4},{8,13},{9,14},{10,... | collective-permute-start | bytes 589832 | tf_op jit(solution)/shard_map/ppermute | solution.py:21
  104.6 0.0 collective-permute-done.4.refs_5_
  104.6 0.0 collective-permute-done.5.refs_6_
  104.7 3.4 %collective-permute-start.6 = (bf16[1024,128]{1,0:T(8,128)(2,1)S(1)}, bf16[1024,128]{1,0:T(8,128)(2,1)S(1)}, u32[]{:S(2)}, u32[]{:S(2)}) collective-permute-start(bf16[1024,128]{1,0:T(8,128)(2,1)S(1)} %broadcast_select_fusion), channel_id=1, source_target_pairs={{0,1},{1,2},{2,3},{3,4},{4,5},{5,6},{6,7},{7,0},{8,15},{9,8},{10,9... | collective-permute-start | bytes 786440 | tf_op jit(solution)/shard_map/ppermute | solution.py:40
  108.1 3.9 %collective-permute-start.7 = (bf16[96,1024]{1,0:T(8,128)(2,1)}, bf16[96,1024]{1,0:T(8,128)(2,1)S(1)}, u32[]{:S(2)}, u32[]{:S(2)}) collective-permute-start(bf16[96,1024]{1,0:T(8,128)(2,1)} %get-tuple-element.28), channel_id=1, source_target_pairs={{0,1},{1,2},{2,3},{3,4},{4,5},{5,6},{6,7},{7,0},{8,9},{9,10},{10,1... | collective-permute-start | bytes 589832 | tf_op jit(solution)/shard_map/ppermute | solution.py:21
  112.0 0.0 collective-permute-done.10.refs_11_.refs_6_
  112.0 3.1 %collective-permute-start.8 = (bf16[96,1024]{1,0:T(8,128)(2,1)}, bf16[96,1024]{1,0:T(8,128)(2,1)S(1)}, u32[]{:S(2)}, u32[]{:S(2)}) collective-permute-start(bf16[96,1024]{1,0:T(8,128)(2,1)} %get-tuple-element.29), channel_id=1, source_target_pairs={{0,7},{1,0},{2,1},{3,2},{4,3},{5,4},{6,5},{7,6},{8,15},{9,8},{10,9... | collective-permute-start | bytes 589832 | tf_op jit(solution)/shard_map/ppermute | solution.py:21
  115.1 0.0 collective-permute-done.11.refs_12_.refs_7_
  115.2 4.1 %collective-permute-start.9 = (bf16[96,1024]{1,0:T(8,128)(2,1)}, bf16[96,1024]{1,0:T(8,128)(2,1)S(1)}, u32[]{:S(2)}, u32[]{:S(2)}) collective-permute-start(bf16[96,1024]{1,0:T(8,128)(2,1)} %get-tuple-element.30), channel_id=1, source_target_pairs={{0,2},{1,3},{2,4},{3,5},{4,6},{5,7},{6,0},{7,1},{8,10},{9,11},{10,... | collective-permute-start | bytes 589832 | tf_op jit(solution)/shard_map/ppermute | solution.py:21
  119.3 3.4 %collective-permute-start.13 = (bf16[96,1024]{1,0:T(8,128)(2,1)}, bf16[96,1024]{1,0:T(8,128)(2,1)}, u32[]{:S(2)}, u32[]{:S(2)}) collective-permute-start(bf16[96,1024]{1,0:T(8,128)(2,1)} %get-tuple-element.34), channel_id=1, source_target_pairs={{0,4},{1,5},{2,6},{3,7},{4,0},{5,1},{6,2},{7,3},{8,12},{9,13},{10,... | collective-permute-start | bytes 589832 | tf_op jit(solution)/shard_map/ppermute | solution.py:21
  122.7 2.7 %collective-permute-done.7.refs_8_.refs_3_ = bf16[96,1024]{1,0:T(8,128)(2,1)S(1)} collective-permute-done((bf16[96,1024]{1,0:T(8,128)(2,1)}, bf16[96,1024]{1,0:T(8,128)(2,1)S(1)}, u32[]{:S(2)}, u32[]{:S(2)}) %collective-permute-start.7) | collective-permute-done | bytes 196640 | tf_op jit(solution)/shard_map/ppermute | solution.py:21
  125.4 6.4 %collective-permute-done.9.refs_10_.refs_5_ = bf16[96,1024]{1,0:T(8,128)(2,1)S(1)} collective-permute-done((bf16[96,1024]{1,0:T(8,128)(2,1)}, bf16[96,1024]{1,0:T(8,128)(2,1)S(1)}, u32[]{:S(2)}, u32[]{:S(2)}) %collective-permute-start.9) | collective-permute-done | bytes 196640 | tf_op jit(solution)/shard_map/ppermute | solution.py:21
  131.9 0.6 copy-done.13
  132.5 4.0 %shard_map.87.refs_0_ = f32[1024,256]{1,0:T(8,128)} custom-call(bf16[1024,128]{1,0:T(8,128)(2,1)} %bitcast.33, bf16[1024,128]{1,0:T(8,128)(2,1)} %copy-done.3, bf16[1024,128]{1,0:T(8,128)(2,1)} %copy-done.4, bf16[1024,128]{1,0:T(8,128)(2,1)} %copy-done.5, bf16[1024,128]{1,0:T(8,128)(2,1)} %copy-done.6, bf16[1024,128]{1,0:T(8,128)(2,1)} %copy-done.1, ...), custom_call_target="tpu_custom_call" | custom-call | tf_op jit(solution)/shard_map/pallas_call | solution.py:190
  136.5 0.0 collective-permute-done.13.refs_9_
  136.5 0.0 collective-permute-done.6.refs_7_.refs_1_
  136.5 0.7 copy-done.7
  137.2 3.6 %shard_map.88 = bf16[64,24,128]{2,1,0:T(8,128)(2,1)} custom-call(f32[1024,256]{1,0:T(8,128)} %shard_map.87.refs_0_, bf16[1024,128]{1,0:T(8,128)(2,1)} %copy-done.7, bf16[96,1024]{1,0:T(8,128)(2,1)} %get-tuple-element.27.refs_7_.refs_2_, bf16[96,1024]{1,0:T(8,128)(2,1)} %copy-done.11, bf16[96,1024]{1,0:T(8,128)(2,1)} %copy-done.12, ...), custom_call_target="tpu_custom_call" | custom-call | tf_op jit(solution)/shard_map/pallas_call | solution.py:201
  140.9 6.7 %all-to-all-start.2 = ((bf16[64,24,128]{2,1,0:T(8,128)(2,1)}), bf16[64,24,128]{2,1,0:T(8,128)(2,1)S(1)}, u32[]{:S(2)}, u32[]{:S(2)}) async-start(bf16[64,24,128]{2,1,0:T(8,128)(2,1)} %shard_map.88), calls=%async_computation.2 | async-start | bytes 786432 | tf_op jit(solution)/shard_map/all_to_all | solution.py:214
  147.6 4.0 %shard_map.85 = (f32[1,128,1024]{2,1,0:T(8,128)}, f32[1,128,1024]{2,1,0:T(8,128)}) custom-call(bf16[1024,128]{1,0:T(8,128)(2,1)} %bitcast.34, bf16[1024,128]{1,0:T(8,128)(2,1)} %copy-done.3, bf16[1024,128]{1,0:T(8,128)(2,1)} %copy-done.4, bf16[1024,128]{1,0:T(8,128)(2,1)} %copy-done.5, bf16[1024,128]{1,0:T(8,128)(2,1)} %copy-done.6, ...), custom_call_target="tpu_custom_call" | custom-call | tf_op jit(solution)/shard_map/pallas_call | solution.py:216
  151.6 10.1 %all-to-all-done.2 = bf16[64,24,128]{2,1,0:T(8,128)(2,1)S(1)} async-done(((bf16[64,24,128]{2,1,0:T(8,128)(2,1)}), bf16[64,24,128]{2,1,0:T(8,128)(2,1)S(1)}, u32[]{:S(2)}, u32[]{:S(2)}) %all-to-all-start.2) | async-done | bytes 393248 | tf_op jit(solution)/shard_map/all_to_all | solution.py:214
  161.7 0.6 gather_fusion.1
  162.3 30.9 %all-gather = bf16[3840,128]{1,0:T(8,128)(2,1)S(1)} all-gather(bf16[480,128]{1,0:T(8,128)(2,1)S(1)} %fusion.3), channel_id=2, replica_groups=mesh['fsdp_0'=4,'fsdp_1'=8,'fsdp_2'=2,'dp'=8] {'dp'}, dimensions={0}, use_global_device_ids=true | all-gather | bytes 1105920 | tf_op jit(solution)/shard_map/all_gather | solution.py:226
  193.2 0.1 slice.40
  193.3 0.1 convert_reduce_fusion
  193.4 0.3 fusion.1
  193.7 1.2 copy.12
  (42 shorter events, 0.2 us)
Async XLA Ops:
  3.2 10.5 %copy-start.14 = (s32[28]{0:T(128)S(1)}, s32[28]{0:T(128)}, u32[]{:S(2)}) copy-start(s32[28]{0:T(128)} %param.9) | copy-start | bytes 340
  3.2 36.4 %all-to-all-start = ((bf16[8,448,128]{2,1,0:T(8,128)(2,1)}), bf16[8,448,128]{2,1,0:T(8,128)(2,1)S(1)}, u32[]{:S(2)}, u32[]{:S(2)}) async-start(bf16[8,448,128]{2,1,0:T(8,128)(2,1)} %bitcast.1), calls=%async_computation | async-start | bytes 1835008 | tf_op jit(solution)/shard_map/all_to_all | solution.py:167
  62.5 69.3 %copy-start = (bf16[64,16,128]{2,1,0:T(8,128)(2,1)}, bf16[64,16,128]{2,1,0:T(8,128)(2,1)S(1)}, u32[]{:S(2)}) copy-start(bf16[64,16,128]{2,1,0:T(8,128)(2,1)S(1)} %all_to_all.15) | copy-start | bytes 786436
  62.5 11.4 %collective-permute-start = (bf16[1024,128]{1,0:T(8,128)(2,1)S(1)}, bf16[1024,128]{1,0:T(8,128)(2,1)S(1)}, u32[]{:S(2)}, u32[]{:S(2)}) collective-permute-start(bf16[1024,128]{1,0:T(8,128)(2,1)S(1)} %bitcast.31), channel_id=1, source_target_pairs={{0,1},{1,2},{2,3},{3,4},{4,5},{5,6},{6,7},{7,0},{8,9},{9,10},{10,1... | collective-permute-start | bytes 786440 | tf_op jit(solution)/shard_map/ppermute | solution.py:21
  65.0 10.9 %collective-permute-start.1 = (bf16[1024,128]{1,0:T(8,128)(2,1)S(1)}, bf16[1024,128]{1,0:T(8,128)(2,1)S(1)}, u32[]{:S(2)}, u32[]{:S(2)}) collective-permute-start(bf16[1024,128]{1,0:T(8,128)(2,1)S(1)} %bitcast.32), channel_id=1, source_target_pairs={{0,7},{1,0},{2,1},{3,2},{4,3},{5,4},{6,5},{7,6},{8,15},{9,8},{10,9... | collective-permute-start | bytes 786440 | tf_op jit(solution)/shard_map/ppermute | solution.py:21
  73.9 57.9 %copy-start.3 = (bf16[1024,128]{1,0:T(8,128)(2,1)}, bf16[1024,128]{1,0:T(8,128)(2,1)S(1)}, u32[]{:S(2)}) copy-start(bf16[1024,128]{1,0:T(8,128)(2,1)S(1)} %collective-permute-done.refs_1_) | copy-start | bytes 786436
  73.9 10.6 %collective-permute-start.2 = (bf16[1024,128]{1,0:T(8,128)(2,1)S(1)}, bf16[1024,128]{1,0:T(8,128)(2,1)S(1)}, u32[]{:S(2)}, u32[]{:S(2)}) collective-permute-start(bf16[1024,128]{1,0:T(8,128)(2,1)S(1)} %collective-permute-done.refs_1_), channel_id=1, source_target_pairs={{0,1},{1,2},{2,3},{3,4},{4,5},{5,6},{6,7},{7,0},{8,9},{9,10},{10,1... | collective-permute-start | bytes 786440 | tf_op jit(solution)/shard_map/ppermute | solution.py:21
  75.9 55.9 %copy-start.4 = (bf16[1024,128]{1,0:T(8,128)(2,1)}, bf16[1024,128]{1,0:T(8,128)(2,1)S(1)}, u32[]{:S(2)}) copy-start(bf16[1024,128]{1,0:T(8,128)(2,1)S(1)} %collective-permute-done.1.refs_2_) | copy-start | bytes 786436
  75.9 10.6 %collective-permute-start.3 = (bf16[1024,128]{1,0:T(8,128)(2,1)S(1)}, bf16[1024,128]{1,0:T(8,128)(2,1)S(1)}, u32[]{:S(2)}, u32[]{:S(2)}) collective-permute-start(bf16[1024,128]{1,0:T(8,128)(2,1)S(1)} %collective-permute-done.1.refs_2_), channel_id=1, source_target_pairs={{0,7},{1,0},{2,1},{3,2},{4,3},{5,4},{6,5},{7,6},{8,15},{9,8},{10,9... | collective-permute-start | bytes 786440 | tf_op jit(solution)/shard_map/ppermute | solution.py:21
  84.5 47.3 %copy-start.5 = (bf16[1024,128]{1,0:T(8,128)(2,1)}, bf16[1024,128]{1,0:T(8,128)(2,1)S(1)}, u32[]{:S(2)}) copy-start(bf16[1024,128]{1,0:T(8,128)(2,1)S(1)} %collective-permute-done.2.refs_3_) | copy-start | bytes 786436
  84.5 20.1 %collective-permute-start.4 = (bf16[1024,128]{1,0:T(8,128)(2,1)S(1)}, bf16[1024,128]{1,0:T(8,128)(2,1)S(1)}, u32[]{:S(2)}, u32[]{:S(2)}) collective-permute-start(bf16[1024,128]{1,0:T(8,128)(2,1)S(1)} %collective-permute-done.2.refs_3_), channel_id=1, source_target_pairs={{0,1},{1,2},{2,3},{3,4},{4,5},{5,6},{6,7},{7,0},{8,9},{9,10},{10,1... | collective-permute-start | bytes 786440 | tf_op jit(solution)/shard_map/ppermute | solution.py:21
  86.4 45.4 %copy-start.6 = (bf16[1024,128]{1,0:T(8,128)(2,1)}, bf16[1024,128]{1,0:T(8,128)(2,1)S(1)}, u32[]{:S(2)}) copy-start(bf16[1024,128]{1,0:T(8,128)(2,1)S(1)} %collective-permute-done.3.refs_4_) | copy-start | bytes 786436
  86.5 18.2 %collective-permute-start.5 = (bf16[1024,128]{1,0:T(8,128)(2,1)S(1)}, bf16[1024,128]{1,0:T(8,128)(2,1)S(1)}, u32[]{:S(2)}, u32[]{:S(2)}) collective-permute-start(bf16[1024,128]{1,0:T(8,128)(2,1)S(1)} %collective-permute-done.3.refs_4_), channel_id=1, source_target_pairs={{0,7},{1,0},{2,1},{3,2},{4,3},{5,4},{6,5},{7,6},{8,15},{9,8},{10,9... | collective-permute-start | bytes 786440 | tf_op jit(solution)/shard_map/ppermute | solution.py:21
  93.8 18.2 %collective-permute-start.10 = (bf16[96,1024]{1,0:T(8,128)(2,1)}, bf16[96,1024]{1,0:T(8,128)(2,1)S(1)}, u32[]{:S(2)}, u32[]{:S(2)}) collective-permute-start(bf16[96,1024]{1,0:T(8,128)(2,1)} %get-tuple-element.31), channel_id=1, source_target_pairs={{0,6},{1,7},{2,0},{3,1},{4,2},{5,3},{6,4},{7,5},{8,14},{9,15},{10,... | collective-permute-start | bytes 589832 | tf_op jit(solution)/shard_map/ppermute | solution.py:21
  95.7 19.4 %collective-permute-start.11 = (bf16[96,1024]{1,0:T(8,128)(2,1)}, bf16[96,1024]{1,0:T(8,128)(2,1)S(1)}, u32[]{:S(2)}, u32[]{:S(2)}) collective-permute-start(bf16[96,1024]{1,0:T(8,128)(2,1)} %get-tuple-element.32), channel_id=1, source_target_pairs={{0,3},{1,4},{2,5},{3,6},{4,7},{5,0},{6,1},{7,2},{8,11},{9,12},{10,... | collective-permute-start | bytes 589832 | tf_op jit(solution)/shard_map/ppermute | solution.py:21
  98.8 20.5 %collective-permute-start.12 = (bf16[96,1024]{1,0:T(8,128)(2,1)}, bf16[96,1024]{1,0:T(8,128)(2,1)S(1)}, u32[]{:S(2)}, u32[]{:S(2)}) collective-permute-start(bf16[96,1024]{1,0:T(8,128)(2,1)} %get-tuple-element.33), channel_id=1, source_target_pairs={{0,5},{1,6},{2,7},{3,0},{4,1},{5,2},{6,3},{7,4},{8,13},{9,14},{10,... | collective-permute-start | bytes 589832 | tf_op jit(solution)/shard_map/ppermute | solution.py:21
  104.6 27.2 %copy-start.1 = (bf16[1024,128]{1,0:T(8,128)(2,1)}, bf16[1024,128]{1,0:T(8,128)(2,1)S(1)}, u32[]{:S(2)}) copy-start(bf16[1024,128]{1,0:T(8,128)(2,1)S(1)} %collective-permute-done.4.refs_5_) | copy-start | bytes 786436
  104.6 27.2 %copy-start.2 = (bf16[1024,128]{1,0:T(8,128)(2,1)}, bf16[1024,128]{1,0:T(8,128)(2,1)S(1)}, u32[]{:S(2)}) copy-start(bf16[1024,128]{1,0:T(8,128)(2,1)S(1)} %collective-permute-done.5.refs_6_) | copy-start | bytes 786436
  104.7 31.8 %collective-permute-start.6 = (bf16[1024,128]{1,0:T(8,128)(2,1)S(1)}, bf16[1024,128]{1,0:T(8,128)(2,1)S(1)}, u32[]{:S(2)}, u32[]{:S(2)}) collective-permute-start(bf16[1024,128]{1,0:T(8,128)(2,1)S(1)} %broadcast_select_fusion), channel_id=1, source_target_pairs={{0,1},{1,2},{2,3},{3,4},{4,5},{5,6},{6,7},{7,0},{8,15},{9,8},{10,9... | collective-permute-start | bytes 786440 | tf_op jit(solution)/shard_map/ppermute | solution.py:40
  108.1 17.3 %collective-permute-start.7 = (bf16[96,1024]{1,0:T(8,128)(2,1)}, bf16[96,1024]{1,0:T(8,128)(2,1)S(1)}, u32[]{:S(2)}, u32[]{:S(2)}) collective-permute-start(bf16[96,1024]{1,0:T(8,128)(2,1)} %get-tuple-element.28), channel_id=1, source_target_pairs={{0,1},{1,2},{2,3},{3,4},{4,5},{5,6},{6,7},{7,0},{8,9},{9,10},{10,1... | collective-permute-start | bytes 589832 | tf_op jit(solution)/shard_map/ppermute | solution.py:21
  112.0 19.9 %copy-start.8 = (bf16[96,1024]{1,0:T(8,128)(2,1)}, bf16[96,1024]{1,0:T(8,128)(2,1)S(1)}, u32[]{:S(2)}) copy-start(bf16[96,1024]{1,0:T(8,128)(2,1)S(1)} %collective-permute-done.10.refs_11_.refs_6_) | copy-start | bytes 589828
  112.0 13.4 %collective-permute-start.8 = (bf16[96,1024]{1,0:T(8,128)(2,1)}, bf16[96,1024]{1,0:T(8,128)(2,1)S(1)}, u32[]{:S(2)}, u32[]{:S(2)}) collective-permute-start(bf16[96,1024]{1,0:T(8,128)(2,1)} %get-tuple-element.29), channel_id=1, source_target_pairs={{0,7},{1,0},{2,1},{3,2},{4,3},{5,4},{6,5},{7,6},{8,15},{9,8},{10,9... | collective-permute-start | bytes 589832 | tf_op jit(solution)/shard_map/ppermute | solution.py:21
  115.2 16.7 %copy-start.9 = (bf16[96,1024]{1,0:T(8,128)(2,1)}, bf16[96,1024]{1,0:T(8,128)(2,1)S(1)}, u32[]{:S(2)}) copy-start(bf16[96,1024]{1,0:T(8,128)(2,1)S(1)} %collective-permute-done.11.refs_12_.refs_7_) | copy-start | bytes 589828
  115.2 16.6 %collective-permute-start.9 = (bf16[96,1024]{1,0:T(8,128)(2,1)}, bf16[96,1024]{1,0:T(8,128)(2,1)S(1)}, u32[]{:S(2)}, u32[]{:S(2)}) collective-permute-start(bf16[96,1024]{1,0:T(8,128)(2,1)} %get-tuple-element.30), channel_id=1, source_target_pairs={{0,2},{1,3},{2,4},{3,5},{4,6},{5,7},{6,0},{7,1},{8,10},{9,11},{10,... | collective-permute-start | bytes 589832 | tf_op jit(solution)/shard_map/ppermute | solution.py:21
  119.3 12.6 %copy-start.10 = (bf16[96,1024]{1,0:T(8,128)(2,1)}, bf16[96,1024]{1,0:T(8,128)(2,1)S(1)}, u32[]{:S(2)}) copy-start(bf16[96,1024]{1,0:T(8,128)(2,1)S(1)} %collective-permute-done.12.refs_13_.refs_8_) | copy-start | bytes 589828
  119.3 17.2 %collective-permute-start.13 = (bf16[96,1024]{1,0:T(8,128)(2,1)}, bf16[96,1024]{1,0:T(8,128)(2,1)}, u32[]{:S(2)}, u32[]{:S(2)}) collective-permute-start(bf16[96,1024]{1,0:T(8,128)(2,1)} %get-tuple-element.34), channel_id=1, source_target_pairs={{0,4},{1,5},{2,6},{3,7},{4,0},{5,1},{6,2},{7,3},{8,12},{9,13},{10,... | collective-permute-start | bytes 589832 | tf_op jit(solution)/shard_map/ppermute | solution.py:21
  125.4 6.5 %copy-start.11 = (bf16[96,1024]{1,0:T(8,128)(2,1)}, bf16[96,1024]{1,0:T(8,128)(2,1)S(1)}, u32[]{:S(2)}) copy-start(bf16[96,1024]{1,0:T(8,128)(2,1)S(1)} %collective-permute-done.7.refs_8_.refs_3_) | copy-start | bytes 589828
  125.4 6.5 %copy-start.12 = (bf16[96,1024]{1,0:T(8,128)(2,1)}, bf16[96,1024]{1,0:T(8,128)(2,1)S(1)}, u32[]{:S(2)}) copy-start(bf16[96,1024]{1,0:T(8,128)(2,1)S(1)} %collective-permute-done.8.refs_9_.refs_4_) | copy-start | bytes 589828
  131.8 0.7 copy-start.13
  136.5 0.7 copy-start.7
  140.9 20.8 %all-to-all-start.2 = ((bf16[64,24,128]{2,1,0:T(8,128)(2,1)}), bf16[64,24,128]{2,1,0:T(8,128)(2,1)S(1)}, u32[]{:S(2)}, u32[]{:S(2)}) async-start(bf16[64,24,128]{2,1,0:T(8,128)(2,1)} %shard_map.88), calls=%async_computation.2 | async-start | bytes 786432 | tf_op jit(solution)/shard_map/all_to_all | solution.py:214

commit v6 on v5

--- a/solution.py
+++ b/solution.py
@@ -26,7 +26,7 @@
     return [0] + [sign * s for s in range(1, half) for sign in (-1, 1)] + [half]
 
 
-def ring_gather(array, axis, cores):
+def ring_gather(array, axis):
     count = lax.axis_size(axis)
     half = count // 2
     up, down, shards = array, array, [array]
@@ -34,10 +34,7 @@
         up = ring(up, axis, 1)
         down = ring(down, axis, -1)
         shards += [up, down]
-    last = jnp.where(lax.axis_index(cores) == 0, up, down)
-    pairs = [(i, (i + 1) % count) for i in range(count)]
-    pairs += [(count + i, count + (i - 1) % count) for i in range(count)]
-    shards.append(lax.ppermute(last, (cores, axis), pairs))
+    shards.append(ring(up, axis, 1))
     return shards
 
 
@@ -182,7 +179,7 @@
     summed = jnp.pad(summed, ((0, 4), (0, 0), (0, 0)))
     outgoing = summed.at[source].get(mode="promise_in_bounds")
     incoming = lax.all_to_all(outgoing, FSDP, 0, 0, tiled=True)
-    shards = ring_gather(incoming.reshape(block_size, shared), "dp", FSDP[2])
+    shards = ring_gather(incoming.reshape(block_size, shared), "dp")
 
     anywhere = pl.BlockSpec(memory_space=pl.ANY)
     before = replicas - 1

time: 196 us -> 193 us (0.985)
  waiting for transfers between devices: 52.9 us -> 46.4 us
  starting transfers between devices: 67 us -> 69.4 us
    ppermute x13 -> x14, waiting for transfers between devices: 17 us -> 10.6 us  [ring(): lax.ppermute(array, axis, [(i, (i + step) % count) for i in range(count)])]
    ppermute x13 -> x14, starting transfers between devices: 46.4 us -> 51.4 us  [ring(): lax.ppermute(array, axis, [(i, (i + step) % count) for i in range(count)])]
    ppermute x1 -> x0, starting transfers between devices: 3.37 us -> none  [ring_gather(): shards.append(lax.ppermute(last, (cores, axis), pairs))]
where the time goes in v6:
time: 193 us; the launch traced here: 192 us
  starting transfers between devices  69.4 us (36%)
  blocking collectives  53.5 us (28%)
  waiting for transfers between devices  46.4 us (24%)
  Pallas kernels  13.9 us (7%)
  local copies, waits for them, and re-layouts  7.2 us (4%)
    ppermute x14, starting transfers between devices, ring(): lax.ppermute(array, axis, [(i, (i + step) % count) for i in range(count)])  51.4 us
    all_gather x1, blocking collectives, step(): lax.all_gather(jnp.concatenate([tiles, terms]), 'dp', axis=0, tiled=False)  31.4 us
    all_to_all x1, waiting for transfers between devices, step(): received = lax.all_to_all(shares, 'dp', 0, 0, tiled=True)  25.8 us
    all_to_all x1, blocking collectives, step(): incoming = lax.all_to_all(outgoing, FSDP, 0, 0, tiled=True)  22.1 us
    ppermute x14, waiting for transfers between devices, ring(): lax.ppermute(array, axis, [(i, (i + step) % count) for i in range(count)])  10.6 us
    all_to_all x1, starting transfers between devices, step(): received = lax.all_to_all(shares, 'dp', 0, 0, tiled=True)  10.4 us
    all_to_all x1, waiting for transfers between devices, step(): back = lax.all_to_all(message, FSDP, 0, 0, tiled=True)  10.1 us
    all_to_all x1, starting transfers between devices, step(): back = lax.all_to_all(message, FSDP, 0, 0, tiled=True)  7.57 us
  transfers between devices with their start and end apart: 16, of which 6 were waited for; matrix products, arithmetic and copies ran while one was open for 0% of the time, Pallas kernels for 5%

profile of v6, /device:TPU:6, one launch (start us, length us, event | category | flops | bytes accessed | tf_op | source)
XLA Modules:
  0.0 192.2 jit_solution(13389431839239273627)
XLA Ops:
  0.6 1.3 copy.14
  1.9 1.3 copy.11
  3.2 10.4 %all-to-all-start = ((bf16[8,448,128]{2,1,0:T(8,128)(2,1)}), bf16[8,448,128]{2,1,0:T(8,128)(2,1)S(1)}, u32[]{:S(2)}, u32[]{:S(2)}) async-start(bf16[8,448,128]{2,1,0:T(8,128)(2,1)} %bitcast.1), calls=%async_computation | async-start | bytes 1835008 | tf_op jit(solution)/shard_map/all_to_all | solution.py:164
  13.7 0.1 select_reduce_fusion
  13.8 25.8 %all-to-all-done = bf16[8,448,128]{2,1,0:T(8,128)(2,1)S(1)} async-done(((bf16[8,448,128]{2,1,0:T(8,128)(2,1)}), bf16[8,448,128]{2,1,0:T(8,128)(2,1)S(1)}, u32[]{:S(2)}, u32[]{:S(2)}) %all-to-all-start) | async-done | bytes 917536 | tf_op jit(solution)/shard_map/all_to_all | solution.py:164
  39.6 0.1 reduce_sum.30
  39.7 0.6 gather_fusion
  40.4 22.1 %all_to_all.15 = bf16[64,16,128]{2,1,0:T(8,128)(2,1)S(1)} all-to-all(bf16[64,16,128]{2,1,0:T(8,128)(2,1)S(1)} %gather_fusion), channel_id=1, replica_groups=mesh['fsdp_0'=4,'fsdp_1'=8,'fsdp_2'=2,'dp'=8] {'fsdp_0','fsdp_1','fsdp_2'}, dimensions={0} | all-to-all | bytes 524288 | tf_op jit(solution)/shard_map/all_to_all | solution.py:181
  62.5 2.5 %collective-permute-start = (bf16[1024,128]{1,0:T(8,128)(2,1)S(1)}, bf16[1024,128]{1,0:T(8,128)(2,1)S(1)}, u32[]{:S(2)}, u32[]{:S(2)}) collective-permute-start(bf16[1024,128]{1,0:T(8,128)(2,1)S(1)} %bitcast.31), channel_id=1, source_target_pairs={{0,1},{1,2},{2,3},{3,4},{4,5},{5,6},{6,7},{7,0},{8,9},{9,10},{10,1... | collective-permute-start | bytes 786440 | tf_op jit(solution)/shard_map/ppermute | solution.py:21
  65.0 4.6 %collective-permute-start.1 = (bf16[1024,128]{1,0:T(8,128)(2,1)S(1)}, bf16[1024,128]{1,0:T(8,128)(2,1)S(1)}, u32[]{:S(2)}, u32[]{:S(2)}) collective-permute-start(bf16[1024,128]{1,0:T(8,128)(2,1)S(1)} %bitcast.32), channel_id=1, source_target_pairs={{0,7},{1,0},{2,1},{3,2},{4,3},{5,4},{6,5},{7,6},{8,15},{9,8},{10,9... | collective-permute-start | bytes 786440 | tf_op jit(solution)/shard_map/ppermute | solution.py:21
  69.6 4.4 %collective-permute-done.refs_1_ = bf16[1024,128]{1,0:T(8,128)(2,1)S(1)} collective-permute-done((bf16[1024,128]{1,0:T(8,128)(2,1)S(1)}, bf16[1024,128]{1,0:T(8,128)(2,1)S(1)}, u32[]{:S(2)}, u32[]{:S(2)}) %collective-permute-start) | collective-permute-done | bytes 262176 | tf_op jit(solution)/shard_map/ppermute | solution.py:21
  73.9 1.9 collective-permute-start.2
  75.9 2.2 %shard_map.86 = (bf16[96,1024]{1,0:T(8,128)(2,1)}, bf16[96,1024]{1,0:T(8,128)(2,1)}, bf16[96,1024]{1,0:T(8,128)(2,1)}, bf16[96,1024]{1,0:T(8,128)(2,1)}, bf16[96...) custom-call(bf16[128,1024]{1,0:T(8,128)(2,1)} %bitcast.39, ...), custom_call_target="tpu_custom_call" | custom-call | tf_op jit(solution)/shard_map/pallas_call | solution.py:166
  78.1 2.9 %collective-permute-start.10 = (bf16[96,1024]{1,0:T(8,128)(2,1)}, bf16[96,1024]{1,0:T(8,128)(2,1)S(1)}, u32[]{:S(2)}, u32[]{:S(2)}) collective-permute-start(bf16[96,1024]{1,0:T(8,128)(2,1)} %get-tuple-element.31), channel_id=1, source_target_pairs={{0,6},{1,7},{2,0},{3,1},{4,2},{5,3},{6,4},{7,5},{8,14},{9,15},{10,... | collective-permute-start | bytes 589832 | tf_op jit(solution)/shard_map/ppermute | solution.py:21
  81.0 0.0 collective-permute-done.1.refs_2_
  81.0 4.1 %collective-permute-start.3 = (bf16[1024,128]{1,0:T(8,128)(2,1)S(1)}, bf16[1024,128]{1,0:T(8,128)(2,1)S(1)}, u32[]{:S(2)}, u32[]{:S(2)}) collective-permute-start(bf16[1024,128]{1,0:T(8,128)(2,1)S(1)} %collective-permute-done.1.refs_2_), channel_id=1, source_target_pairs={{0,7},{1,0},{2,1},{3,2},{4,3},{5,4},{6,5},{7,6},{8,15},{9,8},{10,9... | collective-permute-start | bytes 786440 | tf_op jit(solution)/shard_map/ppermute | solution.py:21
  85.2 0.0 collective-permute-done.2.refs_3_
  85.2 3.4 %collective-permute-start.4 = (bf16[1024,128]{1,0:T(8,128)(2,1)S(1)}, bf16[1024,128]{1,0:T(8,128)(2,1)S(1)}, u32[]{:S(2)}, u32[]{:S(2)}) collective-permute-start(bf16[1024,128]{1,0:T(8,128)(2,1)S(1)} %collective-permute-done.2.refs_3_), channel_id=1, source_target_pairs={{0,1},{1,2},{2,3},{3,4},{4,5},{5,6},{6,7},{7,0},{8,9},{9,10},{10,1... | collective-permute-start | bytes 786440 | tf_op jit(solution)/shard_map/ppermute | solution.py:21
  88.6 2.6 %collective-permute-start.11 = (bf16[96,1024]{1,0:T(8,128)(2,1)}, bf16[96,1024]{1,0:T(8,128)(2,1)S(1)}, u32[]{:S(2)}, u32[]{:S(2)}) collective-permute-start(bf16[96,1024]{1,0:T(8,128)(2,1)} %get-tuple-element.32), channel_id=1, source_target_pairs={{0,3},{1,4},{2,5},{3,6},{4,7},{5,0},{6,1},{7,2},{8,11},{9,12},{10,... | collective-permute-start | bytes 589832 | tf_op jit(solution)/shard_map/ppermute | solution.py:21
  91.2 6.3 %collective-permute-start.12 = (bf16[96,1024]{1,0:T(8,128)(2,1)}, bf16[96,1024]{1,0:T(8,128)(2,1)S(1)}, u32[]{:S(2)}, u32[]{:S(2)}) collective-permute-start(bf16[96,1024]{1,0:T(8,128)(2,1)} %get-tuple-element.33), channel_id=1, source_target_pairs={{0,5},{1,6},{2,7},{3,0},{4,1},{5,2},{6,3},{7,4},{8,13},{9,14},{10,... | collective-permute-start | bytes 589832 | tf_op jit(solution)/shard_map/ppermute | solution.py:21
  97.4 0.0 collective-permute-done.10.refs_11_.refs_6_
  97.4 3.9 %collective-permute-start.7 = (bf16[96,1024]{1,0:T(8,128)(2,1)}, bf16[96,1024]{1,0:T(8,128)(2,1)S(1)}, u32[]{:S(2)}, u32[]{:S(2)}) collective-permute-start(bf16[96,1024]{1,0:T(8,128)(2,1)} %get-tuple-element.28), channel_id=1, source_target_pairs={{0,1},{1,2},{2,3},{3,4},{4,5},{5,6},{6,7},{7,0},{8,9},{9,10},{10,1... | collective-permute-start | bytes 589832 | tf_op jit(solution)/shard_map/ppermute | solution.py:21
  101.4 0.1 collective-permute-done.3.refs_4_
  101.5 3.0 %collective-permute-start.5 = (bf16[1024,128]{1,0:T(8,128)(2,1)S(1)}, bf16[1024,128]{1,0:T(8,128)(2,1)S(1)}, u32[]{:S(2)}, u32[]{:S(2)}) collective-permute-start(bf16[1024,128]{1,0:T(8,128)(2,1)S(1)} %collective-permute-done.3.refs_4_), channel_id=1, source_target_pairs={{0,7},{1,0},{2,1},{3,2},{4,3},{5,4},{6,5},{7,6},{8,15},{9,8},{10,9... | collective-permute-start | bytes 786440 | tf_op jit(solution)/shard_map/ppermute | solution.py:21
  104.6 2.8 %collective-permute-start.6 = (bf16[1024,128]{1,0:T(8,128)(2,1)S(1)}, bf16[1024,128]{1,0:T(8,128)(2,1)S(1)}, u32[]{:S(2)}, u32[]{:S(2)}) collective-permute-start(bf16[1024,128]{1,0:T(8,128)(2,1)S(1)} %collective-permute-done.4.refs_5_), channel_id=1, source_target_pairs={{0,1},{1,2},{2,3},{3,4},{4,5},{5,6},{6,7},{7,0},{8,9},{9,10},{10,1... | collective-permute-start | bytes 786440 | tf_op jit(solution)/shard_map/ppermute | solution.py:21
  107.3 0.4 collective-permute-done.11.refs_12_.refs_7_
  107.7 3.9 %collective-permute-start.8 = (bf16[96,1024]{1,0:T(8,128)(2,1)}, bf16[96,1024]{1,0:T(8,128)(2,1)S(1)}, u32[]{:S(2)}, u32[]{:S(2)}) collective-permute-start(bf16[96,1024]{1,0:T(8,128)(2,1)} %get-tuple-element.29), channel_id=1, source_target_pairs={{0,7},{1,0},{2,1},{3,2},{4,3},{5,4},{6,5},{7,6},{8,15},{9,8},{10,9... | collective-permute-start | bytes 589832 | tf_op jit(solution)/shard_map/ppermute | solution.py:21
  111.6 0.0 collective-permute-done.12.refs_13_.refs_8_
  111.7 3.8 %collective-permute-start.9 = (bf16[96,1024]{1,0:T(8,128)(2,1)}, bf16[96,1024]{1,0:T(8,128)(2,1)S(1)}, u32[]{:S(2)}, u32[]{:S(2)}) collective-permute-start(bf16[96,1024]{1,0:T(8,128)(2,1)} %get-tuple-element.30), channel_id=1, source_target_pairs={{0,2},{1,3},{2,4},{3,5},{4,6},{5,7},{6,0},{7,1},{8,10},{9,11},{10,... | collective-permute-start | bytes 589832 | tf_op jit(solution)/shard_map/ppermute | solution.py:21
  115.5 0.0 collective-permute-done.7.refs_8_.refs_3_
  115.5 0.0 copy-start.11
  115.5 5.7 %collective-permute-start.13 = (bf16[96,1024]{1,0:T(8,128)(2,1)}, bf16[96,1024]{1,0:T(8,128)(2,1)S(1)}, u32[]{:S(2)}, u32[]{:S(2)}) collective-permute-start(bf16[96,1024]{1,0:T(8,128)(2,1)} %get-tuple-element.34), channel_id=1, source_target_pairs={{0,4},{1,5},{2,6},{3,7},{4,0},{5,1},{6,2},{7,3},{8,12},{9,13},{10,... | collective-permute-start | bytes 589832 | tf_op jit(solution)/shard_map/ppermute | solution.py:21
  121.2 5.7 %collective-permute-done.9.refs_10_.refs_5_ = bf16[96,1024]{1,0:T(8,128)(2,1)S(1)} collective-permute-done((bf16[96,1024]{1,0:T(8,128)(2,1)}, bf16[96,1024]{1,0:T(8,128)(2,1)S(1)}, u32[]{:S(2)}, u32[]{:S(2)}) %collective-permute-start.9) | collective-permute-done | bytes 196640 | tf_op jit(solution)/shard_map/ppermute | solution.py:21
  127.0 0.6 copy-done.13
  127.6 0.1 copy-done.6
  127.7 4.0 %shard_map.87.refs_0_ = f32[1024,256]{1,0:T(8,128)} custom-call(bf16[1024,128]{1,0:T(8,128)(2,1)} %bitcast.33, bf16[1024,128]{1,0:T(8,128)(2,1)} %copy-done.1, bf16[1024,128]{1,0:T(8,128)(2,1)} %copy-done.2, bf16[1024,128]{1,0:T(8,128)(2,1)} %copy-done.3, bf16[1024,128]{1,0:T(8,128)(2,1)} %copy-done.4, bf16[1024,128]{1,0:T(8,128)(2,1)} %copy-done.5, ...), custom_call_target="tpu_custom_call" | custom-call | tf_op jit(solution)/shard_map/pallas_call | solution.py:187
  131.7 0.7 copy-done.14
  132.4 0.7 copy-done.7
  133.1 3.6 %shard_map.88 = bf16[64,24,128]{2,1,0:T(8,128)(2,1)} custom-call(f32[1024,256]{1,0:T(8,128)} %shard_map.87.refs_0_, bf16[1024,128]{1,0:T(8,128)(2,1)} %copy-done.7, bf16[96,1024]{1,0:T(8,128)(2,1)} %get-tuple-element.27.refs_7_.refs_2_, bf16[96,1024]{1,0:T(8,128)(2,1)} %copy-done.11, bf16[96,1024]{1,0:T(8,128)(2,1)} %copy-done.12, ...), custom_call_target="tpu_custom_call" | custom-call | tf_op jit(solution)/shard_map/pallas_call | solution.py:198
  136.8 7.6 %all-to-all-start.2 = ((bf16[64,24,128]{2,1,0:T(8,128)(2,1)}), bf16[64,24,128]{2,1,0:T(8,128)(2,1)S(1)}, u32[]{:S(2)}, u32[]{:S(2)}) async-start(bf16[64,24,128]{2,1,0:T(8,128)(2,1)} %shard_map.88), calls=%async_computation.2 | async-start | bytes 786432 | tf_op jit(solution)/shard_map/all_to_all | solution.py:211
  144.3 4.0 %shard_map.85 = (f32[1,128,1024]{2,1,0:T(8,128)}, f32[1,128,1024]{2,1,0:T(8,128)}) custom-call(bf16[1024,128]{1,0:T(8,128)(2,1)} %bitcast.34, bf16[1024,128]{1,0:T(8,128)(2,1)} %copy-done.1, bf16[1024,128]{1,0:T(8,128)(2,1)} %copy-done.2, bf16[1024,128]{1,0:T(8,128)(2,1)} %copy-done.3, bf16[1024,128]{1,0:T(8,128)(2,1)} %copy-done.4, ...), custom_call_target="tpu_custom_call" | custom-call | tf_op jit(solution)/shard_map/pallas_call | solution.py:213
  148.4 10.1 %all-to-all-done.2 = bf16[64,24,128]{2,1,0:T(8,128)(2,1)S(1)} async-done(((bf16[64,24,128]{2,1,0:T(8,128)(2,1)}), bf16[64,24,128]{2,1,0:T(8,128)(2,1)S(1)}, u32[]{:S(2)}, u32[]{:S(2)}) %all-to-all-start.2) | async-done | bytes 393248 | tf_op jit(solution)/shard_map/all_to_all | solution.py:211
  158.4 0.6 gather_fusion.1
  159.1 31.4 %all-gather = bf16[3840,128]{1,0:T(8,128)(2,1)S(1)} all-gather(bf16[480,128]{1,0:T(8,128)(2,1)S(1)} %fusion.3), channel_id=2, replica_groups=mesh['fsdp_0'=4,'fsdp_1'=8,'fsdp_2'=2,'dp'=8] {'dp'}, dimensions={0}, use_global_device_ids=true | all-gather | bytes 1105920 | tf_op jit(solution)/shard_map/all_gather | solution.py:223
  190.5 0.1 slice.40
  190.6 0.1 convert_reduce_fusion
  190.7 0.3 fusion.1
  191.0 1.2 copy.12
  (43 shorter events, 0.2 us)
Async XLA Ops:
  3.2 10.5 %copy-start.15 = (s32[28]{0:T(128)S(1)}, s32[28]{0:T(128)}, u32[]{:S(2)}) copy-start(s32[28]{0:T(128)} %param.9) | copy-start | bytes 340
  3.2 36.4 %all-to-all-start = ((bf16[8,448,128]{2,1,0:T(8,128)(2,1)}), bf16[8,448,128]{2,1,0:T(8,128)(2,1)S(1)}, u32[]{:S(2)}, u32[]{:S(2)}) async-start(bf16[8,448,128]{2,1,0:T(8,128)(2,1)} %bitcast.1), calls=%async_computation | async-start | bytes 1835008 | tf_op jit(solution)/shard_map/all_to_all | solution.py:164
  62.5 64.4 %copy-start = (bf16[64,16,128]{2,1,0:T(8,128)(2,1)}, bf16[64,16,128]{2,1,0:T(8,128)(2,1)S(1)}, u32[]{:S(2)}) copy-start(bf16[64,16,128]{2,1,0:T(8,128)(2,1)S(1)} %all_to_all.15) | copy-start | bytes 786436
  62.5 11.4 %collective-permute-start = (bf16[1024,128]{1,0:T(8,128)(2,1)S(1)}, bf16[1024,128]{1,0:T(8,128)(2,1)S(1)}, u32[]{:S(2)}, u32[]{:S(2)}) collective-permute-start(bf16[1024,128]{1,0:T(8,128)(2,1)S(1)} %bitcast.31), channel_id=1, source_target_pairs={{0,1},{1,2},{2,3},{3,4},{4,5},{5,6},{6,7},{7,0},{8,9},{9,10},{10,1... | collective-permute-start | bytes 786440 | tf_op jit(solution)/shard_map/ppermute | solution.py:21
  65.0 16.0 %collective-permute-start.1 = (bf16[1024,128]{1,0:T(8,128)(2,1)S(1)}, bf16[1024,128]{1,0:T(8,128)(2,1)S(1)}, u32[]{:S(2)}, u32[]{:S(2)}) collective-permute-start(bf16[1024,128]{1,0:T(8,128)(2,1)S(1)} %bitcast.32), channel_id=1, source_target_pairs={{0,7},{1,0},{2,1},{3,2},{4,3},{5,4},{6,5},{7,6},{8,15},{9,8},{10,9... | collective-permute-start | bytes 786440 | tf_op jit(solution)/shard_map/ppermute | solution.py:21
  73.9 53.0 %copy-start.1 = (bf16[1024,128]{1,0:T(8,128)(2,1)}, bf16[1024,128]{1,0:T(8,128)(2,1)S(1)}, u32[]{:S(2)}) copy-start(bf16[1024,128]{1,0:T(8,128)(2,1)S(1)} %collective-permute-done.refs_1_) | copy-start | bytes 786436
  73.9 11.2 %collective-permute-start.2 = (bf16[1024,128]{1,0:T(8,128)(2,1)S(1)}, bf16[1024,128]{1,0:T(8,128)(2,1)S(1)}, u32[]{:S(2)}, u32[]{:S(2)}) collective-permute-start(bf16[1024,128]{1,0:T(8,128)(2,1)S(1)} %collective-permute-done.refs_1_), channel_id=1, source_target_pairs={{0,1},{1,2},{2,3},{3,4},{4,5},{5,6},{6,7},{7,0},{8,9},{9,10},{10,1... | collective-permute-start | bytes 786440 | tf_op jit(solution)/shard_map/ppermute | solution.py:21
  78.1 19.3 %collective-permute-start.10 = (bf16[96,1024]{1,0:T(8,128)(2,1)}, bf16[96,1024]{1,0:T(8,128)(2,1)S(1)}, u32[]{:S(2)}, u32[]{:S(2)}) collective-permute-start(bf16[96,1024]{1,0:T(8,128)(2,1)} %get-tuple-element.31), channel_id=1, source_target_pairs={{0,6},{1,7},{2,0},{3,1},{4,2},{5,3},{6,4},{7,5},{8,14},{9,15},{10,... | collective-permute-start | bytes 589832 | tf_op jit(solution)/shard_map/ppermute | solution.py:21
  81.0 46.0 %copy-start.2 = (bf16[1024,128]{1,0:T(8,128)(2,1)}, bf16[1024,128]{1,0:T(8,128)(2,1)S(1)}, u32[]{:S(2)}) copy-start(bf16[1024,128]{1,0:T(8,128)(2,1)S(1)} %collective-permute-done.1.refs_2_) | copy-start | bytes 786436
  81.0 20.5 %collective-permute-start.3 = (bf16[1024,128]{1,0:T(8,128)(2,1)S(1)}, bf16[1024,128]{1,0:T(8,128)(2,1)S(1)}, u32[]{:S(2)}, u32[]{:S(2)}) collective-permute-start(bf16[1024,128]{1,0:T(8,128)(2,1)S(1)} %collective-permute-done.1.refs_2_), channel_id=1, source_target_pairs={{0,7},{1,0},{2,1},{3,2},{4,3},{5,4},{6,5},{7,6},{8,15},{9,8},{10,9... | collective-permute-start | bytes 786440 | tf_op jit(solution)/shard_map/ppermute | solution.py:21
  85.2 41.8 %copy-start.3 = (bf16[1024,128]{1,0:T(8,128)(2,1)}, bf16[1024,128]{1,0:T(8,128)(2,1)S(1)}, u32[]{:S(2)}) copy-start(bf16[1024,128]{1,0:T(8,128)(2,1)S(1)} %collective-permute-done.2.refs_3_) | copy-start | bytes 786436
  85.2 19.4 %collective-permute-start.4 = (bf16[1024,128]{1,0:T(8,128)(2,1)S(1)}, bf16[1024,128]{1,0:T(8,128)(2,1)S(1)}, u32[]{:S(2)}, u32[]{:S(2)}) collective-permute-start(bf16[1024,128]{1,0:T(8,128)(2,1)S(1)} %collective-permute-done.2.refs_3_), channel_id=1, source_target_pairs={{0,1},{1,2},{2,3},{3,4},{4,5},{5,6},{6,7},{7,0},{8,9},{9,10},{10,1... | collective-permute-start | bytes 786440 | tf_op jit(solution)/shard_map/ppermute | solution.py:21
  88.6 19.2 %collective-permute-start.11 = (bf16[96,1024]{1,0:T(8,128)(2,1)}, bf16[96,1024]{1,0:T(8,128)(2,1)S(1)}, u32[]{:S(2)}, u32[]{:S(2)}) collective-permute-start(bf16[96,1024]{1,0:T(8,128)(2,1)} %get-tuple-element.32), channel_id=1, source_target_pairs={{0,3},{1,4},{2,5},{3,6},{4,7},{5,0},{6,1},{7,2},{8,11},{9,12},{10,... | collective-permute-start | bytes 589832 | tf_op jit(solution)/shard_map/ppermute | solution.py:21
  91.2 20.5 %collective-permute-start.12 = (bf16[96,1024]{1,0:T(8,128)(2,1)}, bf16[96,1024]{1,0:T(8,128)(2,1)S(1)}, u32[]{:S(2)}, u32[]{:S(2)}) collective-permute-start(bf16[96,1024]{1,0:T(8,128)(2,1)} %get-tuple-element.33), channel_id=1, source_target_pairs={{0,5},{1,6},{2,7},{3,0},{4,1},{5,2},{6,3},{7,4},{8,13},{9,14},{10,... | collective-permute-start | bytes 589832 | tf_op jit(solution)/shard_map/ppermute | solution.py:21
  97.4 29.5 %copy-start.8 = (bf16[96,1024]{1,0:T(8,128)(2,1)}, bf16[96,1024]{1,0:T(8,128)(2,1)S(1)}, u32[]{:S(2)}) copy-start(bf16[96,1024]{1,0:T(8,128)(2,1)S(1)} %collective-permute-done.10.refs_11_.refs_6_) | copy-start | bytes 589828
  97.4 18.0 %collective-permute-start.7 = (bf16[96,1024]{1,0:T(8,128)(2,1)}, bf16[96,1024]{1,0:T(8,128)(2,1)S(1)}, u32[]{:S(2)}, u32[]{:S(2)}) collective-permute-start(bf16[96,1024]{1,0:T(8,128)(2,1)} %get-tuple-element.28), channel_id=1, source_target_pairs={{0,1},{1,2},{2,3},{3,4},{4,5},{5,6},{6,7},{7,0},{8,9},{9,10},{10,1... | collective-permute-start | bytes 589832 | tf_op jit(solution)/shard_map/ppermute | solution.py:21
  101.5 25.5 %copy-start.4 = (bf16[1024,128]{1,0:T(8,128)(2,1)}, bf16[1024,128]{1,0:T(8,128)(2,1)S(1)}, u32[]{:S(2)}) copy-start(bf16[1024,128]{1,0:T(8,128)(2,1)S(1)} %collective-permute-done.3.refs_4_) | copy-start | bytes 786436
  101.5 25.4 %collective-permute-start.5 = (bf16[1024,128]{1,0:T(8,128)(2,1)S(1)}, bf16[1024,128]{1,0:T(8,128)(2,1)S(1)}, u32[]{:S(2)}, u32[]{:S(2)}) collective-permute-start(bf16[1024,128]{1,0:T(8,128)(2,1)S(1)} %collective-permute-done.3.refs_4_), channel_id=1, source_target_pairs={{0,7},{1,0},{2,1},{3,2},{4,3},{5,4},{6,5},{7,6},{8,15},{9,8},{10,9... | collective-permute-start | bytes 786440 | tf_op jit(solution)/shard_map/ppermute | solution.py:21
  104.5 22.4 %copy-start.5 = (bf16[1024,128]{1,0:T(8,128)(2,1)}, bf16[1024,128]{1,0:T(8,128)(2,1)S(1)}, u32[]{:S(2)}) copy-start(bf16[1024,128]{1,0:T(8,128)(2,1)S(1)} %collective-permute-done.4.refs_5_) | copy-start | bytes 786436
  104.6 27.2 %collective-permute-start.6 = (bf16[1024,128]{1,0:T(8,128)(2,1)S(1)}, bf16[1024,128]{1,0:T(8,128)(2,1)S(1)}, u32[]{:S(2)}, u32[]{:S(2)}) collective-permute-start(bf16[1024,128]{1,0:T(8,128)(2,1)S(1)} %collective-permute-done.4.refs_5_), channel_id=1, source_target_pairs={{0,1},{1,2},{2,3},{3,4},{4,5},{5,6},{6,7},{7,0},{8,9},{9,10},{10,1... | collective-permute-start | bytes 786440 | tf_op jit(solution)/shard_map/ppermute | solution.py:21
  107.7 19.3 %copy-start.9 = (bf16[96,1024]{1,0:T(8,128)(2,1)}, bf16[96,1024]{1,0:T(8,128)(2,1)S(1)}, u32[]{:S(2)}) copy-start(bf16[96,1024]{1,0:T(8,128)(2,1)S(1)} %collective-permute-done.11.refs_12_.refs_7_) | copy-start | bytes 589828
  107.7 13.5 %collective-permute-start.8 = (bf16[96,1024]{1,0:T(8,128)(2,1)}, bf16[96,1024]{1,0:T(8,128)(2,1)S(1)}, u32[]{:S(2)}, u32[]{:S(2)}) collective-permute-start(bf16[96,1024]{1,0:T(8,128)(2,1)} %get-tuple-element.29), channel_id=1, source_target_pairs={{0,7},{1,0},{2,1},{3,2},{4,3},{5,4},{6,5},{7,6},{8,15},{9,8},{10,9... | collective-permute-start | bytes 589832 | tf_op jit(solution)/shard_map/ppermute | solution.py:21
  111.7 15.4 %copy-start.10 = (bf16[96,1024]{1,0:T(8,128)(2,1)}, bf16[96,1024]{1,0:T(8,128)(2,1)S(1)}, u32[]{:S(2)}) copy-start(bf16[96,1024]{1,0:T(8,128)(2,1)S(1)} %collective-permute-done.12.refs_13_.refs_8_) | copy-start | bytes 589828
  111.7 15.3 %collective-permute-start.9 = (bf16[96,1024]{1,0:T(8,128)(2,1)}, bf16[96,1024]{1,0:T(8,128)(2,1)S(1)}, u32[]{:S(2)}, u32[]{:S(2)}) collective-permute-start(bf16[96,1024]{1,0:T(8,128)(2,1)} %get-tuple-element.30), channel_id=1, source_target_pairs={{0,2},{1,3},{2,4},{3,5},{4,6},{5,7},{6,0},{7,1},{8,10},{9,11},{10,... | collective-permute-start | bytes 589832 | tf_op jit(solution)/shard_map/ppermute | solution.py:21
  115.5 11.5 %copy-start.11 = (bf16[96,1024]{1,0:T(8,128)(2,1)}, bf16[96,1024]{1,0:T(8,128)(2,1)S(1)}, u32[]{:S(2)}) copy-start(bf16[96,1024]{1,0:T(8,128)(2,1)S(1)} %collective-permute-done.7.refs_8_.refs_3_) | copy-start | bytes 589828
  115.5 16.2 %collective-permute-start.13 = (bf16[96,1024]{1,0:T(8,128)(2,1)}, bf16[96,1024]{1,0:T(8,128)(2,1)S(1)}, u32[]{:S(2)}, u32[]{:S(2)}) collective-permute-start(bf16[96,1024]{1,0:T(8,128)(2,1)} %get-tuple-element.34), channel_id=1, source_target_pairs={{0,4},{1,5},{2,6},{3,7},{4,0},{5,1},{6,2},{7,3},{8,12},{9,13},{10,... | collective-permute-start | bytes 589832 | tf_op jit(solution)/shard_map/ppermute | solution.py:21
  121.2 5.8 %copy-start.12 = (bf16[96,1024]{1,0:T(8,128)(2,1)}, bf16[96,1024]{1,0:T(8,128)(2,1)S(1)}, u32[]{:S(2)}) copy-start(bf16[96,1024]{1,0:T(8,128)(2,1)S(1)} %collective-permute-done.8.refs_9_.refs_4_) | copy-start | bytes 589828
  126.9 0.7 copy-start.13
  126.9 0.8 copy-start.6
  131.7 0.7 copy-start.14
  132.4 0.7 copy-start.7
  136.8 21.7 %all-to-all-start.2 = ((bf16[64,24,128]{2,1,0:T(8,128)(2,1)}), bf16[64,24,128]{2,1,0:T(8,128)(2,1)S(1)}, u32[]{:S(2)}, u32[]{:S(2)}) async-start(bf16[64,24,128]{2,1,0:T(8,128)(2,1)} %shard_map.88), calls=%async_computation.2 | async-start | bytes 786432 | tf_op jit(solution)/shard_map/all_to_all | solution.py:211

commit v7 on v6

--- a/solution.py
+++ b/solution.py
@@ -23,7 +23,8 @@
 
 def offsets(count):
     half = count // 2
-    return [0] + [sign * s for s in range(1, half) for sign in (-1, 1)] + [half]
+    near = [sign * s for s in range(1, half) for sign in (-1, 1)]
+    return [0] + near[1:] + [near[0], half]
 
 
 def ring_gather(array, axis):
@@ -35,7 +36,7 @@
         down = ring(down, axis, -1)
         shards += [up, down]
     shards.append(ring(up, axis, 1))
-    return shards
+    return shards[:1] + shards[2:-1] + [shards[1], shards[-1]]
 
 
 def dot(a, b, dims=((1,), (0,))):
@@ -89,28 +90,30 @@
 
 
 def precondition_kernel(count, *refs):
-    inner_in, shard_in, sources = refs[0], refs[1], refs[2 : 2 + count]
-    out, inner_buffer, shard_buffer, root_buffer, left, arrived = refs[2 + count :]
+    inner_in, shards_in, sources = refs[0], refs[1:3], refs[3 : 3 + count]
+    out, inner_buffer, shard_buffer, root_buffer, left, arrived = refs[3 + count :]
     half = left.shape[0] // count
+    late = list(zip(shards_in, [shard_buffer.at[i] for i in range(2)]))
+    late += zip(sources[-2:], [root_buffer.at[i] for i in range(2)])
+    late += [(inner_in, inner_buffer)]
+    lefts = [(sources[i].at[:half], left.at[i * half : (i + 1) * half]) for i in range(count)]
     copies = [
-        pltpu.make_async_copy(shard_in, shard_buffer, arrived.at[0]),
-        pltpu.make_async_copy(sources[-1], root_buffer, arrived.at[1]),
-        pltpu.make_async_copy(inner_in, inner_buffer, arrived.at[2]),
+        pltpu.make_async_copy(source, target, arrived.at[i])
+        for i, (source, target) in enumerate(late + lefts)
     ]
-    for i in range(count):
-        rows = left.at[i * half : (i + 1) * half]
-        copies.append(pltpu.make_async_copy(sources[i].at[:half], rows, arrived.at[3 + i]))
     for copy in copies:
         copy.start()
-    for copy in copies[:3]:
+    for copy in copies[:5]:
         copy.wait()
     me = lax.axis_index("dp")
-    width = shard_buffer.shape[1]
-    last = dot(shard_buffer[...], jnp.concatenate(right_rows(root_buffer), axis=0))
+    width = shard_buffer.shape[2]
+    pair = jnp.concatenate([shard_buffer[i] for i in range(2)], axis=1)
+    rights = [r for i in range(2) for r in right_rows(root_buffer.at[i])]
+    last = dot(pair, jnp.concatenate(rights, axis=0))
     inner = inner_buffer[...] + last
     high = inner.astype(jnp.bfloat16)
     low = (inner - high.astype(jnp.float32)).astype(jnp.bfloat16)
-    for copy in copies[3:]:
+    for copy in copies[5:]:
         copy.wait()
     both = dot(left[...], high) + dot(left[...], low)
     total = jnp.sum(jnp.sum(both * both, axis=0, keepdims=True), axis=1, keepdims=True)
@@ -182,7 +185,7 @@
     shards = ring_gather(incoming.reshape(block_size, shared), "dp")
 
     anywhere = pl.BlockSpec(memory_space=pl.ANY)
-    before = replicas - 1
+    before = replicas - 2
     quarter = block_size // quarters
     inner = pl.pallas_call(
         functools.partial(inner_kernel, before),
@@ -194,20 +197,20 @@
             pltpu.VMEM((before,) + roots[0].shape, jnp.bfloat16),
             pltpu.SemaphoreType.DMA((2 * before,)),
         ],
-    )(*shards[:-1], *roots[:-1])
+    )(*shards[:before], *roots[:before])
     message = pl.pallas_call(
         functools.partial(precondition_kernel, replicas),
         out_shape=jax.ShapeDtypeStruct((total_slots, row_dev + 8, shared), jnp.bfloat16),
-        in_specs=[anywhere] * (2 + replicas),
+        in_specs=[anywhere] * (3 + replicas),
         out_specs=VMEM,
         scratch_shapes=[
             pltpu.VMEM(inner.shape, jnp.float32),
-            pltpu.VMEM(shards[0].shape, jnp.bfloat16),
-            pltpu.VMEM(roots[0].shape, jnp.bfloat16),
+            pltpu.VMEM((2,) + shards[0].shape, jnp.bfloat16),
+            pltpu.VMEM((2,) + roots[0].shape, jnp.bfloat16),
             pltpu.VMEM((block_size // 2, block_size), jnp.bfloat16),
-            pltpu.SemaphoreType.DMA((3 + replicas,)),
+            pltpu.SemaphoreType.DMA((5 + replicas,)),
         ],
-    )(inner, shards[-1], *roots)
+    )(inner, *shards[before:], *roots)
     back = lax.all_to_all(message, FSDP, 0, 0, tiled=True)
 
     left_new, right_new = pl.pallas_call(

time: 193 us -> 193 us (level)
  the two profiles are of different devices: /device:TPU:6 before, /device:TPU:8 now
where the time goes in v7:
time: 193 us; the launch traced here: 192 us
  starting transfers between devices  63.1 us (33%)
  waiting for transfers between devices  56 us (29%)
  blocking collectives  50.1 us (26%)
  Pallas kernels  13.6 us (7%)
  local copies, waits for them, and re-layouts  7.26 us (4%)
    ppermute x14, starting transfers between devices, ring(): lax.ppermute(array, axis, [(i, (i + step) % count) for i in range(count)])  46.6 us
    all_gather x1, blocking collectives, step(): lax.all_gather(jnp.concatenate([tiles, terms]), 'dp', axis=0, tiled=False)  28 us
    all_to_all x1, waiting for transfers between devices, step(): received = lax.all_to_all(shares, 'dp', 0, 0, tiled=True)  25.8 us
    all_to_all x1, blocking collectives, step(): incoming = lax.all_to_all(outgoing, FSDP, 0, 0, tiled=True)  22.1 us
    ppermute x14, waiting for transfers between devices, ring(): lax.ppermute(array, axis, [(i, (i + step) % count) for i in range(count)])  19.9 us
    all_to_all x1, starting transfers between devices, step(): received = lax.all_to_all(shares, 'dp', 0, 0, tiled=True)  10.4 us
    all_to_all x1, waiting for transfers between devices, step(): back = lax.all_to_all(message, FSDP, 0, 0, tiled=True)  10.4 us
    all_to_all x1, starting transfers between devices, step(): back = lax.all_to_all(message, FSDP, 0, 0, tiled=True)  6.07 us
  transfers between devices with their start and end apart: 16, of which 6 were waited for; matrix products, arithmetic and copies ran while one was open for 0% of the time, Pallas kernels for 5%

profile of v7, /device:TPU:8, one launch (start us, length us, event | category | flops | bytes accessed | tf_op | source)
XLA Modules:
  0.0 191.9 jit_solution(632370637484417495)
XLA Ops:
  0.6 1.3 copy.14
  1.9 1.3 copy.11
  3.2 10.4 %all-to-all-start = ((bf16[8,448,128]{2,1,0:T(8,128)(2,1)}), bf16[8,448,128]{2,1,0:T(8,128)(2,1)S(1)}, u32[]{:S(2)}, u32[]{:S(2)}) async-start(bf16[8,448,128]{2,1,0:T(8,128)(2,1)} %bitcast.1), calls=%async_computation | async-start | bytes 1835008 | tf_op jit(solution)/shard_map/all_to_all | solution.py:167
  13.7 0.1 select_reduce_fusion
  13.8 25.8 %all-to-all-done = bf16[8,448,128]{2,1,0:T(8,128)(2,1)S(1)} async-done(((bf16[8,448,128]{2,1,0:T(8,128)(2,1)}), bf16[8,448,128]{2,1,0:T(8,128)(2,1)S(1)}, u32[]{:S(2)}, u32[]{:S(2)}) %all-to-all-start) | async-done | bytes 917536 | tf_op jit(solution)/shard_map/all_to_all | solution.py:167
  39.6 0.1 reduce_sum.30
  39.7 0.6 gather_fusion
  40.4 22.1 %all_to_all.15 = bf16[64,16,128]{2,1,0:T(8,128)(2,1)S(1)} all-to-all(bf16[64,16,128]{2,1,0:T(8,128)(2,1)S(1)} %gather_fusion), channel_id=1, replica_groups=mesh['fsdp_0'=4,'fsdp_1'=8,'fsdp_2'=2,'dp'=8] {'fsdp_0','fsdp_1','fsdp_2'}, dimensions={0} | all-to-all | bytes 524288 | tf_op jit(solution)/shard_map/all_to_all | solution.py:184
  62.5 2.5 %collective-permute-start.1 = (bf16[1024,128]{1,0:T(8,128)(2,1)S(1)}, bf16[1024,128]{1,0:T(8,128)(2,1)S(1)}, u32[]{:S(2)}, u32[]{:S(2)}) collective-permute-start(bf16[1024,128]{1,0:T(8,128)(2,1)S(1)} %bitcast.31), channel_id=1, source_target_pairs={{0,1},{1,2},{2,3},{3,4},{4,5},{5,6},{6,7},{7,0},{8,9},{9,10},{10,1... | collective-permute-start | bytes 786440 | tf_op jit(solution)/shard_map/ppermute | solution.py:21
  64.9 4.6 %collective-permute-start = (bf16[1024,128]{1,0:T(8,128)(2,1)S(1)}, bf16[1024,128]{1,0:T(8,128)(2,1)S(1)}, u32[]{:S(2)}, u32[]{:S(2)}) collective-permute-start(bf16[1024,128]{1,0:T(8,128)(2,1)S(1)} %bitcast.32), channel_id=1, source_target_pairs={{0,7},{1,0},{2,1},{3,2},{4,3},{5,4},{6,5},{7,6},{8,15},{9,8},{10,9... | collective-permute-start | bytes 786440 | tf_op jit(solution)/shard_map/ppermute | solution.py:21
  69.5 4.4 %collective-permute-done.1.refs_6_.refs_1_ = bf16[1024,128]{1,0:T(8,128)(2,1)S(1)} collective-permute-done((bf16[1024,128]{1,0:T(8,128)(2,1)S(1)}, bf16[1024,128]{1,0:T(8,128)(2,1)S(1)}, u32[]{:S(2)}, u32[]{:S(2)}) %collective-permute-start.1) | collective-permute-done | bytes 262176 | tf_op jit(solution)/shard_map/ppermute | solution.py:21
  73.9 1.9 collective-permute-start.2
  75.8 2.2 %shard_map.86 = (bf16[96,1024]{1,0:T(8,128)(2,1)}, bf16[96,1024]{1,0:T(8,128)(2,1)}, bf16[96,1024]{1,0:T(8,128)(2,1)}, bf16[96,1024]{1,0:T(8,128)(2,1)}, bf16[96...) custom-call(bf16[128,1024]{1,0:T(8,128)(2,1)} %bitcast.39, ...), custom_call_target="tpu_custom_call" | custom-call | tf_op jit(solution)/shard_map/pallas_call | solution.py:169
  78.0 3.0 %collective-permute-start.10 = (bf16[96,1024]{1,0:T(8,128)(2,1)}, bf16[96,1024]{1,0:T(8,128)(2,1)S(1)}, u32[]{:S(2)}, u32[]{:S(2)}) collective-permute-start(bf16[96,1024]{1,0:T(8,128)(2,1)} %get-tuple-element.31), channel_id=1, source_target_pairs={{0,3},{1,4},{2,5},{3,6},{4,7},{5,0},{6,1},{7,2},{8,11},{9,12},{10,... | collective-permute-start | bytes 589832 | tf_op jit(solution)/shard_map/ppermute | solution.py:21
  81.1 4.0 %collective-permute-start.3 = (bf16[1024,128]{1,0:T(8,128)(2,1)S(1)}, bf16[1024,128]{1,0:T(8,128)(2,1)S(1)}, u32[]{:S(2)}, u32[]{:S(2)}) collective-permute-start(bf16[1024,128]{1,0:T(8,128)(2,1)S(1)} %collective-permute-done.refs_1_), channel_id=1, source_target_pairs={{0,7},{1,0},{2,1},{3,2},{4,3},{5,4},{6,5},{7,6},{8,15},{9,8},{10,9... | collective-permute-start | bytes 786440 | tf_op jit(solution)/shard_map/ppermute | solution.py:21
  85.1 4.9 %collective-permute-done.2.refs_2_ = bf16[1024,128]{1,0:T(8,128)(2,1)S(1)} collective-permute-done((bf16[1024,128]{1,0:T(8,128)(2,1)S(1)}, bf16[1024,128]{1,0:T(8,128)(2,1)S(1)}, u32[]{:S(2)}, u32[]{:S(2)}) %collective-permute-start.2) | collective-permute-done | bytes 262176 | tf_op jit(solution)/shard_map/ppermute | solution.py:21
  90.0 1.9 collective-permute-start.4
  91.9 1.9 %collective-permute-start.11 = (bf16[96,1024]{1,0:T(8,128)(2,1)}, bf16[96,1024]{1,0:T(8,128)(2,1)S(1)}, u32[]{:S(2)}, u32[]{:S(2)}) collective-permute-start(bf16[96,1024]{1,0:T(8,128)(2,1)} %get-tuple-element.32), channel_id=1, source_target_pairs={{0,5},{1,6},{2,7},{3,0},{4,1},{5,2},{6,3},{7,4},{8,13},{9,14},{10,... | collective-permute-start | bytes 589832 | tf_op jit(solution)/shard_map/ppermute | solution.py:21
  93.8 5.1 %collective-permute-start.7 = (bf16[96,1024]{1,0:T(8,128)(2,1)}, bf16[96,1024]{1,0:T(8,128)(2,1)S(1)}, u32[]{:S(2)}, u32[]{:S(2)}) collective-permute-start(bf16[96,1024]{1,0:T(8,128)(2,1)} %get-tuple-element.28), channel_id=1, source_target_pairs={{0,7},{1,0},{2,1},{3,2},{4,3},{5,4},{6,5},{7,6},{8,15},{9,8},{10,9... | collective-permute-start | bytes 589832 | tf_op jit(solution)/shard_map/ppermute | solution.py:21
  99.0 0.0 collective-permute-done.10.refs_10_.refs_7_
  99.0 4.3 %collective-permute-start.8 = (bf16[96,1024]{1,0:T(8,128)(2,1)}, bf16[96,1024]{1,0:T(8,128)(2,1)S(1)}, u32[]{:S(2)}, u32[]{:S(2)}) collective-permute-start(bf16[96,1024]{1,0:T(8,128)(2,1)} %get-tuple-element.29), channel_id=1, source_target_pairs={{0,2},{1,3},{2,4},{3,5},{4,6},{5,7},{6,0},{7,1},{8,10},{9,11},{10,... | collective-permute-start | bytes 589832 | tf_op jit(solution)/shard_map/ppermute | solution.py:21
  103.3 1.9 %collective-permute-start.5 = (bf16[1024,128]{1,0:T(8,128)(2,1)S(1)}, bf16[1024,128]{1,0:T(8,128)(2,1)S(1)}, u32[]{:S(2)}, u32[]{:S(2)}) collective-permute-start(bf16[1024,128]{1,0:T(8,128)(2,1)S(1)} %collective-permute-done.3.refs_3_), channel_id=1, source_target_pairs={{0,7},{1,0},{2,1},{3,2},{4,3},{5,4},{6,5},{7,6},{8,15},{9,8},{10,9... | collective-permute-start | bytes 786440 | tf_op jit(solution)/shard_map/ppermute | solution.py:21
  105.2 1.0 collective-permute-done.4.refs_4_
  106.2 2.9 %collective-permute-start.6 = (bf16[1024,128]{1,0:T(8,128)(2,1)S(1)}, bf16[1024,128]{1,0:T(8,128)(2,1)S(1)}, u32[]{:S(2)}, u32[]{:S(2)}) collective-permute-start(bf16[1024,128]{1,0:T(8,128)(2,1)S(1)} %collective-permute-done.4.refs_4_), channel_id=1, source_target_pairs={{0,1},{1,2},{2,3},{3,4},{4,5},{5,6},{6,7},{7,0},{8,9},{9,10},{10,1... | collective-permute-start | bytes 786440 | tf_op jit(solution)/shard_map/ppermute | solution.py:21
  109.2 0.0 collective-permute-done.11.refs_11_.refs_8_
  109.2 3.7 %collective-permute-start.9 = (bf16[96,1024]{1,0:T(8,128)(2,1)}, bf16[96,1024]{1,0:T(8,128)(2,1)S(1)}, u32[]{:S(2)}, u32[]{:S(2)}) collective-permute-start(bf16[96,1024]{1,0:T(8,128)(2,1)} %get-tuple-element.30), channel_id=1, source_target_pairs={{0,6},{1,7},{2,0},{3,1},{4,2},{5,3},{6,4},{7,5},{8,14},{9,15},{10,... | collective-permute-start | bytes 589832 | tf_op jit(solution)/shard_map/ppermute | solution.py:21
  112.9 0.0 collective-permute-done.7.refs_7_.refs_4_
  112.9 3.8 %collective-permute-start.12 = (bf16[96,1024]{1,0:T(8,128)(2,1)}, bf16[96,1024]{1,0:T(8,128)(2,1)S(1)}, u32[]{:S(2)}, u32[]{:S(2)}) collective-permute-start(bf16[96,1024]{1,0:T(8,128)(2,1)} %get-tuple-element.33), channel_id=1, source_target_pairs={{0,1},{1,2},{2,3},{3,4},{4,5},{5,6},{6,7},{7,0},{8,9},{9,10},{10,1... | collective-permute-start | bytes 589832 | tf_op jit(solution)/shard_map/ppermute | solution.py:21
  116.7 5.1 %collective-permute-start.13 = (bf16[96,1024]{1,0:T(8,128)(2,1)}, bf16[96,1024]{1,0:T(8,128)(2,1)S(1)}, u32[]{:S(2)}, u32[]{:S(2)}) collective-permute-start(bf16[96,1024]{1,0:T(8,128)(2,1)} %get-tuple-element.34), channel_id=1, source_target_pairs={{0,4},{1,5},{2,6},{3,7},{4,0},{5,1},{6,2},{7,3},{8,12},{9,13},{10,... | collective-permute-start | bytes 589832 | tf_op jit(solution)/shard_map/ppermute | solution.py:21
  121.8 9.6 %collective-permute-done.9.refs_9_.refs_6_ = bf16[96,1024]{1,0:T(8,128)(2,1)S(1)} collective-permute-done((bf16[96,1024]{1,0:T(8,128)(2,1)}, bf16[96,1024]{1,0:T(8,128)(2,1)S(1)}, u32[]{:S(2)}, u32[]{:S(2)}) %collective-permute-start.9) | collective-permute-done | bytes 196640 | tf_op jit(solution)/shard_map/ppermute | solution.py:21
  131.4 0.0 collective-permute-done.5.refs_5_
  131.4 0.6 copy-done.12
  132.0 0.1 copy-done.7
  132.1 3.6 %shard_map.87.refs_0_ = f32[1024,256]{1,0:T(8,128)} custom-call(bf16[1024,128]{1,0:T(8,128)(2,1)} %bitcast.33, bf16[1024,128]{1,0:T(8,128)(2,1)} %copy-done.3, bf16[1024,128]{1,0:T(8,128)(2,1)} %copy-done.4, bf16[1024,128]{1,0:T(8,128)(2,1)} %copy-done.5, bf16[1024,128]{1,0:T(8,128)(2,1)} %copy-done.6, bf16[1024,128]{1,0:T(8,128)(2,1)} %copy-done.7, ...), custom_call_target="tpu_custom_call" | custom-call | tf_op jit(solution)/shard_map/pallas_call | solution.py:190
  135.7 0.0 copy-start.13
  135.8 0.6 copy-done.13
  136.4 0.1 copy-done.14
  136.5 0.7 copy-done.2
  137.2 3.8 %shard_map.88 = bf16[64,24,128]{2,1,0:T(8,128)(2,1)} custom-call(f32[1024,256]{1,0:T(8,128)} %shard_map.87.refs_0_, bf16[1024,128]{1,0:T(8,128)(2,1)} %copy-done.1, bf16[1024,128]{1,0:T(8,128)(2,1)} %copy-done.2, bf16[96,1024]{1,0:T(8,128)(2,1)} %get-tuple-element.27.refs_6_.refs_3_, bf16[96,1024]{1,0:T(8,128)(2,1)} %copy-done.10, ...), custom_call_target="tpu_custom_call" | custom-call | tf_op jit(solution)/shard_map/pallas_call | solution.py:201
  141.0 6.1 %all-to-all-start.2 = ((bf16[64,24,128]{2,1,0:T(8,128)(2,1)}), bf16[64,24,128]{2,1,0:T(8,128)(2,1)S(1)}, u32[]{:S(2)}, u32[]{:S(2)}) async-start(bf16[64,24,128]{2,1,0:T(8,128)(2,1)} %shard_map.88), calls=%async_computation.2 | async-start | bytes 786432 | tf_op jit(solution)/shard_map/all_to_all | solution.py:214
  147.1 4.0 %shard_map.85 = (f32[1,128,1024]{2,1,0:T(8,128)}, f32[1,128,1024]{2,1,0:T(8,128)}) custom-call(bf16[1024,128]{1,0:T(8,128)(2,1)} %bitcast.34, bf16[1024,128]{1,0:T(8,128)(2,1)} %copy-done.3, bf16[1024,128]{1,0:T(8,128)(2,1)} %copy-done.4, bf16[1024,128]{1,0:T(8,128)(2,1)} %copy-done.5, bf16[1024,128]{1,0:T(8,128)(2,1)} %copy-done.6, ...), custom_call_target="tpu_custom_call" | custom-call | tf_op jit(solution)/shard_map/pallas_call | solution.py:216
  151.1 10.4 %all-to-all-done.2 = bf16[64,24,128]{2,1,0:T(8,128)(2,1)S(1)} async-done(((bf16[64,24,128]{2,1,0:T(8,128)(2,1)}), bf16[64,24,128]{2,1,0:T(8,128)(2,1)S(1)}, u32[]{:S(2)}, u32[]{:S(2)}) %all-to-all-start.2) | async-done | bytes 393248 | tf_op jit(solution)/shard_map/all_to_all | solution.py:214
  161.5 0.6 gather_fusion.1
  162.2 28.0 %all-gather = bf16[3840,128]{1,0:T(8,128)(2,1)S(1)} all-gather(bf16[480,128]{1,0:T(8,128)(2,1)S(1)} %fusion.3), channel_id=2, replica_groups=mesh['fsdp_0'=4,'fsdp_1'=8,'fsdp_2'=2,'dp'=8] {'dp'}, dimensions={0}, use_global_device_ids=true | all-gather | bytes 1105920 | tf_op jit(solution)/shard_map/all_gather | solution.py:226
  190.2 0.1 slice.40
  190.3 0.1 convert_reduce_fusion
  190.4 0.3 fusion.1
  190.7 1.2 copy.12
  (43 shorter events, 0.2 us)
Async XLA Ops:
  3.2 10.5 %copy-start.15 = (s32[28]{0:T(128)S(1)}, s32[28]{0:T(128)}, u32[]{:S(2)}) copy-start(s32[28]{0:T(128)} %param.9) | copy-start | bytes 340
  3.2 36.4 %all-to-all-start = ((bf16[8,448,128]{2,1,0:T(8,128)(2,1)}), bf16[8,448,128]{2,1,0:T(8,128)(2,1)S(1)}, u32[]{:S(2)}, u32[]{:S(2)}) async-start(bf16[8,448,128]{2,1,0:T(8,128)(2,1)} %bitcast.1), calls=%async_computation | async-start | bytes 1835008 | tf_op jit(solution)/shard_map/all_to_all | solution.py:167
  62.5 68.9 %copy-start = (bf16[64,16,128]{2,1,0:T(8,128)(2,1)}, bf16[64,16,128]{2,1,0:T(8,128)(2,1)S(1)}, u32[]{:S(2)}) copy-start(bf16[64,16,128]{2,1,0:T(8,128)(2,1)S(1)} %all_to_all.15) | copy-start | bytes 786436
  62.5 11.5 %collective-permute-start.1 = (bf16[1024,128]{1,0:T(8,128)(2,1)S(1)}, bf16[1024,128]{1,0:T(8,128)(2,1)S(1)}, u32[]{:S(2)}, u32[]{:S(2)}) collective-permute-start(bf16[1024,128]{1,0:T(8,128)(2,1)S(1)} %bitcast.31), channel_id=1, source_target_pairs={{0,1},{1,2},{2,3},{3,4},{4,5},{5,6},{6,7},{7,0},{8,9},{9,10},{10,1... | collective-permute-start | bytes 786440 | tf_op jit(solution)/shard_map/ppermute | solution.py:21
  64.9 16.1 %collective-permute-start = (bf16[1024,128]{1,0:T(8,128)(2,1)S(1)}, bf16[1024,128]{1,0:T(8,128)(2,1)S(1)}, u32[]{:S(2)}, u32[]{:S(2)}) collective-permute-start(bf16[1024,128]{1,0:T(8,128)(2,1)S(1)} %bitcast.32), channel_id=1, source_target_pairs={{0,7},{1,0},{2,1},{3,2},{4,3},{5,4},{6,5},{7,6},{8,15},{9,8},{10,9... | collective-permute-start | bytes 786440 | tf_op jit(solution)/shard_map/ppermute | solution.py:21
  73.9 61.8 %copy-start.1 = (bf16[1024,128]{1,0:T(8,128)(2,1)}, bf16[1024,128]{1,0:T(8,128)(2,1)S(1)}, u32[]{:S(2)}) copy-start(bf16[1024,128]{1,0:T(8,128)(2,1)S(1)} %collective-permute-done.1.refs_6_.refs_1_) | copy-start | bytes 786436
  73.9 16.1 %collective-permute-start.2 = (bf16[1024,128]{1,0:T(8,128)(2,1)S(1)}, bf16[1024,128]{1,0:T(8,128)(2,1)S(1)}, u32[]{:S(2)}, u32[]{:S(2)}) collective-permute-start(bf16[1024,128]{1,0:T(8,128)(2,1)S(1)} %collective-permute-done.1.refs_6_.refs_1_), channel_id=1, source_target_pairs={{0,1},{1,2},{2,3},{3,4},{4,5},{5,6},{6,7},{7,0},{8,9},{9,10},{10,1... | collective-permute-start | bytes 786440 | tf_op jit(solution)/shard_map/ppermute | solution.py:21
  78.0 20.9 %collective-permute-start.10 = (bf16[96,1024]{1,0:T(8,128)(2,1)}, bf16[96,1024]{1,0:T(8,128)(2,1)S(1)}, u32[]{:S(2)}, u32[]{:S(2)}) collective-permute-start(bf16[96,1024]{1,0:T(8,128)(2,1)} %get-tuple-element.31), channel_id=1, source_target_pairs={{0,3},{1,4},{2,5},{3,6},{4,7},{5,0},{6,1},{7,2},{8,11},{9,12},{10,... | collective-permute-start | bytes 589832 | tf_op jit(solution)/shard_map/ppermute | solution.py:21
  81.1 50.3 %copy-start.3 = (bf16[1024,128]{1,0:T(8,128)(2,1)}, bf16[1024,128]{1,0:T(8,128)(2,1)S(1)}, u32[]{:S(2)}) copy-start(bf16[1024,128]{1,0:T(8,128)(2,1)S(1)} %collective-permute-done.refs_1_) | copy-start | bytes 786436
  81.1 22.2 %collective-permute-start.3 = (bf16[1024,128]{1,0:T(8,128)(2,1)S(1)}, bf16[1024,128]{1,0:T(8,128)(2,1)S(1)}, u32[]{:S(2)}, u32[]{:S(2)}) collective-permute-start(bf16[1024,128]{1,0:T(8,128)(2,1)S(1)} %collective-permute-done.refs_1_), channel_id=1, source_target_pairs={{0,7},{1,0},{2,1},{3,2},{4,3},{5,4},{6,5},{7,6},{8,15},{9,8},{10,9... | collective-permute-start | bytes 786440 | tf_op jit(solution)/shard_map/ppermute | solution.py:21
  90.0 41.4 %copy-start.4 = (bf16[1024,128]{1,0:T(8,128)(2,1)}, bf16[1024,128]{1,0:T(8,128)(2,1)S(1)}, u32[]{:S(2)}) copy-start(bf16[1024,128]{1,0:T(8,128)(2,1)S(1)} %collective-permute-done.2.refs_2_) | copy-start | bytes 786436
  90.0 16.2 %collective-permute-start.4 = (bf16[1024,128]{1,0:T(8,128)(2,1)S(1)}, bf16[1024,128]{1,0:T(8,128)(2,1)S(1)}, u32[]{:S(2)}, u32[]{:S(2)}) collective-permute-start(bf16[1024,128]{1,0:T(8,128)(2,1)S(1)} %collective-permute-done.2.refs_2_), channel_id=1, source_target_pairs={{0,1},{1,2},{2,3},{3,4},{4,5},{5,6},{6,7},{7,0},{8,9},{9,10},{10,1... | collective-permute-start | bytes 786440 | tf_op jit(solution)/shard_map/ppermute | solution.py:21
  91.9 17.3 %collective-permute-start.11 = (bf16[96,1024]{1,0:T(8,128)(2,1)}, bf16[96,1024]{1,0:T(8,128)(2,1)S(1)}, u32[]{:S(2)}, u32[]{:S(2)}) collective-permute-start(bf16[96,1024]{1,0:T(8,128)(2,1)} %get-tuple-element.32), channel_id=1, source_target_pairs={{0,5},{1,6},{2,7},{3,0},{4,1},{5,2},{6,3},{7,4},{8,13},{9,14},{10,... | collective-permute-start | bytes 589832 | tf_op jit(solution)/shard_map/ppermute | solution.py:21
  93.8 19.1 %collective-permute-start.7 = (bf16[96,1024]{1,0:T(8,128)(2,1)}, bf16[96,1024]{1,0:T(8,128)(2,1)S(1)}, u32[]{:S(2)}, u32[]{:S(2)}) collective-permute-start(bf16[96,1024]{1,0:T(8,128)(2,1)} %get-tuple-element.28), channel_id=1, source_target_pairs={{0,7},{1,0},{2,1},{3,2},{4,3},{5,4},{6,5},{7,6},{8,15},{9,8},{10,9... | collective-permute-start | bytes 589832 | tf_op jit(solution)/shard_map/ppermute | solution.py:21
  99.0 32.4 %copy-start.8 = (bf16[96,1024]{1,0:T(8,128)(2,1)}, bf16[96,1024]{1,0:T(8,128)(2,1)S(1)}, u32[]{:S(2)}) copy-start(bf16[96,1024]{1,0:T(8,128)(2,1)S(1)} %collective-permute-done.10.refs_10_.refs_7_) | copy-start | bytes 589828
  99.0 17.7 %collective-permute-start.8 = (bf16[96,1024]{1,0:T(8,128)(2,1)}, bf16[96,1024]{1,0:T(8,128)(2,1)S(1)}, u32[]{:S(2)}, u32[]{:S(2)}) collective-permute-start(bf16[96,1024]{1,0:T(8,128)(2,1)} %get-tuple-element.29), channel_id=1, source_target_pairs={{0,2},{1,3},{2,4},{3,5},{4,6},{5,7},{6,0},{7,1},{8,10},{9,11},{10,... | collective-permute-start | bytes 589832 | tf_op jit(solution)/shard_map/ppermute | solution.py:21
  103.3 28.1 %copy-start.5 = (bf16[1024,128]{1,0:T(8,128)(2,1)}, bf16[1024,128]{1,0:T(8,128)(2,1)S(1)}, u32[]{:S(2)}) copy-start(bf16[1024,128]{1,0:T(8,128)(2,1)S(1)} %collective-permute-done.3.refs_3_) | copy-start | bytes 786436
  103.3 28.1 %collective-permute-start.5 = (bf16[1024,128]{1,0:T(8,128)(2,1)S(1)}, bf16[1024,128]{1,0:T(8,128)(2,1)S(1)}, u32[]{:S(2)}, u32[]{:S(2)}) collective-permute-start(bf16[1024,128]{1,0:T(8,128)(2,1)S(1)} %collective-permute-done.3.refs_3_), channel_id=1, source_target_pairs={{0,7},{1,0},{2,1},{3,2},{4,3},{5,4},{6,5},{7,6},{8,15},{9,8},{10,9... | collective-permute-start | bytes 786440 | tf_op jit(solution)/shard_map/ppermute | solution.py:21
  106.2 25.2 %copy-start.6 = (bf16[1024,128]{1,0:T(8,128)(2,1)}, bf16[1024,128]{1,0:T(8,128)(2,1)S(1)}, u32[]{:S(2)}) copy-start(bf16[1024,128]{1,0:T(8,128)(2,1)S(1)} %collective-permute-done.4.refs_4_) | copy-start | bytes 786436
  106.2 29.5 %collective-permute-start.6 = (bf16[1024,128]{1,0:T(8,128)(2,1)S(1)}, bf16[1024,128]{1,0:T(8,128)(2,1)S(1)}, u32[]{:S(2)}, u32[]{:S(2)}) collective-permute-start(bf16[1024,128]{1,0:T(8,128)(2,1)S(1)} %collective-permute-done.4.refs_4_), channel_id=1, source_target_pairs={{0,1},{1,2},{2,3},{3,4},{4,5},{5,6},{6,7},{7,0},{8,9},{9,10},{10,1... | collective-permute-start | bytes 786440 | tf_op jit(solution)/shard_map/ppermute | solution.py:21
  109.2 22.2 %copy-start.9 = (bf16[96,1024]{1,0:T(8,128)(2,1)}, bf16[96,1024]{1,0:T(8,128)(2,1)S(1)}, u32[]{:S(2)}) copy-start(bf16[96,1024]{1,0:T(8,128)(2,1)S(1)} %collective-permute-done.11.refs_11_.refs_8_) | copy-start | bytes 589828
  109.2 22.2 %collective-permute-start.9 = (bf16[96,1024]{1,0:T(8,128)(2,1)}, bf16[96,1024]{1,0:T(8,128)(2,1)S(1)}, u32[]{:S(2)}, u32[]{:S(2)}) collective-permute-start(bf16[96,1024]{1,0:T(8,128)(2,1)} %get-tuple-element.30), channel_id=1, source_target_pairs={{0,6},{1,7},{2,0},{3,1},{4,2},{5,3},{6,4},{7,5},{8,14},{9,15},{10,... | collective-permute-start | bytes 589832 | tf_op jit(solution)/shard_map/ppermute | solution.py:21
  112.9 18.5 %copy-start.10 = (bf16[96,1024]{1,0:T(8,128)(2,1)}, bf16[96,1024]{1,0:T(8,128)(2,1)S(1)}, u32[]{:S(2)}) copy-start(bf16[96,1024]{1,0:T(8,128)(2,1)S(1)} %collective-permute-done.7.refs_7_.refs_4_) | copy-start | bytes 589828
  112.9 22.8 %collective-permute-start.12 = (bf16[96,1024]{1,0:T(8,128)(2,1)}, bf16[96,1024]{1,0:T(8,128)(2,1)S(1)}, u32[]{:S(2)}, u32[]{:S(2)}) collective-permute-start(bf16[96,1024]{1,0:T(8,128)(2,1)} %get-tuple-element.33), channel_id=1, source_target_pairs={{0,1},{1,2},{2,3},{3,4},{4,5},{5,6},{6,7},{7,0},{8,9},{9,10},{10,1... | collective-permute-start | bytes 589832 | tf_op jit(solution)/shard_map/ppermute | solution.py:21
  116.7 14.7 %copy-start.11 = (bf16[96,1024]{1,0:T(8,128)(2,1)}, bf16[96,1024]{1,0:T(8,128)(2,1)S(1)}, u32[]{:S(2)}) copy-start(bf16[96,1024]{1,0:T(8,128)(2,1)S(1)} %collective-permute-done.8.refs_8_.refs_5_) | copy-start | bytes 589828
  116.7 19.0 %collective-permute-start.13 = (bf16[96,1024]{1,0:T(8,128)(2,1)}, bf16[96,1024]{1,0:T(8,128)(2,1)S(1)}, u32[]{:S(2)}, u32[]{:S(2)}) collective-permute-start(bf16[96,1024]{1,0:T(8,128)(2,1)} %get-tuple-element.34), channel_id=1, source_target_pairs={{0,4},{1,5},{2,6},{3,7},{4,0},{5,1},{6,2},{7,3},{8,12},{9,13},{10,... | collective-permute-start | bytes 589832 | tf_op jit(solution)/shard_map/ppermute | solution.py:21
  131.4 0.7 copy-start.12
  131.4 0.8 copy-start.7
  135.7 0.7 copy-start.13
  135.8 0.7 copy-start.14
  136.5 0.7 copy-start.2
  141.0 20.5 %all-to-all-start.2 = ((bf16[64,24,128]{2,1,0:T(8,128)(2,1)}), bf16[64,24,128]{2,1,0:T(8,128)(2,1)S(1)}, u32[]{:S(2)}, u32[]{:S(2)}) async-start(bf16[64,24,128]{2,1,0:T(8,128)(2,1)} %shard_map.88), calls=%async_computation.2 | async-start | bytes 786432 | tf_op jit(solution)/shard_map/all_to_all | solution.py:214
